TPU v7x, 8 devices: a whole 2x2x1 slice. The times are simulated.
8 devices in a mesh: dp: 2 (over z, y), sp: 4 (over x, core).
Axes of the slice: x: 2, y: 2, z: 1, core: 2. Of those that a mesh axis runs over, the one named last changes fastest.
Arguments:
- x_in: bfloat16 [6144, 1536], P(('dp', 'sp')), parts along dimension 0
- seg_ids: int32 [6144], P(('dp', 'sp')), parts along dimension 0
- norm_gains: float32 [4, 1536], replicated
- w_in: bfloat16 [1536, 6448], replicated
- ssm_head: float32 [3, 48], replicated
- y_gain: float32 [3072], replicated
- w_out: bfloat16 [3072, 1536], replicated
- mlp_up: bfloat16 [2, 1536, 12288], replicated
- mlp_down: bfloat16 [2, 6144, 1536], replicated
- w_qkv: bfloat16 [1536, 36, 128], replicated
- w_attn_out: bfloat16 [12, 128, 1536], replicated
Outputs:
- output: bfloat16 [6144, 1536], P(('dp', 'sp')), parts along dimension 0
There are 2 independent parts. A program takes and returns all parts, laid end to end along the dimension named above; an argument that names none is the same for every part.
All inputs are finite; a program needn't handle non-finite values.
Results may differ from a plain program's by a relative error of at most 0.017019.
Values are sent between devices in bfloat16 or wider.
A program may use at most 1 GiB of HBM per device.

v0:
```python
import functools
import math

import jax
import jax.numpy as jnp
from jax import lax
from jax.experimental import pallas as pl
from jax.experimental.pallas import tpu as pltpu
from jax.sharding import PartitionSpec as P


CHUNK = 64
NORM_EPS = 1e-6
ROPE_BASE = 10000.0
F32 = jnp.float32
BF16 = jnp.bfloat16
VMEM_LIMIT = 60 * 1024 * 1024
NT = (((1,), (1,)), ((), ()))


def dot(a, b, dims=(((1,), (0,)), ((), ()))):
    return lax.dot_general(a, b, dims, preferred_element_type=F32)


def params(sem):
    return pltpu.CompilerParams(dimension_semantics=sem, vmem_limit_bytes=VMEM_LIMIT)


def cost(flops, bytes_accessed, trans=0):
    return pl.CostEstimate(flops=int(flops), bytes_accessed=int(bytes_accessed), transcendentals=int(trans))


def norm_rows(values, gain):
    wide = values.astype(F32)
    inv = lax.rsqrt(jnp.mean(wide * wide, axis=-1, keepdims=True) + NORM_EPS)
    return (wide * inv * gain).astype(BF16)


SMEM_SPEC = pl.BlockSpec(memory_space=pltpu.SMEM)


def full_spec(shape):
    zeros = (0,) * len(shape)
    return pl.BlockSpec(shape, lambda *_: zeros)


def in_proj_kernel(n_heads, x_ref, gain_ref, w_ref, head_ref, h_ref, xs_ref, bc_ref, dt_ref, cum_ref):
    step = pl.program_id(0)

    @pl.when(step == 0)
    def _():
        hid = norm_rows(x_ref[...], gain_ref[0:1, :])
        h_ref[...] = hid
        out = dot(hid, w_ref[...], NT)
        n_bc = bc_ref.shape[1]
        bc_ref[...] = out[:, :n_bc].astype(BF16)
        lanes = dt_ref.shape[1]
        raw = out[:, n_bc:n_bc + lanes] + head_ref[0:1, :]
        dt = jnp.maximum(raw, 0.0) + jnp.log1p(jnp.exp(-jnp.abs(raw)))
        lane = lax.broadcasted_iota(jnp.int32, dt.shape, 1)
        dt = jnp.where(lane < n_heads, dt, 0.0)
        dt_ref[...] = dt
        cum = dt * head_ref[1:2, :]
        row = lax.broadcasted_iota(jnp.int32, dt.shape, 0) % CHUNK
        shift = 1
        while shift < CHUNK:
            cum = cum + jnp.where(row >= shift, pltpu.roll(cum, shift, 0), 0.0)
            shift *= 2
        cum_ref[...] = cum

    @pl.when(step > 0)
    def _():
        xs_ref[...] = dot(h_ref[...], w_ref[...], NT).astype(BF16)


def in_proj(x_rows, gains, w_in_t, head_pad, inner, n_heads):
    tokens, dim = x_rows.shape
    tile = 512
    n_x = inner // tile
    last = 2 * inner // tile
    out_shape = (
        jax.ShapeDtypeStruct((tokens, dim), BF16),
        jax.ShapeDtypeStruct((tokens, inner), BF16),
        jax.ShapeDtypeStruct((tokens, 256), BF16),
        jax.ShapeDtypeStruct((tokens, 128), F32),
        jax.ShapeDtypeStruct((tokens, 128), F32),
    )
    return pl.pallas_call(
        functools.partial(in_proj_kernel, n_heads),
        grid=(n_x + 1,),
        in_specs=[
            full_spec((tokens, dim)),
            full_spec(gains.shape),
            pl.BlockSpec((tile, dim), lambda i: (jnp.where(i == 0, last, i - 1), 0)),
            full_spec((8, 128)),
        ],
        out_specs=(
            full_spec((tokens, dim)),
            pl.BlockSpec((tokens, tile), lambda i: (0, jnp.maximum(i - 1, 0))),
            full_spec((tokens, 256)),
            full_spec((tokens, 128)),
            full_spec((tokens, 128)),
        ),
        out_shape=out_shape,
        compiler_params=params(("arbitrary",)),
        cost_estimate=cost(2 * tokens * dim * (inner + tile), 16e6),
        name="in_proj",
    )(x_rows, gains, w_in_t, head_pad)


def z_proj_kernel(h_ref, w_ref, z_ref):
    z_ref[...] = dot(h_ref[...], w_ref[...], NT)


def z_proj(hid, w_in_t, inner):
    tokens, dim = hid.shape
    tile = 512
    first = inner // tile
    return pl.pallas_call(
        z_proj_kernel,
        grid=(inner // tile,),
        in_specs=[full_spec((tokens, dim)), pl.BlockSpec((tile, dim), lambda i: (i + first, 0))],
        out_specs=pl.BlockSpec((tokens, tile), lambda i: (0, i)),
        out_shape=jax.ShapeDtypeStruct((tokens, inner), F32),
        compiler_params=params(("arbitrary",)),
        cost_estimate=cost(2 * tokens * dim * inner, 21e6),
        name="z_proj",
    )(hid, w_in_t)


def head_lanes(cols, first, width):
    rows = cols.shape[0]
    lane = lax.broadcasted_iota(jnp.int32, (rows, 128), 1)
    parts = []
    for k in range(width // 128):
        left = jnp.broadcast_to(cols[:, first + 2 * k:first + 2 * k + 1], (rows, 128))
        right = jnp.broadcast_to(cols[:, first + 2 * k + 1:first + 2 * k + 2], (rows, 128))
        parts.append(jnp.where(lane < 64, left, right))
    return jnp.concatenate(parts, axis=1)


def chunk_weights(dt, cum, rel):
    last_rel = rel[CHUNK - 1:CHUNK, :]
    pos = lax.broadcasted_iota(jnp.int32, cum.shape, 0)
    last_cum = cum[CHUNK - 1:CHUNK, :]
    end_w = jnp.where(pos >= last_rel, jnp.exp(last_cum - cum), 0.0) * dt
    carry = jnp.where(rel < 0, jnp.exp(cum), 0.0)
    return end_w, carry


def state_step(state_ref, cols, xg, bt, end_w, dec_row, first):
    xw = (xg.astype(F32) * head_lanes(end_w, first, xg.shape[1])).astype(BF16)
    state_ref[:, cols] = dec_row * state_ref[:, cols] + dot(bt, xw)


def block_rel(sc_ref, seg_ref):
    return doc_start(seg_ref[...], sc_ref, N_SRC) - (sc_ref[N_SRC - 1] + pl.program_id(0) * CHUNK)


def ssd_state_kernel(sc_ref, x_ref, bc_ref, dt_ref, cum_ref, seg_ref, end_ref, decay_ref):
    step = pl.program_id(0)

    @pl.when(step == 0)
    def _():
        end_ref[...] = jnp.zeros_like(end_ref)
        decay_ref[...] = jnp.ones_like(decay_ref)

    end_w, carry = chunk_weights(dt_ref[...], cum_ref[...], block_rel(sc_ref, seg_ref))
    bt = bc_ref[:, :128].astype(F32).T.astype(BF16)
    for g in range(x_ref.shape[1] // 256):
        cols = slice(g * 256, (g + 1) * 256)
        dec_row = head_lanes(carry[CHUNK - 8:, :], 4 * g, 256)[7:8]
        state_step(end_ref, cols, x_ref[:, cols], bt, end_w, dec_row, 4 * g)
        decay_ref[:, cols] = decay_ref[:, cols] * dec_row


def ssd_state(scalars, xs, bc, dt, cum, seg_wide):
    tokens, inner = xs.shape
    row = lambda width: pl.BlockSpec((CHUNK, width), lambda i: (i, 0))
    return pl.pallas_call(
        ssd_state_kernel,
        grid=(tokens // CHUNK,),
        in_specs=[SMEM_SPEC, row(inner), row(256), row(128), row(128), row(128)],
        out_specs=(full_spec((128, inner)), full_spec((1, inner))),
        out_shape=(jax.ShapeDtypeStruct((128, inner), F32), jax.ShapeDtypeStruct((1, inner), F32)),
        compiler_params=params(("arbitrary",)),
        cost_estimate=cost(2 * tokens * 256 * inner, 8e6),
        name="ssd_state",
    )(scalars, xs, bc, dt, cum, seg_wide)


def ssd_full_kernel(sc_ref, x_ref, bc_ref, dt_ref, cum_ref, seg_ref, pack_ref, z_ref, hin_ref, skip_ref, gain_ref, out_ref, state_ref, y_ref):
    step = pl.program_id(0)

    @pl.when(step == 0)
    def _():
        state_ref[...] = hin_ref[...]

    inner = x_ref.shape[1]
    cum = cum_ref[...]
    rel = block_rel(sc_ref, seg_ref)
    end_w, carry = chunk_weights(dt_ref[...], cum, rel)
    b_blk = bc_ref[:, :128]
    c_blk = bc_ref[:, 128:]
    bt = b_blk.astype(F32).T.astype(BF16)
    row_id = lax.broadcasted_iota(jnp.int32, (CHUNK, 128), 0)
    lane_id = lax.broadcasted_iota(jnp.int32, (CHUNK, 128), 1)
    src = jnp.where(lane_id < 64, lane_id, lane_id - 64)
    visible = (src >= rel) & (src <= row_id)
    scores = dot(c_blk, jnp.concatenate([b_blk, b_blk], axis=0), NT)
    scores = jnp.where(visible, scores, 0.0)
    blk_row = lax.broadcasted_iota(jnp.int32, (256, 256), 0) // 64
    blk_col = lax.broadcasted_iota(jnp.int32, (256, 256), 1) // 64
    diag = blk_row == blk_col
    n_pairs = inner // 128
    sumsq = jnp.zeros((CHUNK, 128), F32)
    for g in range(inner // 256):
        cols = slice(g * 256, (g + 1) * 256)
        xg = x_ref[:, cols]
        carry_x = head_lanes(carry, 4 * g, 256)
        cum_x = head_lanes(cum, 4 * g, 256)
        mixes = []
        for k in range(2):
            pair = 2 * g + k
            cum_s = pack_ref[0, pair:pair + 1, :]
            dt_s = pack_ref[0, n_pairs + pair:n_pairs + pair + 1, :]
            decay = jnp.exp(jnp.minimum(cum_x[:, k * 128:(k + 1) * 128] - cum_s, 0.0))
            mixes.append((scores * decay * dt_s).astype(BF16))
        mix = jnp.concatenate(mixes, axis=1)
        x_diag = jnp.where(diag, jnp.concatenate([xg, xg, xg, xg], axis=0), jnp.zeros((), BF16))
        y_in = dot(mix, x_diag)
        y_carry = dot(c_blk, state_ref[:, cols].astype(BF16)) * carry_x
        y = y_in + skip_ref[:, cols] * xg.astype(F32) + y_carry
        y_ref[:, cols] = y
        sq = y * y
        sumsq = sumsq + sq[:, :128] + sq[:, 128:]
        state_step(state_ref, cols, xg, bt, end_w, carry_x[CHUNK - 1:CHUNK, :], 4 * g)
    inv = lax.rsqrt(jnp.sum(sumsq, axis=-1, keepdims=True) * (1.0 / inner) + NORM_EPS)
    for g in range(inner // 512):
        cols = slice(g * 512, (g + 1) * 512)
        z = z_ref[:, cols]
        out_ref[:, cols] = (y_ref[:, cols] * inv * gain_ref[:, cols] * (z * jax.nn.sigmoid(z))).astype(BF16)


def ssd_full(scalars, xs, bc, dt, cum, seg_wide, pack, z, h_in, skip, gain):
    tokens, inner = xs.shape
    row = lambda width: pl.BlockSpec((CHUNK, width), lambda i: (i, 0))
    return pl.pallas_call(
        ssd_full_kernel,
        grid=(tokens // CHUNK,),
        in_specs=[
            SMEM_SPEC, row(inner), row(256), row(128), row(128), row(128),
            pl.BlockSpec((1, pack.shape[1], 128), lambda i: (i, 0, 0)),
            row(inner), full_spec((128, inner)), full_spec((1, inner)), full_spec((1, inner)),
        ],
        out_specs=row(inner),
        out_shape=jax.ShapeDtypeStruct((tokens, inner), BF16),
        scratch_shapes=[pltpu.VMEM((128, inner), F32), pltpu.VMEM((CHUNK, inner), F32)],
        compiler_params=params(("arbitrary",)),
        cost_estimate=cost(12e9, 20e6),
        name="ssd_full",
    )(scalars, xs, bc, dt, cum, seg_wide, pack, z, h_in, skip, gain)


def proj_add_kernel(a_ref, w_ref, *refs):
    out_ref = refs[-1]
    res = jnp.concatenate([r[...] for r in refs[:-1]], axis=0)
    out_ref[...] = (res.astype(F32) + dot(a_ref[...], w_ref[...])).astype(BF16)


def proj_add(a, w, res):
    tokens, depth = a.shape
    dim = w.shape[1]
    tile = 256
    col = lambda rows: pl.BlockSpec((rows, tile), lambda i: (0, i))
    return pl.pallas_call(
        proj_add_kernel,
        grid=(dim // tile,),
        in_specs=[full_spec((tokens, depth)), col(depth)] + [col(r.shape[0]) for r in res],
        out_specs=col(tokens),
        out_shape=jax.ShapeDtypeStruct((tokens, dim), BF16),
        compiler_params=params(("arbitrary",)),
        cost_estimate=cost(2 * tokens * depth * dim, 2 * (tokens * depth + depth * dim + 2 * tokens * dim)),
        name="proj_add",
    )(a, w, *res)


def mlp_kernel(layer, x_ref, gain_ref, wg_ref, wu_ref, wd_ref, out_ref, h_ref, acc_ref):
    step = pl.program_id(0)

    @pl.when(step == 0)
    def _():
        h_ref[...] = norm_rows(x_ref[...], gain_ref[2 * layer + 1:2 * layer + 2, :])
        acc_ref[...] = jnp.zeros_like(acc_ref)

    hid = h_ref[...]
    gate = dot(hid, wg_ref[0])
    up = dot(hid, wu_ref[0])
    act = (gate * jax.nn.sigmoid(gate) * up).astype(BF16)
    acc_ref[...] += dot(act, wd_ref[0])

    @pl.when(step == pl.num_programs(0) - 1)
    def _():
        out_ref[...] = (x_ref[...].astype(F32) + acc_ref[...]).astype(BF16)


def mlp(x_rows, gains, mlp_up, mlp_down, layer, part, parts):
    tokens, dim = x_rows.shape
    tokens //= parts
    ff = mlp_down.shape[1]
    tile = 512
    n_ff = ff // tile
    return pl.pallas_call(
        functools.partial(mlp_kernel, layer),
        grid=(n_ff,),
        in_specs=[
            pl.BlockSpec((tokens, dim), lambda i: (part, 0)),
            full_spec(gains.shape),
            pl.BlockSpec((1, dim, tile), lambda i: (layer, 0, i)),
            pl.BlockSpec((1, dim, tile), lambda i: (layer, 0, i + n_ff)),
            pl.BlockSpec((1, tile, dim), lambda i: (layer, i, 0)),
        ],
        out_specs=full_spec((tokens, dim)),
        out_shape=jax.ShapeDtypeStruct((tokens, dim), BF16),
        scratch_shapes=[pltpu.VMEM((tokens, dim), BF16), pltpu.VMEM((tokens, dim), F32)],
        compiler_params=params(("arbitrary",)),
        cost_estimate=cost(6 * tokens * dim * ff, 6 * dim * ff),
        name="mlp",
    )(x_rows, gains, mlp_up, mlp_up, mlp_down)


def rope_tables(positions, head_dim):
    half = head_dim // 2
    inv_freq = ROPE_BASE ** (-jnp.arange(half, dtype=F32) * 2.0 / head_dim)
    angle = positions[:, None] * inv_freq[None, :]
    cos, sin = jnp.cos(angle), jnp.sin(angle)
    return jnp.concatenate([cos, cos], axis=1), jnp.concatenate([-sin, sin], axis=1)


def qkv_kernel(n_q, n_rot, xa_ref, xb_ref, gain_ref, cos_ref, sin_ref, w_ref, *refs):
    h_ref = refs[-1]
    kv_ref = refs[-2]
    step = pl.program_id(0)

    @pl.when(step == 0)
    def _():
        rows = xa_ref.shape[0]
        h_ref[:rows] = norm_rows(xa_ref[...], gain_ref[2:3, :])
        h_ref[rows:] = norm_rows(xb_ref[...], gain_ref[2:3, :])

    heads, _, head_dim = w_ref.shape
    w_all = jnp.concatenate([w_ref[k] for k in range(heads)], axis=1)
    out = dot(h_ref[...], w_all)

    def rotated(k):
        val = out[:, k * head_dim:(k + 1) * head_dim]
        return (val * cos_ref[...] + pltpu.roll(val, head_dim // 2, 1) * sin_ref[...]).astype(BF16)

    if n_q:
        @pl.when(step < n_q)
        def _():
            for k in range(heads):
                refs[0][k] = rotated(k)

    @pl.when((step >= n_q) & (step < n_rot))
    def _():
        for k in range(heads):
            kv_ref[k] = rotated(k)

    @pl.when(step >= n_rot)
    def _():
        for k in range(heads):
            kv_ref[k] = out[:, k * head_dim:(k + 1) * head_dim].astype(BF16)


def qkv_proj(x_a, x_b, gains, cos, sin, w_heads, n_query, with_q):
    tokens, dim = x_a.shape
    tokens *= 2
    n_heads, _, head_dim = w_heads.shape
    n_kv = n_heads - n_query
    per = 4
    n_q = n_query // per if with_q else 0
    skip = 0 if with_q else n_query // per
    n_rot = n_q + n_kv // 2 // per
    steps = n_heads // per - skip
    out_specs = [pl.BlockSpec((per, tokens, head_dim), lambda i: (jnp.maximum(i - n_q, 0), 0, 0))]
    out_shape = [jax.ShapeDtypeStruct((n_kv, tokens, head_dim), BF16)]
    if with_q:
        out_specs.insert(0, pl.BlockSpec((per, tokens, head_dim), lambda i: (jnp.minimum(i, n_q - 1), 0, 0)))
        out_shape.insert(0, jax.ShapeDtypeStruct((n_query, tokens, head_dim), BF16))
    return pl.pallas_call(
        functools.partial(qkv_kernel, n_q, n_rot),
        grid=(steps,),
        in_specs=[
            full_spec(x_a.shape), full_spec(x_a.shape), full_spec(gains.shape), full_spec((tokens, head_dim)),
            full_spec((tokens, head_dim)),
            pl.BlockSpec((per, dim, head_dim), lambda i: (i + skip, 0, 0)),
        ],
        out_specs=tuple(out_specs),
        out_shape=tuple(out_shape),
        scratch_shapes=[pltpu.VMEM((tokens, dim), BF16)],
        compiler_params=params(("arbitrary",)),
        cost_estimate=cost(2 * tokens * dim * steps * per * head_dim, 2 * dim * steps * per * head_dim + 8e6),
        name="qkv" if with_q else "kv",
    )(x_a, x_b, gains, cos, sin, w_heads)


BLOCK = 256
HEAD_GROUP = 4
N_SRC = 4
NEG = -1e30


def doc_start(seg, sc_ref, first):
    start = jnp.zeros_like(seg)
    for doc in range(4):
        start = jnp.where(seg > doc, sc_ref[first + doc], start)
    return start


def attn_kernel(sc_ref, q_ref, seg_ref, *refs):
    kv_refs = refs[:2 * N_SRC]
    o_ref, m_ref, l_ref, acc_ref, bias_ref = refs[2 * N_SRC:]
    j = pl.program_id(1)
    heads, _, head_dim = q_ref.shape
    scale = (head_dim ** -0.5) * math.log2(math.e)
    q0 = sc_ref[N_SRC - 1] + j * BLOCK
    first_start = doc_start(sc_ref[N_SRC + 4 + j], sc_ref, N_SRC)
    start = doc_start(seg_ref[...], sc_ref, N_SRC)
    start = jnp.concatenate([start, start], axis=1)
    col_id = lax.broadcasted_iota(jnp.int32, (BLOCK, BLOCK), 1)
    row_id = lax.broadcasted_iota(jnp.int32, (BLOCK, BLOCK), 0)

    def weights(h, k_ref, rows, bias):
        s = dot(q_ref[h], k_ref[h, rows, :], NT) + bias
        return s, jnp.max(s, axis=-1, keepdims=True)

    k_ref, v_ref = kv_refs[2 * N_SRC - 2:]
    rows = pl.ds(pl.multiple_of(j * BLOCK, BLOCK), BLOCK)
    bias_ref[...] = jnp.where((col_id + q0 >= start) & (col_id <= row_id), 0.0, NEG)
    for h in range(heads):
        s, top = weights(h, k_ref, rows, bias_ref[...])
        m_new = jnp.broadcast_to(top, (BLOCK, 128))
        p = jnp.exp2((s - jnp.concatenate([m_new, m_new], axis=1)) * scale)
        m_ref[h] = m_new
        l_ref[h] = p[:, :128] + p[:, 128:]
        acc_ref[h] = dot(p.astype(BF16), v_ref[h, rows, :])

    for i in reversed(range(N_SRC)):
        base = sc_ref[i]
        k_ref, v_ref = kv_refs[2 * i], kv_refs[2 * i + 1]
        lo = jnp.maximum(first_start - base, 0) // BLOCK
        hi = jnp.clip(q0 - base, 0, k_ref.shape[1]) // BLOCK

        def body(kb, carry, k_ref=k_ref, v_ref=v_ref, base=base):
            rows = pl.ds(pl.multiple_of(kb * BLOCK, BLOCK), BLOCK)
            bias_ref[...] = jnp.where(col_id + (base + kb * BLOCK) >= start, 0.0, NEG)
            for h in range(heads):
                s, top = weights(h, k_ref, rows, bias_ref[...])
                m_old = m_ref[h]
                m_new = jnp.maximum(m_old, top)
                p = jnp.exp2((s - jnp.concatenate([m_new, m_new], axis=1)) * scale)
                alpha = jnp.exp2((m_old - m_new) * scale)
                m_ref[h] = m_new
                l_ref[h] = l_ref[h] * alpha + (p[:, :128] + p[:, 128:])
                acc_ref[h] = acc_ref[h] * alpha + dot(p.astype(BF16), v_ref[h, rows, :])
            return carry

        lax.fori_loop(lo, hi, body, 0)
    for h in range(heads):
        total = jnp.sum(l_ref[h], axis=-1, keepdims=True)
        o_ref[:, h * head_dim:(h + 1) * head_dim] = (acc_ref[h] / total).astype(BF16)


def attention(scalars, q, seg_wide, kv_list):
    n_heads, tokens, head_dim = q.shape
    per = HEAD_GROUP
    groups = n_heads // per
    in_specs = [
        pl.BlockSpec((per, BLOCK, head_dim), lambda h, j, sc: (h, j, 0)),
        pl.BlockSpec((BLOCK, 128), lambda h, j, sc: (j, 0)),
    ]
    args = [q, seg_wide]
    for kv in kv_list:
        in_specs.append(pl.BlockSpec((per, tokens, head_dim), lambda h, j, sc: (h, 0, 0)))
        in_specs.append(pl.BlockSpec((per, tokens, head_dim), lambda h, j, sc: (h + groups, 0, 0)))
        args += [kv, kv]
    return pl.pallas_call(
        attn_kernel,
        grid_spec=pltpu.PrefetchScalarGridSpec(
            num_scalar_prefetch=1,
            grid=(groups, tokens // BLOCK),
            in_specs=in_specs,
            out_specs=pl.BlockSpec((BLOCK, per * head_dim), lambda h, j, sc: (j, h)),
            scratch_shapes=[pltpu.VMEM((per, BLOCK, 128), F32)] * 2
            + [pltpu.VMEM((per, BLOCK, head_dim), F32), pltpu.VMEM((BLOCK, BLOCK), F32)],
        ),
        out_shape=jax.ShapeDtypeStruct((tokens, n_heads * head_dim), BF16),
        compiler_params=params(("arbitrary", "arbitrary")),
        cost_estimate=cost(4 * n_heads * tokens * 2 * tokens * head_dim, 20e6, n_heads * tokens * tokens),
        name="attention",
    )(scalars, *args)


def solution(mesh):
    n_dev = mesh.shape['sp']
    swap_perm = [(d, d ^ 1) for d in range(n_dev)]
    cross_perm = [(d, d + 2) for d in range(n_dev - 2)]
    row_spec = P(('dp', 'sp'), None)
    tok_spec = P(('dp', 'sp'))
    replicated = P()

    def layers(x_rows, seg_ids, norm_gains, w_in, ssm_head, y_gain, w_out, mlp_up, mlp_down, w_qkv, w_attn_out):
        dev = lax.axis_index('sp')
        tokens, dim = x_rows.shape
        inner = y_gain.shape[0]
        n_heads = ssm_head.shape[1]
        n_chunks = tokens // CHUNK
        n_query, head_dim = w_attn_out.shape[:2]

        counts = jnp.sum((seg_ids[None, :] <= jnp.arange(4, dtype=jnp.int32)[:, None]).astype(jnp.int32), axis=1)
        earlier = [lax.ppermute(counts, 'sp', [(d, d + k) for d in range(n_dev - k)]) for k in range(1, n_dev)]
        seg_wide = jnp.broadcast_to(seg_ids[:, None], (tokens, 128))
        head_pad = jnp.pad(ssm_head, ((0, 5), (0, 128 - n_heads)))
        skip = jnp.repeat(ssm_head[2:3], inner // n_heads, axis=1)
        w_in_t = w_in.T
        hid, xs, bc, dt, cum = in_proj(x_rows, norm_gains, w_in_t, head_pad, inner, n_heads)
        first_pos = dev * tokens
        far = jnp.int32(1 << 24)
        pair_pos = (dev ^ 1) * tokens
        earlier, cum = lax.optimization_barrier((earlier, cum))
        doc_starts = counts + sum(earlier)
        slot = jnp.arange(4, dtype=jnp.int32)
        bases = jnp.where(slot == 3, first_pos, pair_pos)
        bases = jnp.where(slot >= 2, bases, jnp.where(dev >= 2, jnp.where(slot == 0, first_pos, pair_pos) - 2 * tokens, far))
        edge_seg = jnp.pad(seg_ids[::BLOCK], (0, 8 - tokens // BLOCK))
        scalars = jnp.concatenate([bases, doc_starts, edge_seg])
        state_end, decay = ssd_state(scalars, xs, bc, dt, cum, seg_wide)

        odd = (dev % 2) == 1
        pair_state = lax.ppermute(state_end, 'sp', swap_perm)
        pair_decay = lax.ppermute(decay, 'sp', swap_perm)
        chip_state = jnp.where(odd, decay * pair_state + state_end, pair_decay * state_end + pair_state)
        half = state_end.shape[0] // 2
        mine = jnp.where(odd, chip_state[half:], chip_state[:half])
        mine, hid, cum = lax.optimization_barrier((mine, hid, cum))
        got = lax.ppermute(mine, 'sp', cross_perm)
        z = z_proj(hid, w_in_t, inner)
        pack = jnp.stack([cum[:, :n_heads], dt[:, :n_heads]]).reshape(2, n_chunks, CHUNK, n_heads)
        pack = pack.transpose(1, 0, 3, 2).reshape(n_chunks, n_heads, 2 * CHUNK)
        pos = (first_pos + jnp.arange(tokens)).astype(F32)
        cos, sin = rope_tables(pos, head_dim)
        cos_far, sin_far = rope_tables(pos - 2.0 * tokens, head_dim)
        got, z, pack, cos, sin, cos_far, sin_far = lax.optimization_barrier((got, z, pack, cos, sin, cos_far, sin_far))
        other = lax.ppermute(got, 'sp', swap_perm)
        chip_in = jnp.where(odd, jnp.concatenate([other, got], axis=0), jnp.concatenate([got, other], axis=0))
        h_in = jnp.where(odd, pair_decay * chip_in + pair_state, chip_in)

        gated = ssd_full(scalars, xs, bc, dt, cum, seg_wide, pack, z, h_in, skip, y_gain[None, :])
        x_one = proj_add(gated, w_out, [x_rows])
        x_a = mlp(x_one, norm_gains, mlp_up, mlp_down, 0, 0, 2)
        far_a = lax.ppermute(x_a, 'sp', cross_perm)
        x_one, x_a = lax.optimization_barrier((x_one, x_a))
        x_b = mlp(x_one, norm_gains, mlp_up, mlp_down, 0, 1, 2)
        far_b = lax.ppermute(x_b, 'sp', cross_perm)
        w_heads = w_qkv.transpose(1, 0, 2)
        q, kv = qkv_proj(x_a, x_b, norm_gains, cos, sin, w_heads, n_query, True)
        kv_pair = lax.ppermute(kv, 'sp', swap_perm)
        far_a, far_b, q = lax.optimization_barrier((far_a, far_b, q))
        kv_far, = qkv_proj(far_a, far_b, norm_gains, cos_far, sin_far, w_heads, n_query, False)
        kv_far_pair = lax.ppermute(kv_far, 'sp', swap_perm)
        attn = attention(scalars, q, seg_wide, [kv_far, kv_far_pair, kv_pair, kv])
        x_three = proj_add(attn, w_attn_out.reshape(n_query * head_dim, dim), [x_a, x_b])
        return mlp(x_three, norm_gains, mlp_up, mlp_down, 1, 0, 1)

    return jax.shard_map(layers, mesh=mesh, in_specs=(row_spec, tok_spec) + (replicated,) * 9, out_specs=row_spec, check_vma=False)
```

profile of v0, /device:TPU:2, one launch (start us, length us, event | category | flops | bytes accessed | tf_op | source)
XLA Modules:
  0.0 370.2 jit_solution(4957493228880790370)
XLA Ops:
  0.0 0.8 convert_reduce_fusion
  0.8 0.7 collective-permute-start.2
  1.5 1.3 collective-permute-start.1
  2.8 2.4 collective-permute-start
  5.2 0.8 slice.20
  5.9 1.3 pad.8.head_ref
  7.2 0.0 copy-start.5
  7.2 15.4 %in_proj.1 = (bf16[768,1536]{1,0:T(8,128)(2,1)}, bf16[768,3072]{1,0:T(8,128)(2,1)}, bf16[768,256]{1,0:T(8,128)(2,1)}, f32[768,128]{1,0:T(8,128)}, f32[768,128]{1,0:T(8,128)}) custom-call(bf16[768,1536]{1,0:T(8,128)(2,1)} %refs_0_.1, f32[4,1536]{1,0:T(4,128)} %gain_ref.11, bf16[6448,1536]{1,0:T(8,128)(2,1)} %bitcast.16, f32[8,128]{1,0:T(8,128)} %pad.8.head_ref), custom_call_target="tpu_custom_call" | custom-call | flops 8455716864 | bytes 16000000 | tf_op jit(solution)/shard_map/in_proj/pallas_call | solution.py:88
  22.6 0.0 collective-permute-done.2
  22.7 0.0 collective-permute-done.1
  22.7 0.0 collective-permute-done
  22.7 0.7 pad_add_fusion.sc_ref
  23.4 0.0 copy-done.5
  23.4 0.9 broadcast_in_dim.37.seg_ref
  24.3 13.9 %ssd_state.1 = (f32[128,3072]{1,0:T(8,128)}, f32[1,3072]{1,0:T(1,128)}) custom-call(s32[16]{0:T(128)} %pad_add_fusion.sc_ref, bf16[768,3072]{1,0:T(8,128)(2,1)} %get-tuple-element.37.x_ref, bf16[768,256]{1,0:T(8,128)(2,1)} %get-tuple-element.38.bc_ref, f32[768,128]{1,0:T(8,128)} %get-tuple-element.39.dt_ref, f32[768,128]{1,0:T(8,128)} %get-tuple-element.44.cum_ref, ...), custom_call_target="tpu_custom_call" | custom-call | flops 1207959552 | bytes 8000000 | tf_op jit(solution)/shard_map/ssd_state/pallas_call | solution.py:180
  38.2 0.0 collective-permute-start.3
  38.2 2.8 fusion.1
  41.1 0.0 copy-start.1
  41.1 1.2 pad_maximum_fusion.2
  42.2 0.0 copy-start
  42.2 0.5 collective-permute-start.4
  42.7 1.2 pad_maximum_fusion
  43.9 0.0 copy-done.1
  43.9 0.9 copy.15
  44.8 0.0 collective-permute-done.4
  44.8 0.0 collective-permute-done.3
  44.8 0.0 copy-done
  44.8 1.0 add_select_fusion.1
  45.8 0.0 copy-start.2
  45.8 0.0 copy-start.3
  45.8 1.0 slice_select_fusion
  46.8 0.0 copy-done.2
  46.8 0.2 copy.14
  47.0 1.5 collective-permute-start.5
  48.4 0.0 copy-done.3
  48.5 0.9 reshape.32.pack_ref
  49.4 13.3 %z_proj.1.z_ref = f32[768,3072]{1,0:T(8,128)} custom-call(bf16[768,1536]{1,0:T(8,128)(2,1)} %get-tuple-element.46.h_ref, bf16[6448,1536]{1,0:T(8,128)(2,1)} %bitcast.17), custom_call_target="tpu_custom_call" | custom-call | flops 7247757312 | bytes 21000000 | tf_op jit(solution)/shard_map/z_proj/pallas_call | solution.py:119
  62.7 6.0 %collective-permute-done.5 = f32[64,3072]{1,0:T(8,128)} collective-permute-done((f32[64,3072]{1,0:T(8,128)}, f32[64,3072]{1,0:T(8,128)}, u32[]{:S(2)}, u32[]{:S(2)}) %collective-permute-start.5) | collective-permute-done | bytes 786464 | tf_op jit(solution)/shard_map/ppermute | solution.py:547
  68.6 0.0 collective-permute-start.6
  68.6 0.7 slice_bitcast_fusion
  69.3 0.1 broadcast_in_dim.38
  69.4 0.7 broadcast_in_dim.39.skip_ref
  70.1 1.1 collective-permute-done.6
  71.1 2.8 add_select_fusion.hin_ref
  73.9 26.6 %ssd_full.1.a_ref = bf16[768,3072]{1,0:T(8,128)(2,1)} custom-call(s32[16]{0:T(128)} %pad_add_fusion.sc_ref, bf16[768,3072]{1,0:T(8,128)(2,1)} %get-tuple-element.37.x_ref, bf16[768,256]{1,0:T(8,128)(2,1)} %get-tuple-element.38.bc_ref, f32[768,128]{1,0:T(8,128)} %get-tuple-element.39.dt_ref, f32[768,128]{1,0:T(8,128)} %get-tuple-element.44.cum_ref, ...), custom_call_target="tpu_custom_call" | custom-call | flops 12000000000 | bytes 20000000 | tf_op jit(solution)/shard_map/ssd_full/pallas_call | solution.py:248
  100.5 12.7 %proj_add.2.x_ref = bf16[768,1536]{1,0:T(8,128)(2,1)} custom-call(bf16[768,3072]{1,0:T(8,128)(2,1)} %ssd_full.1.a_ref, bf16[3072,1536]{1,0:T(8,128)(2,1)} %w_ref.1, bf16[768,1536]{1,0:T(8,128)(2,1)} %refs_0_.1), custom_call_target="tpu_custom_call" | custom-call | flops 7247757312 | bytes 18874368 | tf_op jit(solution)/shard_map/proj_add/pallas_call | solution.py:276
  113.2 31.6 %mlp.3.xa_ref.refs_0_ = bf16[384,1536]{1,0:T(8,128)(2,1)} custom-call(bf16[768,1536]{1,0:T(8,128)(2,1)} %proj_add.2.x_ref, f32[4,1536]{1,0:T(4,128)} %gain_ref.11, bf16[2,1536,12288]{2,1,0:T(8,128)(2,1)} %wu_ref.5, bf16[2,1536,12288]{2,1,0:T(8,128)(2,1)} %wu_ref.5, bf16[2,6144,1536]{2,1,0:T(8,128)(2,1)} %wd_ref.5), custom_call_target="tpu_custom_call" | custom-call | flops 21743271936 | bytes 56623104 | tf_op jit(solution)/shard_map/mlp/pallas_call | solution.py:313
  144.8 31.7 %mlp.4.xb_ref.refs_1_ = bf16[384,1536]{1,0:T(8,128)(2,1)} custom-call(bf16[768,1536]{1,0:T(8,128)(2,1)} %proj_add.2.x_ref, f32[4,1536]{1,0:T(4,128)} %gain_ref.11, bf16[2,1536,12288]{2,1,0:T(8,128)(2,1)} %wu_ref.5, bf16[2,1536,12288]{2,1,0:T(8,128)(2,1)} %wu_ref.5, bf16[2,6144,1536]{2,1,0:T(8,128)(2,1)} %wd_ref.5), custom_call_target="tpu_custom_call" | custom-call | flops 21743271936 | bytes 56623104 | tf_op jit(solution)/shard_map/mlp/pallas_call | solution.py:313
  176.5 1.3 collective-permute-start.8
  177.7 0.0 copy-done.4
  177.8 1.5 collective-permute-start.7
  179.3 20.6 %qkv.1 = (bf16[12,768,128]{2,1,0:T(8,128)(2,1)}, bf16[24,768,128]{2,1,0:T(8,128)(2,1)}) custom-call(bf16[384,1536]{1,0:T(8,128)(2,1)} %mlp.3.xa_ref.refs_0_, bf16[384,1536]{1,0:T(8,128)(2,1)} %mlp.4.xb_ref.refs_1_, f32[4,1536]{1,0:T(4,128)} %gain_ref.11, f32[768,128]{1,0:T(8,128)} %get-tuple-element.52.cos_ref, f32[768,128]{1,0:T(8,128)} %get-tuple-element.53.sin_ref, ...), custom_call_target="tpu_custom_call" | custom-call | flops 10871635968 | bytes 22155776 | tf_op jit(solution)/shard_map/qkv/pallas_call | solution.py:391
  199.9 0.1 collective-permute-start.10
  200.0 7.4 %collective-permute-done.8.xb_ref = bf16[384,1536]{1,0:T(8,128)(2,1)S(1)} collective-permute-done((bf16[384,1536]{1,0:T(8,128)(2,1)}, bf16[384,1536]{1,0:T(8,128)(2,1)S(1)}, u32[]{:S(2)}, u32[]{:S(2)}) %collective-permute-start.8) | collective-permute-done | bytes 1179680 | tf_op jit(solution)/shard_map/ppermute | solution.py:565
  207.4 24.4 %collective-permute-done.7.xa_ref = bf16[384,1536]{1,0:T(8,128)(2,1)S(1)} collective-permute-done((bf16[384,1536]{1,0:T(8,128)(2,1)S(1)}, bf16[384,1536]{1,0:T(8,128)(2,1)S(1)}, u32[]{:S(2)}, u32[]{:S(2)}) %collective-permute-start.7) | collective-permute-done | bytes 1179680 | tf_op jit(solution)/shard_map/ppermute | solution.py:562
  231.8 0.0 copy-done.6
  231.8 1.0 copy-done.7
  232.9 14.5 %kv.1.refs_0_.refs_1_ = bf16[24,768,128]{2,1,0:T(8,128)(2,1)} custom-call(bf16[384,1536]{1,0:T(8,128)(2,1)} %copy-done.7, bf16[384,1536]{1,0:T(8,128)(2,1)} %copy-done.6, f32[4,1536]{1,0:T(4,128)} %gain_ref.11, f32[768,128]{1,0:T(8,128)} %get-tuple-element.58.cos_ref, f32[768,128]{1,0:T(8,128)} %get-tuple-element.59.sin_ref, bf16[36,1536,128]{2,1,0:T(8,128)(2,1)} %bitcast.23), custom_call_target="tpu_custom_call" | custom-call | flops 7247757312 | bytes 17437184 | tf_op jit(solution)/shard_map/kv/pallas_call | solution.py:391
  247.3 0.0 collective-permute-start.9
  247.3 0.0 collective-permute-done.10.refs_4_.refs_5_
  247.3 8.2 %collective-permute-done.9.refs_2_.refs_3_ = bf16[24,768,128]{2,1,0:T(8,128)(2,1)} collective-permute-done((bf16[24,768,128]{2,1,0:T(8,128)(2,1)}, bf16[24,768,128]{2,1,0:T(8,128)(2,1)}, u32[]{:S(2)}, u32[]{:S(2)}) %collective-permute-start.9) | collective-permute-done | bytes 4718624 | tf_op jit(solution)/shard_map/ppermute | solution.py:571
  255.6 52.7 %attention.1.a_ref = bf16[768,1536]{1,0:T(8,128)(2,1)} custom-call(s32[16]{0:T(128)} %pad_add_fusion.sc_ref, bf16[12,768,128]{2,1,0:T(8,128)(2,1)} %get-tuple-element.55.q_ref, s32[768,128]{1,0:T(8,128)} %broadcast_in_dim.37.seg_ref, bf16[24,768,128]{2,1,0:T(8,128)(2,1)} %kv.1.refs_0_.refs_1_, bf16[24,768,128]{2,1,0:T(8,128)(2,1)} %kv.1.refs_0_.refs_1_, ...), custom_call_target="tpu_custom_call" | custom-call | flops 7247757312 | bytes 20000000 | tf_op jit(solution)/shard_map/attention/pallas_call | solution.py:488
  308.3 9.1 %proj_add.3.x_ref = bf16[768,1536]{1,0:T(8,128)(2,1)} custom-call(bf16[768,1536]{1,0:T(8,128)(2,1)} %attention.1.a_ref, bf16[1536,1536]{1,0:T(8,128)(2,1)} %bitcast.24, bf16[384,1536]{1,0:T(8,128)(2,1)} %mlp.3.xa_ref.refs_0_, bf16[384,1536]{1,0:T(8,128)(2,1)} %mlp.4.xb_ref.refs_1_), custom_call_target="tpu_custom_call" | custom-call | flops 3623878656 | bytes 11796480 | tf_op jit(solution)/shard_map/proj_add/pallas_call | solution.py:276
  317.3 52.8 %mlp.5 = bf16[768,1536]{1,0:T(8,128)(2,1)} custom-call(bf16[768,1536]{1,0:T(8,128)(2,1)} %proj_add.3.x_ref, f32[4,1536]{1,0:T(4,128)} %gain_ref.11, bf16[2,1536,12288]{2,1,0:T(8,128)(2,1)} %wu_ref.5, bf16[2,1536,12288]{2,1,0:T(8,128)(2,1)} %wu_ref.5, bf16[2,6144,1536]{2,1,0:T(8,128)(2,1)} %wd_ref.5), custom_call_target="tpu_custom_call" | custom-call | flops 43486543872 | bytes 56623104 | tf_op jit(solution)/shard_map/mlp/pallas_call | solution.py:313
  (9 shorter events, 0.1 us)
Async XLA Ops:
  0.8 21.8 %collective-permute-start.2 = (s32[4]{0:T(128)S(1)}, s32[4]{0:T(128)S(1)}, u32[]{:S(2)}, u32[]{:S(2)}) collective-permute-start(s32[4]{0:T(128)S(1)} %convert_reduce_fusion), channel_id=1, source_target_pairs={{0,3},{4,7}} | collective-permute-start | bytes 56 | tf_op jit(solution)/shard_map/ppermute | solution.py:522
  1.5 21.2 %collective-permute-start.1 = (s32[4]{0:T(128)S(1)}, s32[4]{0:T(128)S(1)}, u32[]{:S(2)}, u32[]{:S(2)}) collective-permute-start(s32[4]{0:T(128)S(1)} %convert_reduce_fusion), channel_id=1, source_target_pairs={{0,2},{1,3},{4,6},{5,7}} | collective-permute-start | bytes 56 | tf_op jit(solution)/shard_map/ppermute | solution.py:522
  2.8 19.9 %collective-permute-start = (s32[4]{0:T(128)S(1)}, s32[4]{0:T(128)S(1)}, u32[]{:S(2)}, u32[]{:S(2)}) collective-permute-start(s32[4]{0:T(128)S(1)} %convert_reduce_fusion), channel_id=1, source_target_pairs={{0,1},{1,2},{2,3},{4,5},{5,6},{6,7}} | collective-permute-start | bytes 56 | tf_op jit(solution)/shard_map/ppermute | solution.py:522
  7.2 16.2 %copy-start.5 = (s32[768]{0:T(1024)S(1)}, s32[768]{0:T(1024)}, u32[]{:S(2)}) copy-start(s32[768]{0:T(1024)} %param.12) | copy-start | bytes 9220
  38.2 6.6 %collective-permute-start.3 = (f32[128,3072]{1,0:T(8,128)}, f32[128,3072]{1,0:T(8,128)S(1)}, u32[]{:S(2)}, u32[]{:S(2)}) collective-permute-start(f32[128,3072]{1,0:T(8,128)} %get-tuple-element.42), channel_id=1, source_target_pairs={{0,1},{1,0},{2,3},{3,2},{4,5},{5,4},{6,7},{7,6}} | collective-permute-start | bytes 4718600 | tf_op jit(solution)/shard_map/ppermute | solution.py:541
  41.1 2.8 copy-start.1
  42.2 2.6 copy-start
  42.2 2.5 collective-permute-start.4
  45.8 1.0 copy-start.2
  45.8 2.6 copy-start.3
  47.0 21.7 %collective-permute-start.5 = (f32[64,3072]{1,0:T(8,128)}, f32[64,3072]{1,0:T(8,128)}, u32[]{:S(2)}, u32[]{:S(2)}) collective-permute-start(f32[64,3072]{1,0:T(8,128)} %slice_select_fusion), channel_id=1, source_target_pairs={{0,2},{1,3},{4,6},{5,7}} | collective-permute-start | bytes 2359304 | tf_op jit(solution)/shard_map/ppermute | solution.py:547
  68.6 2.5 collective-permute-start.6
  144.8 32.9 %copy-start.4 = (bf16[384,1536]{1,0:T(8,128)(2,1)S(1)}, bf16[384,1536]{1,0:T(8,128)(2,1)}, u32[]{:S(2)}) copy-start(bf16[384,1536]{1,0:T(8,128)(2,1)} %mlp.3.xa_ref.refs_0_) | copy-start | bytes 3538948
  176.5 30.9 %collective-permute-start.8 = (bf16[384,1536]{1,0:T(8,128)(2,1)}, bf16[384,1536]{1,0:T(8,128)(2,1)S(1)}, u32[]{:S(2)}, u32[]{:S(2)}) collective-permute-start(bf16[384,1536]{1,0:T(8,128)(2,1)} %mlp.4.xb_ref.refs_1_), channel_id=1, source_target_pairs={{0,2},{1,3},{4,6},{5,7}} | collective-permute-start | bytes 3538952 | tf_op jit(solution)/shard_map/ppermute | solution.py:565
  177.8 54.1 %collective-permute-start.7 = (bf16[384,1536]{1,0:T(8,128)(2,1)S(1)}, bf16[384,1536]{1,0:T(8,128)(2,1)S(1)}, u32[]{:S(2)}, u32[]{:S(2)}) collective-permute-start(bf16[384,1536]{1,0:T(8,128)(2,1)S(1)} %copy-done.4), channel_id=1, source_target_pairs={{0,2},{1,3},{4,6},{5,7}} | collective-permute-start | bytes 3538952 | tf_op jit(solution)/shard_map/ppermute | solution.py:562
  199.9 47.5 %collective-permute-start.10 = (bf16[24,768,128]{2,1,0:T(8,128)(2,1)}, bf16[24,768,128]{2,1,0:T(8,128)(2,1)}, u32[]{:S(2)}, u32[]{:S(2)}) collective-permute-start(bf16[24,768,128]{2,1,0:T(8,128)(2,1)} %get-tuple-element.60.refs_6_.refs_7_), channel_id=1, source_target_pairs={{0,1},{1,0},{2,3},{3,2},{4,5},{5,4},{6,7},{7,6}} | collective-permute-start | bytes 14155784 | tf_op jit(solution)/shard_map/ppermute | solution.py:568
  207.4 24.5 %copy-start.6 = (bf16[384,1536]{1,0:T(8,128)(2,1)}, bf16[384,1536]{1,0:T(8,128)(2,1)S(1)}, u32[]{:S(2)}) copy-start(bf16[384,1536]{1,0:T(8,128)(2,1)S(1)} %collective-permute-done.8.xb_ref) | copy-start | bytes 3538948
  231.8 1.0 copy-start.7
  247.3 8.3 %collective-permute-start.9 = (bf16[24,768,128]{2,1,0:T(8,128)(2,1)}, bf16[24,768,128]{2,1,0:T(8,128)(2,1)}, u32[]{:S(2)}, u32[]{:S(2)}) collective-permute-start(bf16[24,768,128]{2,1,0:T(8,128)(2,1)} %kv.1.refs_0_.refs_1_), channel_id=1, source_target_pairs={{0,1},{1,0},{2,3},{3,2},{4,5},{5,4},{6,7},{7,6}} | collective-permute-start | bytes 14155784 | tf_op jit(solution)/shard_map/ppermute | solution.py:571
where the time goes:
time: 372 us; the launch traced here: 370 us
  Pallas kernels  295 us (79%)
  waiting for transfers between devices  47.1 us (13%)
  other arithmetic  11.4 us (3%)
  starting transfers between devices  9.22 us (2%)
  local copies, waits for them, and re-layouts  7.38 us (2%)
    pallas_call x3, Pallas kernels, mlp(): pl.pallas_call(functools.partial(mlp_kernel, layer), grid=(n_ff,), in_spe...  116 us
    pallas_call x1, Pallas kernels, attention(): pl.pallas_call(attn_kernel, grid_spec=pltpu.PrefetchScalarGridSpec(num_sc...  52.7 us
    pallas_call x2, Pallas kernels, qkv_proj(): pl.pallas_call(functools.partial(qkv_kernel, n_q, n_rot), grid=(steps,),...  35.1 us
    pallas_call x1, Pallas kernels, ssd_full(): pl.pallas_call(ssd_full_kernel, grid=(tokens // CHUNK,), in_specs=[SMEM_S...  26.6 us
    ppermute x1, waiting for transfers between devices, layers(): far_a = lax.ppermute(x_a, 'sp', cross_perm)  24.4 us
    pallas_call x2, Pallas kernels, proj_add(): pl.pallas_call(proj_add_kernel, grid=(dim // tile,), in_specs=[full_spec(...  21.7 us
    pallas_call x1, Pallas kernels, in_proj(): pl.pallas_call(functools.partial(in_proj_kernel, n_heads), grid=(n_x + 1,...  15.4 us
    pallas_call x1, Pallas kernels, ssd_state(): pl.pallas_call(ssd_state_kernel, grid=(tokens // CHUNK,), in_specs=[SMEM_...  13.9 us
  transfers between devices with their start and end apart: 11, of which 5 were waited for; matrix products, arithmetic and copies ran while one was open for 3% of the time, Pallas kernels for 17%

commit v1 on v0

v1 whole, which is shorter than its diff:
```python
import functools
import math

import jax
import jax.numpy as jnp
from jax import lax
from jax.experimental import pallas as pl
from jax.experimental.pallas import tpu as pltpu
from jax.sharding import PartitionSpec as P


CHUNK = 64
NORM_EPS = 1e-6
ROPE_BASE = 10000.0
F32 = jnp.float32
BF16 = jnp.bfloat16
VMEM_LIMIT = 60 * 1024 * 1024
NT = (((1,), (1,)), ((), ()))


def dot(a, b, dims=(((1,), (0,)), ((), ()))):
    return lax.dot_general(a, b, dims, preferred_element_type=F32)


def params(sem):
    return pltpu.CompilerParams(dimension_semantics=sem, vmem_limit_bytes=VMEM_LIMIT)


def cost(flops, bytes_accessed, trans=0):
    return pl.CostEstimate(flops=int(flops), bytes_accessed=int(bytes_accessed), transcendentals=int(trans))


def norm_rows(values, gain):
    wide = values.astype(F32)
    inv = lax.rsqrt(jnp.mean(wide * wide, axis=-1, keepdims=True) + NORM_EPS)
    return (wide * inv * gain).astype(BF16)


SMEM_SPEC = pl.BlockSpec(memory_space=pltpu.SMEM)


def full_spec(shape):
    zeros = (0,) * len(shape)
    return pl.BlockSpec(shape, lambda *_: zeros)


def in_proj_kernel(n_heads, x_ref, gain_ref, w_ref, head_ref, h_ref, xs_ref, bc_ref, dt_ref, cum_ref):
    step = pl.program_id(0)

    @pl.when(step == 0)
    def _():
        hid = norm_rows(x_ref[...], gain_ref[0:1, :])
        h_ref[...] = hid
        n_bc = bc_ref.shape[1]
        out = dot(hid, w_ref[:n_bc + dt_ref.shape[1], :], NT)
        bc_ref[...] = out[:, :n_bc].astype(BF16)
        lanes = dt_ref.shape[1]
        raw = out[:, n_bc:n_bc + lanes] + head_ref[0:1, :]
        dt = jnp.maximum(raw, 0.0) + jnp.log1p(jnp.exp(-jnp.abs(raw)))
        lane = lax.broadcasted_iota(jnp.int32, dt.shape, 1)
        dt = jnp.where(lane < n_heads, dt, 0.0)
        dt_ref[...] = dt
        cum = dt * head_ref[1:2, :]
        row = lax.broadcasted_iota(jnp.int32, dt.shape, 0) % CHUNK
        shift = 1
        while shift < CHUNK:
            cum = cum + jnp.where(row >= shift, pltpu.roll(cum, shift, 0), 0.0)
            shift *= 2
        cum_ref[...] = cum

    @pl.when(step > 0)
    def _():
        xs_ref[...] = dot(h_ref[...], w_ref[...], NT).astype(BF16)


def in_proj(x_rows, gains, w_in_t, head_pad, inner, n_heads):
    tokens, dim = x_rows.shape
    tile = 1024
    n_x = inner // tile
    last = 2 * inner // tile
    out_shape = (
        jax.ShapeDtypeStruct((tokens, dim), BF16),
        jax.ShapeDtypeStruct((tokens, inner), BF16),
        jax.ShapeDtypeStruct((tokens, 256), BF16),
        jax.ShapeDtypeStruct((tokens, 128), F32),
        jax.ShapeDtypeStruct((tokens, 128), F32),
    )
    return pl.pallas_call(
        functools.partial(in_proj_kernel, n_heads),
        grid=(n_x + 1,),
        in_specs=[
            full_spec((tokens, dim)),
            full_spec(gains.shape),
            pl.BlockSpec((tile, dim), lambda i: (jnp.where(i == 0, last, i - 1), 0)),
            full_spec((8, 128)),
        ],
        out_specs=(
            full_spec((tokens, dim)),
            pl.BlockSpec((tokens, tile), lambda i: (0, jnp.maximum(i - 1, 0))),
            full_spec((tokens, 256)),
            full_spec((tokens, 128)),
            full_spec((tokens, 128)),
        ),
        out_shape=out_shape,
        compiler_params=params(("arbitrary",)),
        cost_estimate=cost(2 * tokens * dim * (inner + tile), 16e6),
        name="in_proj",
    )(x_rows, gains, w_in_t, head_pad)


def z_proj_kernel(h_ref, w_ref, z_ref):
    z = dot(h_ref[...], w_ref[...], NT)
    z_ref[...] = z * jax.nn.sigmoid(z)


def z_proj(hid, w_in_t, inner):
    tokens, dim = hid.shape
    tile = 1024
    first = inner // tile
    return pl.pallas_call(
        z_proj_kernel,
        grid=(inner // tile,),
        in_specs=[full_spec((tokens, dim)), pl.BlockSpec((tile, dim), lambda i: (i + first, 0))],
        out_specs=pl.BlockSpec((tokens, tile), lambda i: (0, i)),
        out_shape=jax.ShapeDtypeStruct((tokens, inner), F32),
        compiler_params=params(("arbitrary",)),
        cost_estimate=cost(2 * tokens * dim * inner, 21e6),
        name="z_proj",
    )(hid, w_in_t)


STEP = 2 * CHUNK
LOG2E = math.log2(math.e)


def split3(x):
    hi = x.astype(BF16).astype(F32)
    rest = x - hi
    mid = rest.astype(BF16).astype(F32)
    low = rest - mid
    return jnp.concatenate([hi + pltpu.roll(mid, 64, 1), low], axis=1).astype(BF16)


def fill_spread(e_ref):
    rows, width = e_ref.shape
    for g in range(width // 512):
        head = lax.broadcasted_iota(jnp.int32, (rows, 512), 0) % 64
        lane = lax.broadcasted_iota(jnp.int32, (rows, 512), 1) + g * 512
        e_ref[:, g * 512:(g + 1) * 512] = jnp.where(head == lane // 64, 1.0, 0.0).astype(BF16)


def step_weights(sc_ref, seg_ref, dt, cum2):
    row = lax.broadcasted_iota(jnp.int32, (STEP, 128), 0)
    start = doc_start(seg_ref[...], sc_ref, N_SRC) - (sc_ref[N_SRC - 1] + pl.program_id(0) * STEP)
    upper = row < CHUNK
    last = lambda v: jnp.where(upper, v[CHUNK - 1:CHUNK, :], v[STEP - 1:STEP, :])
    end_w = jnp.where(row >= last(start), jnp.exp2(last(cum2) - cum2), 0.0) * dt
    rel = jnp.where(upper, start, start - CHUNK)
    return rel, end_w


def half_rows(c):
    return slice(c * CHUNK, (c + 1) * CHUNK)


def b_transposed(bc_ref, c):
    return bc_ref[half_rows(c), :128].astype(F32).T.astype(BF16)


def ssd_state_kernel(sc_ref, x_ref, bc_ref, dt_ref, cum_ref, seg_ref, end_ref, decay_ref, e_ref, xp_ref, xw_ref):
    @pl.when(pl.program_id(0) == 0)
    def _():
        end_ref[...] = jnp.zeros_like(end_ref)
        decay_ref[...] = jnp.ones_like(decay_ref)
        fill_spread(e_ref)

    cum2 = cum_ref[...] * LOG2E
    rel, end_w = step_weights(sc_ref, seg_ref, dt_ref[...], cum2)
    lane = lax.broadcasted_iota(jnp.int32, (STEP, 128), 1)
    carry = jnp.where((rel < 0) & (lane < 64), jnp.exp2(cum2), 0.0)
    ends = [jnp.broadcast_to(carry[r:r + 1, :], (8, 128)) for r in (CHUNK - 1, STEP - 1)]
    xp_ref[...] = dot(split3(jnp.concatenate([end_w] + ends, axis=0)), e_ref[...])
    xw_ref[...] = (x_ref[...].astype(F32) * xp_ref[:STEP, :]).astype(BF16)
    add = [dot(b_transposed(bc_ref, c), xw_ref[half_rows(c), :]) for c in range(2)]
    dec = [xp_ref[STEP + 8 * c:STEP + 8 * c + 1, :] for c in range(2)]
    end_ref[...] = dec[1] * (dec[0] * end_ref[...] + add[0]) + add[1]
    decay_ref[...] = decay_ref[...] * dec[0] * dec[1]


def ssd_state(scalars, xs, bc, dt, cum, seg_wide):
    tokens, inner = xs.shape
    row = lambda width: pl.BlockSpec((STEP, width), lambda i: (i, 0))
    return pl.pallas_call(
        ssd_state_kernel,
        grid=(tokens // STEP,),
        in_specs=[SMEM_SPEC, row(inner), row(256), row(128), row(128), row(128)],
        out_specs=(full_spec((128, inner)), full_spec((1, inner))),
        out_shape=(jax.ShapeDtypeStruct((128, inner), F32), jax.ShapeDtypeStruct((1, inner), F32)),
        scratch_shapes=[pltpu.VMEM((256, inner), BF16), pltpu.VMEM((STEP + 16, inner), F32), pltpu.VMEM((STEP, inner), BF16)],
        compiler_params=params(("arbitrary",)),
        cost_estimate=cost(2 * tokens * 256 * inner, 8e6),
        name="ssd_state",
    )(scalars, xs, bc, dt, cum, seg_wide)


def ssd_full_kernel(sc_ref, x_ref, bc_ref, dt_ref, cum_ref, seg_ref, z_ref, hin_ref, skip_ref, gain_ref, out_ref,
                    state_ref, y_ref, e_ref, xp_ref, xw_ref, turn_ref, pack_ref):
    @pl.when(pl.program_id(0) == 0)
    def _():
        state_ref[...] = hin_ref[...]
        fill_spread(e_ref)

    inner = x_ref.shape[1]
    n_heads = inner // 64
    dt = dt_ref[...]
    cum2 = cum_ref[...] * LOG2E
    rel, end_w = step_weights(sc_ref, seg_ref, dt, cum2)
    xp_ref[...] = dot(split3(jnp.concatenate([cum2, end_w], axis=0)), e_ref[...])
    xw_ref[...] = (x_ref[...].astype(F32) * xp_ref[STEP:, :]).astype(BF16)

    turn_ref[0] = cum2.T
    turn_ref[1] = dt.T
    left = lax.broadcasted_iota(jnp.int32, (n_heads // 2, STEP), 1) < 64
    for k in range(2):
        even = turn_ref[k, pl.ds(0, n_heads // 2, stride=2), :]
        odd = turn_ref[k, pl.ds(1, n_heads // 2, stride=2), :]
        pack_ref[0, k] = jnp.where(left, even, pltpu.roll(odd, 64, 1))
        pack_ref[1, k] = jnp.where(left, pltpu.roll(even, 64, 1), odd)

    row_id = lax.broadcasted_iota(jnp.int32, (CHUNK, 128), 0)
    lane_id = lax.broadcasted_iota(jnp.int32, (CHUNK, 128), 1)
    left = lane_id < 64
    src = jnp.where(left, lane_id, lane_id - 64)
    for c in range(2):
        rows = half_rows(c)
        state = state_ref[...]
        opens = rel[rows] < 0
        c_open = jnp.where(opens, bc_ref[rows, 128:].astype(F32), 0.0).astype(BF16)
        carried = dot(c_open, state.astype(BF16))
        carry_x = jnp.exp2(xp_ref[rows, :])
        keep = jnp.where(opens[CHUNK - 1:CHUNK, :], 1.0, 0.0)
        dec = carry_x[CHUNK - 1:CHUNK, :] * jnp.concatenate([keep] * (inner // 128), axis=1)
        y_ref[rows, :] = carried * carry_x + skip_ref[...] * x_ref[rows, :].astype(F32)
        state_ref[...] = dec * state + dot(b_transposed(bc_ref, c), xw_ref[rows, :])

    for c in range(2):
        rows = half_rows(c)
        visible = (src >= rel[rows]) & (src <= row_id)
        b_blk = bc_ref[rows, :128]
        scores = dot(bc_ref[rows, 128:], jnp.concatenate([b_blk, b_blk], axis=0), NT)
        scores = jnp.where(visible, scores, 0.0)
        left16 = lax.broadcasted_iota(jnp.int32, (CHUNK, 128), 1) < 64
        zero = jnp.zeros((CHUNK, 128), BF16)
        for g in range(inner // 256):
            cols = slice(g * 256, (g + 1) * 256)
            mixes, diag = [], []
            for k in range(2):
                pair = 2 * g + k
                sub = slice(pair * 128, (pair + 1) * 128)
                cum_s = pack_ref[c, 0, pair:pair + 1, :]
                dt_s = pack_ref[c, 1, pair:pair + 1, :]
                decay = jnp.exp2(jnp.minimum(xp_ref[rows, sub] - cum_s, 0.0))
                mixes.append((scores * decay * dt_s).astype(BF16))
                xk = x_ref[rows, sub]
                for keep in (jnp.where(left16, xk, zero), jnp.where(left16, zero, xk)):
                    diag.append(jnp.concatenate([keep, zero] if k == 0 else [zero, keep], axis=1))
            y_ref[rows, cols] += dot(jnp.concatenate(mixes, axis=1), jnp.concatenate(diag, axis=0))

    y = y_ref[...]
    inv = lax.rsqrt(jnp.mean(y * y, axis=-1, keepdims=True) + NORM_EPS)
    out_ref[...] = (y * inv * gain_ref[...] * z_ref[...]).astype(BF16)


def ssd_full(scalars, xs, bc, dt, cum, seg_wide, z, h_in, skip, gain):
    tokens, inner = xs.shape
    row = lambda width: pl.BlockSpec((STEP, width), lambda i: (i, 0))
    return pl.pallas_call(
        ssd_full_kernel,
        grid=(tokens // STEP,),
        in_specs=[
            SMEM_SPEC, row(inner), row(256), row(128), row(128), row(128),
            row(inner), full_spec((128, inner)), full_spec((1, inner)), full_spec((1, inner)),
        ],
        out_specs=row(inner),
        out_shape=jax.ShapeDtypeStruct((tokens, inner), BF16),
        scratch_shapes=[
            pltpu.VMEM((128, inner), F32), pltpu.VMEM((STEP, inner), F32), pltpu.VMEM((256, inner), BF16),
            pltpu.VMEM((2 * STEP, inner), F32), pltpu.VMEM((STEP, inner), BF16), pltpu.VMEM((2, 128, STEP), F32),
            pltpu.VMEM((2, 2, inner // 128, STEP), F32),
        ],
        compiler_params=params(("arbitrary",)),
        cost_estimate=cost(12e9, 20e6),
        name="ssd_full",
    )(scalars, xs, bc, dt, cum, seg_wide, z, h_in, skip, gain)


def proj_add_kernel(a_ref, w_ref, *refs):
    out_ref = refs[-1]
    res = jnp.concatenate([r[...] for r in refs[:-1]], axis=0)
    out_ref[...] = (res.astype(F32) + dot(a_ref[...], w_ref[...])).astype(BF16)


def proj_add(a, w, res):
    tokens, depth = a.shape
    dim = w.shape[1]
    tile = 512
    col = lambda rows: pl.BlockSpec((rows, tile), lambda i: (0, i))
    return pl.pallas_call(
        proj_add_kernel,
        grid=(dim // tile,),
        in_specs=[full_spec((tokens, depth)), col(depth)] + [col(r.shape[0]) for r in res],
        out_specs=col(tokens),
        out_shape=jax.ShapeDtypeStruct((tokens, dim), BF16),
        compiler_params=params(("arbitrary",)),
        cost_estimate=cost(2 * tokens * depth * dim, 2 * (tokens * depth + depth * dim + 2 * tokens * dim)),
        name="proj_add",
    )(a, w, *res)


def mlp_kernel(layer, x_ref, gain_ref, wg_ref, wu_ref, wd_ref, out_ref, h_ref, acc_ref):
    step = pl.program_id(0)

    @pl.when(step == 0)
    def _():
        h_ref[...] = norm_rows(x_ref[...], gain_ref[2 * layer + 1:2 * layer + 2, :])
        acc_ref[...] = jnp.zeros_like(acc_ref)

    hid = h_ref[...]
    gate = dot(hid, wg_ref[0])
    up = dot(hid, wu_ref[0])
    act = (gate * jax.nn.sigmoid(gate) * up).astype(BF16)
    acc_ref[...] += dot(act, wd_ref[0])

    @pl.when(step == pl.num_programs(0) - 1)
    def _():
        out_ref[...] = (x_ref[...].astype(F32) + acc_ref[...]).astype(BF16)


def mlp(x_rows, gains, mlp_up, mlp_down, layer, part, parts):
    tokens, dim = x_rows.shape
    tokens //= parts
    ff = mlp_down.shape[1]
    tile = 1024
    n_ff = ff // tile
    return pl.pallas_call(
        functools.partial(mlp_kernel, layer),
        grid=(n_ff,),
        in_specs=[
            pl.BlockSpec((tokens, dim), lambda i: (part, 0)),
            full_spec(gains.shape),
            pl.BlockSpec((1, dim, tile), lambda i: (layer, 0, i)),
            pl.BlockSpec((1, dim, tile), lambda i: (layer, 0, i + n_ff)),
            pl.BlockSpec((1, tile, dim), lambda i: (layer, i, 0)),
        ],
        out_specs=full_spec((tokens, dim)),
        out_shape=jax.ShapeDtypeStruct((tokens, dim), BF16),
        scratch_shapes=[pltpu.VMEM((tokens, dim), BF16), pltpu.VMEM((tokens, dim), F32)],
        compiler_params=params(("arbitrary",)),
        cost_estimate=cost(6 * tokens * dim * ff, 6 * dim * ff),
        name="mlp",
    )(x_rows, gains, mlp_up, mlp_up, mlp_down)


def rope_tables(positions, head_dim):
    half = head_dim // 2
    inv_freq = ROPE_BASE ** (-jnp.arange(half, dtype=F32) * 2.0 / head_dim)
    angle = positions[:, None] * inv_freq[None, :]
    cos, sin = jnp.cos(angle), jnp.sin(angle)
    return jnp.concatenate([cos, cos], axis=1), jnp.concatenate([-sin, sin], axis=1)


def qkv_kernel(n_q, n_rot, n_parts, *refs):
    x_refs = refs[:n_parts]
    gain_ref, cos_ref, sin_ref, w_ref = refs[n_parts:n_parts + 4]
    kv_ref, h_ref = refs[-2:]
    step = pl.program_id(0)

    @pl.when(step == 0)
    def _():
        first = 0
        for x_ref in x_refs:
            h_ref[first:first + x_ref.shape[0]] = norm_rows(x_ref[...], gain_ref[2:3, :])
            first += x_ref.shape[0]

    heads, _, head_dim = w_ref.shape
    turns = step < n_rot
    cos = jnp.where(turns, cos_ref[...], 1.0)
    sin = jnp.where(turns, sin_ref[...], 0.0)
    for k in range(0, heads, 2):
        out = dot(h_ref[...], jnp.concatenate([w_ref[k], w_ref[k + 1]], axis=1))
        for i in range(2):
            val = out[:, i * head_dim:(i + 1) * head_dim]
            kv_ref[k + i] = (val * cos + pltpu.roll(val, head_dim // 2, 1) * sin).astype(BF16)

    if n_q:
        @pl.when(step < n_q)
        def _():
            refs[n_parts + 4][...] = kv_ref[...]


def qkv_proj(parts, gains, cos, sin, table_part, w_heads, n_query, with_q):
    tokens = sum(x.shape[0] for x in parts)
    dim = parts[0].shape[1]
    n_heads, _, head_dim = w_heads.shape
    n_kv = n_heads - n_query
    per = 6
    n_q = n_query // per if with_q else 0
    skip = 0 if with_q else n_query // per
    n_rot = n_q + n_kv // 2 // per
    steps = n_heads // per - skip
    out_specs = [pl.BlockSpec((per, tokens, head_dim), lambda i: (jnp.maximum(i - n_q, 0), 0, 0))]
    out_shape = [jax.ShapeDtypeStruct((n_kv, tokens, head_dim), BF16)]
    if with_q:
        out_specs.insert(0, pl.BlockSpec((per, tokens, head_dim), lambda i: (jnp.minimum(i, n_q - 1), 0, 0)))
        out_shape.insert(0, jax.ShapeDtypeStruct((n_query, tokens, head_dim), BF16))
    table = pl.BlockSpec((tokens, head_dim), lambda i: (table_part, 0))
    return pl.pallas_call(
        functools.partial(qkv_kernel, n_q, n_rot, len(parts)),
        grid=(steps,),
        in_specs=[full_spec(x.shape) for x in parts] + [
            full_spec(gains.shape), table, table, pl.BlockSpec((per, dim, head_dim), lambda i: (i + skip, 0, 0)),
        ],
        out_specs=tuple(out_specs),
        out_shape=tuple(out_shape),
        scratch_shapes=[pltpu.VMEM((tokens, dim), BF16)],
        compiler_params=params(("arbitrary",)),
        cost_estimate=cost(2 * tokens * dim * steps * per * head_dim, 2 * dim * steps * per * head_dim + 8e6),
        name="qkv" if with_q else "kv",
    )(*parts, gains, cos, sin, w_heads)


BLOCK = 256
HEAD_GROUP = 4
N_SRC = 4
NEG = -1e30


def doc_start(seg, sc_ref, first):
    start = jnp.zeros_like(seg)
    for doc in range(4):
        start = jnp.where(seg > doc, sc_ref[first + doc], start)
    return start


def attn_kernel(sc_ref, q_ref, seg_ref, *refs):
    far_refs, near_refs = refs[:8], refs[8:12]
    o_ref, m_ref, l_ref, acc_ref, bias_ref = refs[12:]
    j = pl.program_id(1)
    heads, _, head_dim = q_ref.shape
    every = range(heads)
    scale = (head_dim ** -0.5) * math.log2(math.e)
    q0 = sc_ref[N_SRC - 1] + j * BLOCK
    first_start = doc_start(sc_ref[N_SRC + 4 + j], sc_ref, N_SRC)
    start = doc_start(seg_ref[...], sc_ref, N_SRC)

    def lanes(x, width):
        return jnp.concatenate([x] * (width // 128), axis=1)

    def fold(x):
        return sum(x[:, i:i + 128] for i in range(128, x.shape[1], 128)) + x[:, :128]

    def weights(h, k_ref, rows, bias):
        s = dot(q_ref[h], k_ref[h, rows, :], NT) + bias
        return s, jnp.max(s, axis=-1, keepdims=True)

    k_ref, v_ref = near_refs[2:]
    rows = pl.ds(pl.multiple_of(j * BLOCK, BLOCK), BLOCK)
    col_id = lax.broadcasted_iota(jnp.int32, (BLOCK, BLOCK), 1)
    row_id = lax.broadcasted_iota(jnp.int32, (BLOCK, BLOCK), 0)
    bias_ref[...] = jnp.where((col_id + q0 >= lanes(start, BLOCK)) & (col_id <= row_id), 0.0, NEG)
    for h in every:
        s, top = weights(h, k_ref, rows, bias_ref[...])
        m_new = jnp.broadcast_to(top, (BLOCK, 128))
        p = jnp.exp2((s - lanes(m_new, BLOCK)) * scale)
        m_ref[h] = m_new
        l_ref[h] = fold(p)
        acc_ref[h] = dot(p.astype(BF16), v_ref[h, rows, :])

    def update(k_ref, v_ref, rows, width, first_col):
        col = lax.broadcasted_iota(jnp.int32, (BLOCK, width), 1) + first_col
        bias = jnp.where(col >= lanes(start, width), 0.0, NEG)
        old = [(m_ref[h], l_ref[h], acc_ref[h]) for h in every]
        scored = [weights(h, k_ref, rows, bias) for h in every]
        m_new = [jnp.maximum(old[h][0], scored[h][1]) for h in every]
        p = [jnp.exp2((scored[h][0] - lanes(m_new[h], width)) * scale) for h in every]
        alpha = [jnp.exp2((old[h][0] - m_new[h]) * scale) for h in every]
        l_new = [old[h][1] * alpha[h] + fold(p[h]) for h in every]
        a_new = [old[h][2] * alpha[h] + dot(p[h].astype(BF16), v_ref[h, rows, :]) for h in every]
        for h in every:
            m_ref[h] = m_new[h]
            l_ref[h] = l_new[h]
            acc_ref[h] = a_new[h]

    for i in (1, 0):
        base = sc_ref[N_SRC - 2 + i]
        k_ref, v_ref = near_refs[2 * i], near_refs[2 * i + 1]
        lo = jnp.maximum(first_start - base, 0) // BLOCK
        hi = jnp.clip(q0 - base, 0, k_ref.shape[1]) // BLOCK

        def body(kb, carry, k_ref=k_ref, v_ref=v_ref, base=base):
            update(k_ref, v_ref, pl.ds(pl.multiple_of(kb * BLOCK, BLOCK), BLOCK), BLOCK, base + kb * BLOCK)
            return carry

        lax.fori_loop(lo, hi, body, 0)

    for i in range(4):
        k_ref, v_ref = far_refs[2 * i], far_refs[2 * i + 1]
        width = k_ref.shape[1]
        base = sc_ref[i // 2] + (i % 2) * width

        @pl.when((base < q0) & (first_start < base + width))
        def _(k_ref=k_ref, v_ref=v_ref, base=base, width=width):
            update(k_ref, v_ref, slice(None), width, base)

    for h in every:
        total = jnp.sum(l_ref[h], axis=-1, keepdims=True)
        o_ref[:, h * head_dim:(h + 1) * head_dim] = (acc_ref[h] / total).astype(BF16)


def attention(scalars, q, seg_wide, kv_list):
    n_heads, tokens, head_dim = q.shape
    per = HEAD_GROUP
    groups = n_heads // per
    in_specs = [
        pl.BlockSpec((per, BLOCK, head_dim), lambda h, j, sc: (h, j, 0)),
        pl.BlockSpec((BLOCK, 128), lambda h, j, sc: (j, 0)),
    ]
    args = [q, seg_wide]
    for kv in kv_list:
        rows = kv.shape[1]
        in_specs.append(pl.BlockSpec((per, rows, head_dim), lambda h, j, sc: (h, 0, 0)))
        in_specs.append(pl.BlockSpec((per, rows, head_dim), lambda h, j, sc: (h + groups, 0, 0)))
        args += [kv, kv]
    return pl.pallas_call(
        attn_kernel,
        grid_spec=pltpu.PrefetchScalarGridSpec(
            num_scalar_prefetch=1,
            grid=(groups, tokens // BLOCK),
            in_specs=in_specs,
            out_specs=pl.BlockSpec((BLOCK, per * head_dim), lambda h, j, sc: (j, h)),
            scratch_shapes=[pltpu.VMEM((per, BLOCK, 128), F32)] * 2
            + [pltpu.VMEM((per, BLOCK, head_dim), F32), pltpu.VMEM((BLOCK, BLOCK), F32)],
        ),
        out_shape=jax.ShapeDtypeStruct((tokens, n_heads * head_dim), BF16),
        compiler_params=params(("arbitrary", "arbitrary")),
        cost_estimate=cost(4 * n_heads * tokens * 2 * tokens * head_dim, 20e6, n_heads * tokens * tokens),
        name="attention",
    )(scalars, *args)


def solution(mesh):
    n_dev = mesh.shape['sp']
    swap_perm = [(d, d ^ 1) for d in range(n_dev)]
    cross_perm = [(d, d + 2) for d in range(n_dev - 2)]
    row_spec = P(('dp', 'sp'), None)
    tok_spec = P(('dp', 'sp'))
    replicated = P()

    def layers(x_rows, seg_ids, norm_gains, w_in, ssm_head, y_gain, w_out, mlp_up, mlp_down, w_qkv, w_attn_out):
        dev = lax.axis_index('sp')
        tokens, dim = x_rows.shape
        inner = y_gain.shape[0]
        n_heads = ssm_head.shape[1]
        n_query, head_dim = w_attn_out.shape[:2]

        counts = jnp.sum((seg_ids[None, :] <= jnp.arange(4, dtype=jnp.int32)[:, None]).astype(jnp.int32), axis=1)
        earlier = [lax.ppermute(counts, 'sp', [(d, d + k) for d in range(n_dev - k)]) for k in range(1, n_dev)]
        seg_wide = jnp.broadcast_to(seg_ids[:, None], (tokens, 128))
        head_pad = jnp.pad(ssm_head, ((0, 5), (0, 128 - n_heads)))
        skip = jnp.repeat(ssm_head[2:3], inner // n_heads, axis=1)
        w_in_t = w_in.T
        hid, xs, bc, dt, cum = in_proj(x_rows, norm_gains, w_in_t, head_pad, inner, n_heads)
        first_pos = dev * tokens
        far = jnp.int32(1 << 24)
        pair_pos = (dev ^ 1) * tokens
        earlier, cum = lax.optimization_barrier((earlier, cum))
        doc_starts = counts + sum(earlier)
        slot = jnp.arange(4, dtype=jnp.int32)
        bases = jnp.where(slot == 3, first_pos, pair_pos)
        bases = jnp.where(slot >= 2, bases, jnp.where(dev >= 2, jnp.where(slot == 0, first_pos, pair_pos) - 2 * tokens, far))
        edge_seg = jnp.pad(seg_ids[::BLOCK], (0, 8 - tokens // BLOCK))
        scalars = jnp.concatenate([bases, doc_starts, edge_seg])
        state_end, decay = ssd_state(scalars, xs, bc, dt, cum, seg_wide)

        odd = (dev % 2) == 1
        pair_state = lax.ppermute(state_end, 'sp', swap_perm)
        pair_decay = lax.ppermute(decay, 'sp', swap_perm)
        chip_state = jnp.where(odd, decay * pair_state + state_end, pair_decay * state_end + pair_state)
        half = state_end.shape[0] // 2
        mine = jnp.where(odd, chip_state[half:], chip_state[:half])
        mine, hid = lax.optimization_barrier((mine, hid))
        got = lax.ppermute(mine, 'sp', cross_perm)
        z = z_proj(hid, w_in_t, inner)
        pos = (first_pos + jnp.arange(tokens)).astype(F32)
        cos, sin = rope_tables(pos, head_dim)
        cos_far, sin_far = rope_tables(pos - 2.0 * tokens, head_dim)
        got, z, cos, sin, cos_far, sin_far = lax.optimization_barrier((got, z, cos, sin, cos_far, sin_far))
        other = lax.ppermute(got, 'sp', swap_perm)
        chip_in = jnp.where(odd, jnp.concatenate([other, got], axis=0), jnp.concatenate([got, other], axis=0))
        h_in = jnp.where(odd, pair_decay * chip_in + pair_state, chip_in)

        gated = ssd_full(scalars, xs, bc, dt, cum, seg_wide, z, h_in, skip, y_gain[None, :])
        x_one = proj_add(gated, w_out, [x_rows])
        x_a = mlp(x_one, norm_gains, mlp_up, mlp_down, 0, 0, 2)
        far_a = lax.ppermute(x_a, 'sp', cross_perm)
        x_one, x_a = lax.optimization_barrier((x_one, x_a))
        x_b = mlp(x_one, norm_gains, mlp_up, mlp_down, 0, 1, 2)
        far_b = lax.ppermute(x_b, 'sp', cross_perm)
        w_heads = w_qkv.transpose(1, 0, 2)
        q, kv = qkv_proj([x_a, x_b], norm_gains, cos, sin, 0, w_heads, n_query, True)
        kv_pair = lax.ppermute(kv, 'sp', swap_perm)
        far_a, q = lax.optimization_barrier((far_a, q))
        kv_far_a, = qkv_proj([far_a], norm_gains, cos_far, sin_far, 0, w_heads, n_query, False)
        kv_fp_a = lax.ppermute(kv_far_a, 'sp', swap_perm)
        far_b, kv_far_a = lax.optimization_barrier((far_b, kv_far_a))
        kv_far_b, = qkv_proj([far_b], norm_gains, cos_far, sin_far, 1, w_heads, n_query, False)
        kv_fp_b = lax.ppermute(kv_far_b, 'sp', swap_perm)
        attn = attention(scalars, q, seg_wide, [kv_far_a, kv_far_b, kv_fp_a, kv_fp_b, kv_pair, kv])
        x_three = proj_add(attn, w_attn_out.reshape(n_query * head_dim, dim), [x_a, x_b])
        return mlp(x_three, norm_gains, mlp_up, mlp_down, 1, 0, 1)

    return jax.shard_map(layers, mesh=mesh, in_specs=(row_spec, tok_spec) + (replicated,) * 9, out_specs=row_spec, check_vma=False)
```

time: 372 us -> 360 us (0.968); the launches traced: 370 us -> 354 us
  Pallas kernels: 295 us -> 268 us
  waiting for transfers between devices: 47.1 us -> 57.3 us
    pallas_call x1, Pallas kernels: 52.7 us -> 41.3 us  [attention(): pl.pallas_call(attn_kernel, grid_spec=pltpu.PrefetchScalarGridSpec(num_sc...]
    pallas_call x4 -> x5, Pallas kernels: 75.6 us -> 65.5 us  [the longest x3 37.5 us: qkv_proj(): pl.pallas_call(functools.partial(qkv_kernel, n_q, n_rot, len(parts)), gri...]
    ppermute x1, waiting for transfers between devices: 7.38 us -> 14.3 us  [layers(): far_b = lax.ppermute(x_b, 'sp', cross_perm)]
    ppermute x1 -> x2, waiting for transfers between devices: 8.24 us -> 7.6 us  [the longest x1 4.23 us: layers(): kv_fp_b = lax.ppermute(kv_far_b, 'sp', swap_perm)]
  transfers between devices with their start and end apart: 11 -> 12, of which waited for: 5 -> 6; matrix products, arithmetic and copies ran while one was open for 3% -> 3% of each run, Pallas kernels for 17% -> 13%
where the time goes in v1:
time: 360 us; the launch traced here: 354 us
  Pallas kernels  268 us (74%)
  waiting for transfers between devices  57.3 us (16%)
  other arithmetic  10.1 us (3%)
  starting transfers between devices  9.76 us (3%)
  local copies, waits for them, and re-layouts  7.93 us (2%)
    pallas_call x3, Pallas kernels, mlp(): pl.pallas_call(functools.partial(mlp_kernel, layer), grid=(n_ff,), in_spe...  114 us
    pallas_call x1, Pallas kernels, attention(): pl.pallas_call(attn_kernel, grid_spec=pltpu.PrefetchScalarGridSpec(num_sc...  41.3 us
    pallas_call x3, Pallas kernels, qkv_proj(): pl.pallas_call(functools.partial(qkv_kernel, n_q, n_rot, len(parts)), gri...  37.5 us
    ppermute x1, waiting for transfers between devices, layers(): far_a = lax.ppermute(x_a, 'sp', cross_perm)  28.1 us
    pallas_call x2, Pallas kernels, proj_add(): pl.pallas_call(proj_add_kernel, grid=(dim // tile,), in_specs=[full_spec(...  20.4 us
    pallas_call x1, Pallas kernels, ssd_full(): pl.pallas_call(ssd_full_kernel, grid=(tokens // STEP,), in_specs=[SMEM_SP...  19 us
    pallas_call x1, Pallas kernels, in_proj(): pl.pallas_call(functools.partial(in_proj_kernel, n_heads), grid=(n_x + 1,...  14.5 us
    ppermute x1, waiting for transfers between devices, layers(): far_b = lax.ppermute(x_b, 'sp', cross_perm)  14.3 us
  transfers between devices with their start and end apart: 12, of which 6 were waited for; matrix products, arithmetic and copies ran while one was open for 3% of the time, Pallas kernels for 13%

profile of v1, /device:TPU:2, one launch (start us, length us, event | category | flops | bytes accessed | tf_op | source)
XLA Modules:
  0.0 353.8 jit_solution(9777821296976629944)
XLA Ops:
  0.0 0.8 convert_reduce_fusion
  0.8 0.7 collective-permute-start.2
  1.5 1.3 collective-permute-start.1
  2.8 2.4 collective-permute-start
  5.2 0.8 slice.14
  5.9 1.3 pad.8.head_ref
  7.2 0.0 copy-start.9
  7.2 14.5 %in_proj.1 = (bf16[768,1536]{1,0:T(8,128)(2,1)}, bf16[768,3072]{1,0:T(8,128)(2,1)}, bf16[768,256]{1,0:T(8,128)(2,1)}, f32[768,128]{1,0:T(8,128)}, f32[768,128]{1,0:T(8,128)}) custom-call(bf16[768,1536]{1,0:T(8,128)(2,1)} %refs_0_.1, f32[4,1536]{1,0:T(4,128)} %gain_ref.7, bf16[6448,1536]{1,0:T(8,128)(2,1)} %bitcast.11, f32[8,128]{1,0:T(8,128)} %pad.8.head_ref), custom_call_target="tpu_custom_call" | custom-call | flops 9663676416 | bytes 16000000 | tf_op jit(solution)/shard_map/in_proj/pallas_call | solution.py:88
  21.7 0.0 collective-permute-done.2
  21.7 0.0 collective-permute-done.1
  21.7 0.0 collective-permute-done
  21.7 0.7 pad_add_fusion.sc_ref
  22.4 0.0 copy-done.9
  22.4 0.9 broadcast_in_dim.37.seg_ref
  23.3 8.9 %ssd_state.1 = (f32[128,3072]{1,0:T(8,128)}, f32[1,3072]{1,0:T(1,128)}) custom-call(s32[16]{0:T(128)} %pad_add_fusion.sc_ref, bf16[768,3072]{1,0:T(8,128)(2,1)} %get-tuple-element.36.x_ref, bf16[768,256]{1,0:T(8,128)(2,1)} %get-tuple-element.37.bc_ref, f32[768,128]{1,0:T(8,128)} %get-tuple-element.38.dt_ref, f32[768,128]{1,0:T(8,128)} %get-tuple-element.39.cum_ref, ...), custom_call_target="tpu_custom_call" | custom-call | flops 1207959552 | bytes 8000000 | tf_op jit(solution)/shard_map/ssd_state/pallas_call | solution.py:193
  32.2 0.0 collective-permute-start.3
  32.3 3.9 %fusion.1 = (f32[768,64]{1,0:T(8,128)S(1)}, f32[768,64]{1,0:T(8,128)S(1)}, f32[768,64]{1,0:T(8,128)S(1)}, f32[768,64]{1,0:T(8,128)S(1)}, f32[768,64]{1,0:T(8,128)}, /*index=5*/f32[768,64]{1,0:T(8,128)}) fusion(f32[64]{0:T(128)S(1)} %multiply_power_fusion, f32[768]{0:T(1024)S(1)} %broadcast_add_fusion, f32[768]{0:T(1024)S(1)} %add_convert_fusion), kind=kLoop, calls=%fused_computation.13 | loop fusion | flops 196608 | bytes 1186048 | tf_op jit(solution)/shard_map/neg | solution.py:369
  36.1 0.5 collective-permute-start.4
  36.6 1.2 pad_maximum_fusion.2
  37.8 0.0 collective-permute-done.4
  37.8 0.0 collective-permute-done.3
  37.8 0.0 copy-done.3
  37.8 1.0 add_select_fusion.1
  38.8 0.0 copy-start.4
  38.8 0.0 copy-start.5
  38.8 0.1 slice_select_fusion
  38.9 1.7 collective-permute-start.5
  40.6 0.0 copy-done.4
  40.6 0.0 copy-done.5
  40.6 1.2 pad_maximum_fusion
  41.8 12.6 %z_proj.1.z_ref = f32[768,3072]{1,0:T(8,128)} custom-call(bf16[768,1536]{1,0:T(8,128)(2,1)} %get-tuple-element.44.h_ref, bf16[6448,1536]{1,0:T(8,128)(2,1)} %bitcast.12), custom_call_target="tpu_custom_call" | custom-call | flops 7247757312 | bytes 21000000 | tf_op jit(solution)/shard_map/z_proj/pallas_call | solution.py:120
  54.5 6.4 %collective-permute-done.5 = f32[64,3072]{1,0:T(8,128)S(1)} collective-permute-done((f32[64,3072]{1,0:T(8,128)S(1)}, f32[64,3072]{1,0:T(8,128)S(1)}, u32[]{:S(2)}, u32[]{:S(2)}) %collective-permute-start.5) | collective-permute-done | bytes 786464 | tf_op jit(solution)/shard_map/ppermute | solution.py:592
  60.9 0.0 collective-permute-start.6
  60.9 0.7 slice_bitcast_fusion
  61.6 0.1 broadcast_in_dim.38
  61.7 0.7 broadcast_in_dim.39.skip_ref
  62.3 0.8 collective-permute-done.6
  63.2 1.4 add_select_fusion.hin_ref
  64.6 19.0 %ssd_full.1.a_ref = bf16[768,3072]{1,0:T(8,128)(2,1)} custom-call(s32[16]{0:T(128)} %pad_add_fusion.sc_ref, bf16[768,3072]{1,0:T(8,128)(2,1)} %get-tuple-element.36.x_ref, bf16[768,256]{1,0:T(8,128)(2,1)} %get-tuple-element.37.bc_ref, f32[768,128]{1,0:T(8,128)} %get-tuple-element.38.dt_ref, f32[768,128]{1,0:T(8,128)} %get-tuple-element.39.cum_ref, ...), custom_call_target="tpu_custom_call" | custom-call | flops 12000000000 | bytes 20000000 | tf_op jit(solution)/shard_map/ssd_full/pallas_call | solution.py:277
  83.5 12.3 %proj_add.2.x_ref = bf16[768,1536]{1,0:T(8,128)(2,1)} custom-call(bf16[768,3072]{1,0:T(8,128)(2,1)} %ssd_full.1.a_ref, bf16[3072,1536]{1,0:T(8,128)(2,1)} %w_ref.1, bf16[768,1536]{1,0:T(8,128)(2,1)} %refs_0_.1), custom_call_target="tpu_custom_call" | custom-call | flops 7247757312 | bytes 18874368 | tf_op jit(solution)/shard_map/proj_add/pallas_call | solution.py:308
  95.8 30.0 %mlp.3.refs_0_ = bf16[384,1536]{1,0:T(8,128)(2,1)} custom-call(bf16[768,1536]{1,0:T(8,128)(2,1)} %proj_add.2.x_ref, f32[4,1536]{1,0:T(4,128)} %gain_ref.7, bf16[2,1536,12288]{2,1,0:T(8,128)(2,1)} %wu_ref.5, bf16[2,1536,12288]{2,1,0:T(8,128)(2,1)} %wu_ref.5, bf16[2,6144,1536]{2,1,0:T(8,128)(2,1)} %wd_ref.5), custom_call_target="tpu_custom_call" | custom-call | flops 21743271936 | bytes 56623104 | tf_op jit(solution)/shard_map/mlp/pallas_call | solution.py:345
  125.8 30.4 %mlp.4.refs_1_ = bf16[384,1536]{1,0:T(8,128)(2,1)} custom-call(bf16[768,1536]{1,0:T(8,128)(2,1)} %proj_add.2.x_ref, f32[4,1536]{1,0:T(4,128)} %gain_ref.7, bf16[2,1536,12288]{2,1,0:T(8,128)(2,1)} %wu_ref.5, bf16[2,1536,12288]{2,1,0:T(8,128)(2,1)} %wu_ref.5, bf16[2,6144,1536]{2,1,0:T(8,128)(2,1)} %wd_ref.5), custom_call_target="tpu_custom_call" | custom-call | flops 21743271936 | bytes 56623104 | tf_op jit(solution)/shard_map/mlp/pallas_call | solution.py:345
  156.2 19.0 %qkv.1 = (bf16[12,768,128]{2,1,0:T(8,128)(2,1)}, bf16[24,768,128]{2,1,0:T(8,128)(2,1)}) custom-call(bf16[384,1536]{1,0:T(8,128)(2,1)} %mlp.3.refs_0_, bf16[384,1536]{1,0:T(8,128)(2,1)} %mlp.4.refs_1_, f32[4,1536]{1,0:T(4,128)} %gain_ref.7, f32[768,128]{1,0:T(8,128)} %get-tuple-element.49.refs_3_, f32[768,128]{1,0:T(8,128)} %get-tuple-element.50.refs_4_, ...), custom_call_target="tpu_custom_call" | custom-call | flops 10871635968 | bytes 22155776 | tf_op jit(solution)/shard_map/qkv/pallas_call | solution.py:417
  175.3 0.2 collective-permute-start.11
  175.4 0.0 copy-done.8
  175.4 1.3 collective-permute-start.7
  176.7 1.3 collective-permute-start.8
  178.0 28.1 %collective-permute-done.7.refs_0_ = bf16[384,1536]{1,0:T(8,128)(2,1)S(1)} collective-permute-done((bf16[384,1536]{1,0:T(8,128)(2,1)S(1)}, bf16[384,1536]{1,0:T(8,128)(2,1)S(1)}, u32[]{:S(2)}, u32[]{:S(2)}) %collective-permute-start.7) | collective-permute-done | bytes 1179680 | tf_op jit(solution)/shard_map/ppermute | solution.py:605
  206.1 1.1 copy-done.7
  207.2 9.3 %kv.2.refs_0_.refs_1_ = bf16[24,384,128]{2,1,0:T(8,128)(2,1)} custom-call(bf16[384,1536]{1,0:T(8,128)(2,1)} %copy-done.7, f32[4,1536]{1,0:T(4,128)} %gain_ref.7, f32[768,128]{1,0:T(8,128)} %get-tuple-element.54.refs_2_, f32[768,128]{1,0:T(8,128)} %get-tuple-element.55.refs_3_, bf16[36,1536,128]{2,1,0:T(8,128)(2,1)} %bitcast.9), custom_call_target="tpu_custom_call" | custom-call | flops 3623878656 | bytes 17437184 | tf_op jit(solution)/shard_map/kv/pallas_call | solution.py:417
  216.6 14.3 %collective-permute-done.8.refs_0_ = bf16[384,1536]{1,0:T(8,128)(2,1)S(1)} collective-permute-done((bf16[384,1536]{1,0:T(8,128)(2,1)}, bf16[384,1536]{1,0:T(8,128)(2,1)S(1)}, u32[]{:S(2)}, u32[]{:S(2)}) %collective-permute-start.8) | collective-permute-done | bytes 1179680 | tf_op jit(solution)/shard_map/ppermute | solution.py:608
  230.8 1.0 copy-done.6
  231.8 9.2 %kv.3.refs_2_.refs_3_ = bf16[24,384,128]{2,1,0:T(8,128)(2,1)} custom-call(bf16[384,1536]{1,0:T(8,128)(2,1)} %copy-done.6, f32[4,1536]{1,0:T(4,128)} %gain_ref.7, f32[768,128]{1,0:T(8,128)} %get-tuple-element.54.refs_2_, f32[768,128]{1,0:T(8,128)} %get-tuple-element.55.refs_3_, bf16[36,1536,128]{2,1,0:T(8,128)(2,1)} %bitcast.10), custom_call_target="tpu_custom_call" | custom-call | flops 3623878656 | bytes 17437184 | tf_op jit(solution)/shard_map/kv/pallas_call | solution.py:417
  241.0 0.0 collective-permute-start.10
  241.0 0.0 copy-done
  241.0 0.5 collective-permute-start.9
  241.5 4.2 %collective-permute-done.10.refs_6_.refs_7_ = bf16[24,384,128]{2,1,0:T(8,128)(2,1)S(1)} collective-permute-done((bf16[24,384,128]{2,1,0:T(8,128)(2,1)}, bf16[24,384,128]{2,1,0:T(8,128)(2,1)S(1)}, u32[]{:S(2)}, u32[]{:S(2)}) %collective-permute-start.10) | collective-permute-done | bytes 2359328 | tf_op jit(solution)/shard_map/ppermute | solution.py:617
  245.8 3.4 collective-permute-done.9.refs_4_.refs_5_
  249.1 0.0 copy-done.1
  249.1 1.4 copy-done.2
  250.6 0.0 collective-permute-done.11.refs_8_.refs_9_
  250.6 41.3 %attention.1.a_ref = bf16[768,1536]{1,0:T(8,128)(2,1)} custom-call(s32[16]{0:T(128)} %pad_add_fusion.sc_ref, bf16[12,768,128]{2,1,0:T(8,128)(2,1)} %get-tuple-element.52.q_ref, s32[768,128]{1,0:T(8,128)} %broadcast_in_dim.37.seg_ref, bf16[24,384,128]{2,1,0:T(8,128)(2,1)} %kv.2.refs_0_.refs_1_, bf16[24,384,128]{2,1,0:T(8,128)(2,1)} %kv.2.refs_0_.refs_1_, ...), custom_call_target="tpu_custom_call" | custom-call | flops 7247757312 | bytes 20000000 | tf_op jit(solution)/shard_map/attention/pallas_call | solution.py:534
  291.9 8.1 %proj_add.3.x_ref = bf16[768,1536]{1,0:T(8,128)(2,1)} custom-call(bf16[768,1536]{1,0:T(8,128)(2,1)} %attention.1.a_ref, bf16[1536,1536]{1,0:T(8,128)(2,1)} %bitcast.15, bf16[384,1536]{1,0:T(8,128)(2,1)} %mlp.3.refs_0_, bf16[384,1536]{1,0:T(8,128)(2,1)} %mlp.4.refs_1_), custom_call_target="tpu_custom_call" | custom-call | flops 3623878656 | bytes 11796480 | tf_op jit(solution)/shard_map/proj_add/pallas_call | solution.py:308
  300.0 53.6 %mlp.5 = bf16[768,1536]{1,0:T(8,128)(2,1)} custom-call(bf16[768,1536]{1,0:T(8,128)(2,1)} %proj_add.3.x_ref, f32[4,1536]{1,0:T(4,128)} %gain_ref.7, bf16[2,1536,12288]{2,1,0:T(8,128)(2,1)} %wu_ref.5, bf16[2,1536,12288]{2,1,0:T(8,128)(2,1)} %wu_ref.5, bf16[2,6144,1536]{2,1,0:T(8,128)(2,1)} %wd_ref.5), custom_call_target="tpu_custom_call" | custom-call | flops 43486543872 | bytes 56623104 | tf_op jit(solution)/shard_map/mlp/pallas_call | solution.py:345
  (12 shorter events, 0.0 us)
Async XLA Ops:
  0.8 20.9 %collective-permute-start.2 = (s32[4]{0:T(128)S(1)}, s32[4]{0:T(128)S(1)}, u32[]{:S(2)}, u32[]{:S(2)}) collective-permute-start(s32[4]{0:T(128)S(1)} %convert_reduce_fusion), channel_id=1, source_target_pairs={{0,3},{4,7}} | collective-permute-start | bytes 56 | tf_op jit(solution)/shard_map/ppermute | solution.py:567
  1.5 20.2 %collective-permute-start.1 = (s32[4]{0:T(128)S(1)}, s32[4]{0:T(128)S(1)}, u32[]{:S(2)}, u32[]{:S(2)}) collective-permute-start(s32[4]{0:T(128)S(1)} %convert_reduce_fusion), channel_id=1, source_target_pairs={{0,2},{1,3},{4,6},{5,7}} | collective-permute-start | bytes 56 | tf_op jit(solution)/shard_map/ppermute | solution.py:567
  2.8 18.9 %collective-permute-start = (s32[4]{0:T(128)S(1)}, s32[4]{0:T(128)S(1)}, u32[]{:S(2)}, u32[]{:S(2)}) collective-permute-start(s32[4]{0:T(128)S(1)} %convert_reduce_fusion), channel_id=1, source_target_pairs={{0,1},{1,2},{2,3},{4,5},{5,6},{6,7}} | collective-permute-start | bytes 56 | tf_op jit(solution)/shard_map/ppermute | solution.py:567
  7.2 15.2 %copy-start.9 = (s32[768]{0:T(1024)S(1)}, s32[768]{0:T(1024)}, u32[]{:S(2)}) copy-start(s32[768]{0:T(1024)} %param.12) | copy-start | bytes 9220
  32.2 5.6 %collective-permute-start.3 = (f32[128,3072]{1,0:T(8,128)}, f32[128,3072]{1,0:T(8,128)S(1)}, u32[]{:S(2)}, u32[]{:S(2)}) collective-permute-start(f32[128,3072]{1,0:T(8,128)} %get-tuple-element.41), channel_id=1, source_target_pairs={{0,1},{1,0},{2,3},{3,2},{4,5},{5,4},{6,7},{7,6}} | collective-permute-start | bytes 4718600 | tf_op jit(solution)/shard_map/ppermute | solution.py:586
  36.1 1.7 copy-start.3
  36.1 1.7 collective-permute-start.4
  38.8 1.8 copy-start.4
  38.8 1.8 copy-start.5
  38.9 22.0 %collective-permute-start.5 = (f32[64,3072]{1,0:T(8,128)S(1)}, f32[64,3072]{1,0:T(8,128)S(1)}, u32[]{:S(2)}, u32[]{:S(2)}) collective-permute-start(f32[64,3072]{1,0:T(8,128)S(1)} %slice_select_fusion), channel_id=1, source_target_pairs={{0,2},{1,3},{4,6},{5,7}} | collective-permute-start | bytes 2359304 | tf_op jit(solution)/shard_map/ppermute | solution.py:592
  60.9 2.3 collective-permute-start.6
  156.2 19.2 %copy-start.8 = (bf16[384,1536]{1,0:T(8,128)(2,1)S(1)}, bf16[384,1536]{1,0:T(8,128)(2,1)}, u32[]{:S(2)}) copy-start(bf16[384,1536]{1,0:T(8,128)(2,1)} %mlp.3.refs_0_) | copy-start | bytes 3538948
  175.3 75.3 %collective-permute-start.11 = (bf16[24,768,128]{2,1,0:T(8,128)(2,1)}, bf16[24,768,128]{2,1,0:T(8,128)(2,1)}, u32[]{:S(2)}, u32[]{:S(2)}) collective-permute-start(bf16[24,768,128]{2,1,0:T(8,128)(2,1)} %get-tuple-element.58.refs_10_.refs_11_), channel_id=1, source_target_pairs={{0,1},{1,0},{2,3},{3,2},{4,5},{5,4},{6,7},{7,6}} | collective-permute-start | bytes 14155784 | tf_op jit(solution)/shard_map/ppermute | solution.py:611
  175.4 30.7 %collective-permute-start.7 = (bf16[384,1536]{1,0:T(8,128)(2,1)S(1)}, bf16[384,1536]{1,0:T(8,128)(2,1)S(1)}, u32[]{:S(2)}, u32[]{:S(2)}) collective-permute-start(bf16[384,1536]{1,0:T(8,128)(2,1)S(1)} %copy-done.8), channel_id=1, source_target_pairs={{0,2},{1,3},{4,6},{5,7}} | collective-permute-start | bytes 3538952 | tf_op jit(solution)/shard_map/ppermute | solution.py:605
  176.7 54.1 %collective-permute-start.8 = (bf16[384,1536]{1,0:T(8,128)(2,1)}, bf16[384,1536]{1,0:T(8,128)(2,1)S(1)}, u32[]{:S(2)}, u32[]{:S(2)}) collective-permute-start(bf16[384,1536]{1,0:T(8,128)(2,1)} %mlp.4.refs_1_), channel_id=1, source_target_pairs={{0,2},{1,3},{4,6},{5,7}} | collective-permute-start | bytes 3538952 | tf_op jit(solution)/shard_map/ppermute | solution.py:608
  206.1 1.1 copy-start.7
  216.6 24.5 %copy-start = (bf16[24,384,128]{2,1,0:T(8,128)(2,1)S(1)}, bf16[24,384,128]{2,1,0:T(8,128)(2,1)}, u32[]{:S(2)}) copy-start(bf16[24,384,128]{2,1,0:T(8,128)(2,1)} %kv.2.refs_0_.refs_1_) | copy-start | bytes 7077892
  230.8 1.0 copy-start.6
  241.0 4.7 %collective-permute-start.10 = (bf16[24,384,128]{2,1,0:T(8,128)(2,1)}, bf16[24,384,128]{2,1,0:T(8,128)(2,1)S(1)}, u32[]{:S(2)}, u32[]{:S(2)}) collective-permute-start(bf16[24,384,128]{2,1,0:T(8,128)(2,1)} %kv.3.refs_2_.refs_3_), channel_id=1, source_target_pairs={{0,1},{1,0},{2,3},{3,2},{4,5},{5,4},{6,7},{7,6}} | collective-permute-start | bytes 7077896 | tf_op jit(solution)/shard_map/ppermute | solution.py:617
  241.0 8.1 %collective-permute-start.9 = (bf16[24,384,128]{2,1,0:T(8,128)(2,1)S(1)}, bf16[24,384,128]{2,1,0:T(8,128)(2,1)S(1)}, u32[]{:S(2)}, u32[]{:S(2)}) collective-permute-start(bf16[24,384,128]{2,1,0:T(8,128)(2,1)S(1)} %copy-done), channel_id=1, source_target_pairs={{0,1},{1,0},{2,3},{3,2},{4,5},{5,4},{6,7},{7,6}} | collective-permute-start | bytes 7077896 | tf_op jit(solution)/shard_map/ppermute | solution.py:614
  245.8 3.4 copy-start.1
  249.1 1.4 copy-start.2

commit v2 on v1

--- a/solution.py
+++ b/solution.py
@@ -14,7 +14,6 @@
 ROPE_BASE = 10000.0
 F32 = jnp.float32
 BF16 = jnp.bfloat16
-VMEM_LIMIT = 60 * 1024 * 1024
 NT = (((1,), (1,)), ((), ()))
 
 
@@ -22,8 +21,8 @@
     return lax.dot_general(a, b, dims, preferred_element_type=F32)
 
 
-def params(sem):
-    return pltpu.CompilerParams(dimension_semantics=sem, vmem_limit_bytes=VMEM_LIMIT)
+def params(sem, mib):
+    return pltpu.CompilerParams(dimension_semantics=sem, vmem_limit_bytes=mib * 1024 * 1024)
 
 
 def cost(flops, bytes_accessed, trans=0):
@@ -102,7 +101,7 @@
             full_spec((tokens, 128)),
         ),
         out_shape=out_shape,
-        compiler_params=params(("arbitrary",)),
+        compiler_params=params(("arbitrary",), 40),
         cost_estimate=cost(2 * tokens * dim * (inner + tile), 16e6),
         name="in_proj",
     )(x_rows, gains, w_in_t, head_pad)
@@ -123,7 +122,7 @@
         in_specs=[full_spec((tokens, dim)), pl.BlockSpec((tile, dim), lambda i: (i + first, 0))],
         out_specs=pl.BlockSpec((tokens, tile), lambda i: (0, i)),
         out_shape=jax.ShapeDtypeStruct((tokens, inner), F32),
-        compiler_params=params(("arbitrary",)),
+        compiler_params=params(("arbitrary",), 40),
         cost_estimate=cost(2 * tokens * dim * inner, 21e6),
         name="z_proj",
     )(hid, w_in_t)
@@ -197,7 +196,7 @@
         out_specs=(full_spec((128, inner)), full_spec((1, inner))),
         out_shape=(jax.ShapeDtypeStruct((128, inner), F32), jax.ShapeDtypeStruct((1, inner), F32)),
         scratch_shapes=[pltpu.VMEM((256, inner), BF16), pltpu.VMEM((STEP + 16, inner), F32), pltpu.VMEM((STEP, inner), BF16)],
-        compiler_params=params(("arbitrary",)),
+        compiler_params=params(("arbitrary",), 40),
         cost_estimate=cost(2 * tokens * 256 * inner, 8e6),
         name="ssd_state",
     )(scalars, xs, bc, dt, cum, seg_wide)
@@ -288,7 +287,7 @@
             pltpu.VMEM((2 * STEP, inner), F32), pltpu.VMEM((STEP, inner), BF16), pltpu.VMEM((2, 128, STEP), F32),
             pltpu.VMEM((2, 2, inner // 128, STEP), F32),
         ],
-        compiler_params=params(("arbitrary",)),
+        compiler_params=params(("arbitrary",), 40),
         cost_estimate=cost(12e9, 20e6),
         name="ssd_full",
     )(scalars, xs, bc, dt, cum, seg_wide, z, h_in, skip, gain)
@@ -311,7 +310,7 @@
         in_specs=[full_spec((tokens, depth)), col(depth)] + [col(r.shape[0]) for r in res],
         out_specs=col(tokens),
         out_shape=jax.ShapeDtypeStruct((tokens, dim), BF16),
-        compiler_params=params(("arbitrary",)),
+        compiler_params=params(("arbitrary",), 40),
         cost_estimate=cost(2 * tokens * depth * dim, 2 * (tokens * depth + depth * dim + 2 * tokens * dim)),
         name="proj_add",
     )(a, w, *res)
@@ -340,7 +339,7 @@
     tokens, dim = x_rows.shape
     tokens //= parts
     ff = mlp_down.shape[1]
-    tile = 1024
+    tile = 512 * parts
     n_ff = ff // tile
     return pl.pallas_call(
         functools.partial(mlp_kernel, layer),
@@ -355,7 +354,7 @@
         out_specs=full_spec((tokens, dim)),
         out_shape=jax.ShapeDtypeStruct((tokens, dim), BF16),
         scratch_shapes=[pltpu.VMEM((tokens, dim), BF16), pltpu.VMEM((tokens, dim), F32)],
-        compiler_params=params(("arbitrary",)),
+        compiler_params=params(("arbitrary",), 40),
         cost_estimate=cost(6 * tokens * dim * ff, 6 * dim * ff),
         name="mlp",
     )(x_rows, gains, mlp_up, mlp_up, mlp_down)
@@ -423,7 +422,7 @@
         out_specs=tuple(out_specs),
         out_shape=tuple(out_shape),
         scratch_shapes=[pltpu.VMEM((tokens, dim), BF16)],
-        compiler_params=params(("arbitrary",)),
+        compiler_params=params(("arbitrary",), 40),
         cost_estimate=cost(2 * tokens * dim * steps * per * head_dim, 2 * dim * steps * per * head_dim + 8e6),
         name="qkv" if with_q else "kv",
     )(*parts, gains, cos, sin, w_heads)
@@ -542,7 +541,7 @@
             + [pltpu.VMEM((per, BLOCK, head_dim), F32), pltpu.VMEM((BLOCK, BLOCK), F32)],
         ),
         out_shape=jax.ShapeDtypeStruct((tokens, n_heads * head_dim), BF16),
-        compiler_params=params(("arbitrary", "arbitrary")),
+        compiler_params=params(("arbitrary", "arbitrary"), 40),
         cost_estimate=cost(4 * n_heads * tokens * 2 * tokens * head_dim, 20e6, n_heads * tokens * tokens),
         name="attention",
     )(scalars, *args)

time: 360 us -> 333 us (0.925); the launches traced: 354 us -> 332 us
  Pallas kernels: 268 us -> 238 us
  local copies, waits for them, and re-layouts: 7.93 us -> 14.6 us
    unnamed x20 -> x48, local copies, waits for them, and re-layouts: 3.53 us -> 12.2 us
    pallas_call x3, Pallas kernels: 114 us -> 108 us  [mlp(): pl.pallas_call(functools.partial(mlp_kernel, layer), grid=(n_ff,), in_spe...]
    pallas_call x2, Pallas kernels: 20.4 us -> 14.8 us  [proj_add(): pl.pallas_call(proj_add_kernel, grid=(dim // tile,), in_specs=[full_spec(...]
    pallas_call x3, Pallas kernels: 37.5 us -> 32.3 us  [qkv_proj(): pl.pallas_call(functools.partial(qkv_kernel, n_q, n_rot, len(parts)), gri...]
    pallas_call x1, Pallas kernels: 41.3 us -> 37.2 us  [attention(): pl.pallas_call(attn_kernel, grid_spec=pltpu.PrefetchScalarGridSpec(num_sc...]
  transfers between devices with their start and end apart: 12 -> 12, of which waited for: 6 -> 7; matrix products, arithmetic and copies ran while one was open for 3% -> 2% of each run, Pallas kernels for 13% -> 11%
where the time goes in v2:
time: 333 us; the launch traced here: 332 us
  Pallas kernels  238 us (71%)
  waiting for transfers between devices  59.3 us (18%)
  local copies, waits for them, and re-layouts  14.6 us (4%)
  other arithmetic  9.82 us (3%)
  starting transfers between devices  9.69 us (3%)
    pallas_call x3, Pallas kernels, mlp(): pl.pallas_call(functools.partial(mlp_kernel, layer), grid=(n_ff,), in_spe...  108 us
    pallas_call x1, Pallas kernels, attention(): pl.pallas_call(attn_kernel, grid_spec=pltpu.PrefetchScalarGridSpec(num_sc...  37.2 us
    pallas_call x3, Pallas kernels, qkv_proj(): pl.pallas_call(functools.partial(qkv_kernel, n_q, n_rot, len(parts)), gri...  32.3 us
    ppermute x1, waiting for transfers between devices, layers(): far_a = lax.ppermute(x_a, 'sp', cross_perm)  28.1 us
    pallas_call x1, Pallas kernels, ssd_full(): pl.pallas_call(ssd_full_kernel, grid=(tokens // STEP,), in_specs=[SMEM_SP...  17.2 us
    ppermute x1, waiting for transfers between devices, layers(): far_b = lax.ppermute(x_b, 'sp', cross_perm)  16.9 us
    pallas_call x2, Pallas kernels, proj_add(): pl.pallas_call(proj_add_kernel, grid=(dim // tile,), in_specs=[full_spec(...  14.8 us
    unnamed x48, local copies, waits for them, and re-layouts  12.2 us
  transfers between devices with their start and end apart: 12, of which 7 were waited for; matrix products, arithmetic and copies ran while one was open for 2% of the time, Pallas kernels for 11%

profile of v2, /device:TPU:2, one launch (start us, length us, event | category | flops | bytes accessed | tf_op | source)
XLA Modules:
  0.0 332.0 jit_solution(5302184509582679130)
XLA Ops:
  0.0 0.8 convert_reduce_fusion
  0.8 0.7 collective-permute-start.2
  1.5 1.3 collective-permute-start.1
  2.8 2.4 collective-permute-start
  5.2 0.8 slice.14
  5.9 0.7 pad.8.head_ref
  6.6 0.7 copy-done.8
  7.4 1.7 copy-done.17
  9.0 11.7 %in_proj.1 = (bf16[768,1536]{1,0:T(8,128)(2,1)S(1)}, bf16[768,3072]{1,0:T(8,128)(2,1)S(1)}, bf16[768,256]{1,0:T(8,128)(2,1)S(1)}, f32[768,128]{1,0:T(8,128)S(1)}, f32[768,128]{1,0:T(8,128)S(1)}) custom-call(bf16[768,1536]{1,0:T(8,128)(2,1)S(1)} %copy-done.17, f32[4,1536]{1,0:T(4,128)S(1)} %copy-done.8, bf16[6448,1536]{1,0:T(8,128)(2,1)} %bitcast.14, ...), custom_call_target="tpu_custom_call" | custom-call | flops 9663676416 | bytes 16000000 | tf_op jit(solution)/shard_map/in_proj/pallas_call | solution.py:87
  20.7 0.0 copy-start.4
  20.7 1.4 copy-done.4
  22.1 0.0 collective-permute-done.2
  22.1 0.0 collective-permute-done.1
  22.1 0.0 collective-permute-done
  22.1 0.1 pad_add_fusion.sc_ref
  22.2 0.2 broadcast_in_dim.37.seg_ref
  22.4 6.8 %ssd_state.1 = (f32[128,3072]{1,0:T(8,128)S(1)}, f32[1,3072]{1,0:T(1,128)S(1)}) custom-call(s32[16]{0:T(128)S(1)} %pad_add_fusion.sc_ref, bf16[768,3072]{1,0:T(8,128)(2,1)S(1)} %get-tuple-element.36.x_ref, bf16[768,256]{1,0:T(8,128)(2,1)S(1)} %get-tuple-element.37.bc_ref, f32[768,128]{1,0:T(8,128)S(1)} %get-tuple-element.38.dt_ref, ...), custom_call_target="tpu_custom_call" | custom-call | flops 1207959552 | bytes 8000000 | tf_op jit(solution)/shard_map/ssd_state/pallas_call | solution.py:192
  29.2 0.0 collective-permute-start.3
  29.3 3.9 %fusion.1 = (f32[768,64]{1,0:T(8,128)S(1)}, f32[768,64]{1,0:T(8,128)S(1)}, f32[768,64]{1,0:T(8,128)S(1)}, f32[768,64]{1,0:T(8,128)}, f32[768,64]{1,0:T(8,128)}, /*index=5*/f32[768,64]{1,0:T(8,128)}) fusion(f32[64]{0:T(128)S(1)} %multiply_power_fusion, f32[768]{0:T(1024)S(1)} %broadcast_add_fusion, f32[768]{0:T(1024)S(1)} %add_convert_fusion), kind=kLoop, calls=%fused_computation.13 | loop fusion | flops 196608 | bytes 1186048 | tf_op jit(solution)/shard_map/neg | solution.py:368
  33.2 0.5 collective-permute-start.4
  33.7 0.3 pad_maximum_fusion.2
  34.0 0.5 collective-permute-done.4
  34.5 0.0 collective-permute-done.3
  34.6 1.8 add_select_fusion.1
  36.4 0.0 copy-start.5
  36.4 0.1 slice_select_fusion
  36.5 1.6 collective-permute-start.5
  38.1 1.2 pad_maximum_fusion
  39.3 10.5 %z_proj.1.z_ref = f32[768,3072]{1,0:T(8,128)S(1)} custom-call(bf16[768,1536]{1,0:T(8,128)(2,1)S(1)} %copy-done.5, bf16[6448,1536]{1,0:T(8,128)(2,1)} %bitcast.15), custom_call_target="tpu_custom_call" | custom-call | flops 7247757312 | bytes 21000000 | tf_op jit(solution)/shard_map/z_proj/pallas_call | solution.py:119
  49.8 3.6 %copy-done.1 = f32[768,3072]{1,0:T(8,128)} copy-done((f32[768,3072]{1,0:T(8,128)}, f32[768,3072]{1,0:T(8,128)S(1)}, u32[]{:S(2)}) %copy-start.1) | copy-done | bytes 9437208
  53.4 4.9 %collective-permute-done.5 = f32[64,3072]{1,0:T(8,128)S(1)} collective-permute-done((f32[64,3072]{1,0:T(8,128)S(1)}, f32[64,3072]{1,0:T(8,128)S(1)}, u32[]{:S(2)}, u32[]{:S(2)}) %collective-permute-start.5) | collective-permute-done | bytes 786464 | tf_op jit(solution)/shard_map/ppermute | solution.py:591
  58.3 0.0 collective-permute-start.6
  58.3 0.7 slice_bitcast_fusion
  59.0 0.1 broadcast_in_dim.38
  59.1 0.1 broadcast_in_dim.39.skip_ref
  59.2 0.0 copy-start.19
  59.2 1.4 collective-permute-done.6
  60.6 1.6 add_select_fusion.hin_ref
  62.3 2.3 copy-done.3
  64.6 17.2 %ssd_full.1.a_ref = bf16[768,3072]{1,0:T(8,128)(2,1)S(1)} custom-call(s32[16]{0:T(128)S(1)} %pad_add_fusion.sc_ref, bf16[768,3072]{1,0:T(8,128)(2,1)S(1)} %copy-done.3, bf16[768,256]{1,0:T(8,128)(2,1)S(1)} %get-tuple-element.37.bc_ref, f32[768,128]{1,0:T(8,128)S(1)} %copy-done.11, f32[768,128]{1,0:T(8,128)S(1)} %copy-done.13, ...), custom_call_target="tpu_custom_call" | custom-call | flops 12000000000 | bytes 20000000 | tf_op jit(solution)/shard_map/ssd_full/pallas_call | solution.py:276
  81.9 0.0 copy-start.9
  81.9 10.0 %proj_add.2.x_ref = bf16[768,1536]{1,0:T(8,128)(2,1)S(1)} custom-call(bf16[768,3072]{1,0:T(8,128)(2,1)S(1)} %ssd_full.1.a_ref, bf16[3072,1536]{1,0:T(8,128)(2,1)} %w_ref.1, bf16[768,1536]{1,0:T(8,128)(2,1)S(1)} %copy-done.18), custom_call_target="tpu_custom_call" | custom-call | flops 7247757312 | bytes 18874368 | tf_op jit(solution)/shard_map/proj_add/pallas_call | solution.py:307
  91.9 27.7 %mlp.3.refs_0_ = bf16[384,1536]{1,0:T(8,128)(2,1)S(1)} custom-call(bf16[768,1536]{1,0:T(8,128)(2,1)S(1)} %proj_add.2.x_ref, f32[4,1536]{1,0:T(4,128)S(1)} %copy-done.9, bf16[2,1536,12288]{2,1,0:T(8,128)(2,1)} %wu_ref.5, bf16[2,1536,12288]{2,1,0:T(8,128)(2,1)} %wu_ref.5, bf16[2,6144,1536]{2,1,0:T(8,128)(2,1)} %wd_ref.5), custom_call_target="tpu_custom_call" | custom-call | flops 21743271936 | bytes 56623104 | tf_op jit(solution)/shard_map/mlp/pallas_call | solution.py:344
  119.6 27.9 %mlp.4.refs_1_ = bf16[384,1536]{1,0:T(8,128)(2,1)S(1)} custom-call(bf16[768,1536]{1,0:T(8,128)(2,1)S(1)} %proj_add.2.x_ref, f32[4,1536]{1,0:T(4,128)S(1)} %copy-done.9, bf16[2,1536,12288]{2,1,0:T(8,128)(2,1)} %wu_ref.5, bf16[2,1536,12288]{2,1,0:T(8,128)(2,1)} %wu_ref.5, bf16[2,6144,1536]{2,1,0:T(8,128)(2,1)} %wd_ref.5), custom_call_target="tpu_custom_call" | custom-call | flops 21743271936 | bytes 56623104 | tf_op jit(solution)/shard_map/mlp/pallas_call | solution.py:344
  147.5 0.0 copy-start.6
  147.6 16.9 %qkv.1 = (bf16[12,768,128]{2,1,0:T(8,128)(2,1)S(1)}, bf16[24,768,128]{2,1,0:T(8,128)(2,1)S(1)}) custom-call(bf16[384,1536]{1,0:T(8,128)(2,1)S(1)} %mlp.3.refs_0_, bf16[384,1536]{1,0:T(8,128)(2,1)S(1)} %mlp.4.refs_1_, f32[4,1536]{1,0:T(4,128)S(1)} %copy-done.9, f32[768,128]{1,0:T(8,128)S(1)} %copy-done.14, f32[768,128]{1,0:T(8,128)S(1)} %copy-done.15, ...), custom_call_target="tpu_custom_call" | custom-call | flops 10871635968 | bytes 22155776 | tf_op jit(solution)/shard_map/qkv/pallas_call | solution.py:416
  164.5 0.2 collective-permute-start.11
  164.6 1.3 collective-permute-start.7
  165.9 1.3 collective-permute-start.8
  167.2 28.1 %collective-permute-done.7.refs_0_ = bf16[384,1536]{1,0:T(8,128)(2,1)S(1)} collective-permute-done((bf16[384,1536]{1,0:T(8,128)(2,1)S(1)}, bf16[384,1536]{1,0:T(8,128)(2,1)S(1)}, u32[]{:S(2)}, u32[]{:S(2)}) %collective-permute-start.7) | collective-permute-done | bytes 1179680 | tf_op jit(solution)/shard_map/ppermute | solution.py:604
  195.3 7.7 %kv.2.refs_0_.refs_1_ = bf16[24,384,128]{2,1,0:T(8,128)(2,1)S(1)} custom-call(bf16[384,1536]{1,0:T(8,128)(2,1)S(1)} %collective-permute-done.7.refs_0_, f32[4,1536]{1,0:T(4,128)S(1)} %copy-done.9, f32[768,128]{1,0:T(8,128)S(1)} %get-tuple-element.54.refs_2_, f32[768,128]{1,0:T(8,128)S(1)} %get-tuple-element.55.refs_3_, bf16[36,1536,128]{2,1,0:T(8,128)(2,1)} %bitcast.12), custom_call_target="tpu_custom_call" | custom-call | flops 3623878656 | bytes 17437184 | tf_op jit(solution)/shard_map/kv/pallas_call | solution.py:416
  203.1 16.9 %collective-permute-done.8.refs_0_ = bf16[384,1536]{1,0:T(8,128)(2,1)S(1)} collective-permute-done((bf16[384,1536]{1,0:T(8,128)(2,1)S(1)}, bf16[384,1536]{1,0:T(8,128)(2,1)S(1)}, u32[]{:S(2)}, u32[]{:S(2)}) %collective-permute-start.8) | collective-permute-done | bytes 1179680 | tf_op jit(solution)/shard_map/ppermute | solution.py:607
  220.0 7.7 %kv.3.refs_2_.refs_3_ = bf16[24,384,128]{2,1,0:T(8,128)(2,1)S(1)} custom-call(bf16[384,1536]{1,0:T(8,128)(2,1)S(1)} %collective-permute-done.8.refs_0_, f32[4,1536]{1,0:T(4,128)S(1)} %copy-done.9, f32[768,128]{1,0:T(8,128)S(1)} %get-tuple-element.54.refs_2_, f32[768,128]{1,0:T(8,128)S(1)} %get-tuple-element.55.refs_3_, bf16[36,1536,128]{2,1,0:T(8,128)(2,1)} %bitcast.13), custom_call_target="tpu_custom_call" | custom-call | flops 3623878656 | bytes 17437184 | tf_op jit(solution)/shard_map/kv/pallas_call | solution.py:416
  227.8 0.0 copy-start.7
  227.8 0.0 collective-permute-start.10
  227.8 0.5 collective-permute-start.9
  228.3 4.0 %collective-permute-done.10.refs_6_.refs_7_ = bf16[24,384,128]{2,1,0:T(8,128)(2,1)S(1)} collective-permute-done((bf16[24,384,128]{2,1,0:T(8,128)(2,1)S(1)}, bf16[24,384,128]{2,1,0:T(8,128)(2,1)S(1)}, u32[]{:S(2)}, u32[]{:S(2)}) %collective-permute-start.10) | collective-permute-done | bytes 2359328 | tf_op jit(solution)/shard_map/ppermute | solution.py:616
  232.3 3.4 %collective-permute-done.9.refs_4_.refs_5_ = bf16[24,384,128]{2,1,0:T(8,128)(2,1)S(1)} collective-permute-done((bf16[24,384,128]{2,1,0:T(8,128)(2,1)S(1)}, bf16[24,384,128]{2,1,0:T(8,128)(2,1)S(1)}, u32[]{:S(2)}, u32[]{:S(2)}) %collective-permute-start.9) | collective-permute-done | bytes 2359328 | tf_op jit(solution)/shard_map/ppermute | solution.py:613
  235.7 0.0 collective-permute-done.11.refs_8_.refs_9_
  235.7 37.2 %attention.1.a_ref = bf16[768,1536]{1,0:T(8,128)(2,1)S(1)} custom-call(s32[16]{0:T(128)S(1)} %pad_add_fusion.sc_ref, bf16[12,768,128]{2,1,0:T(8,128)(2,1)S(1)} %get-tuple-element.52.q_ref, s32[768,128]{1,0:T(8,128)S(1)} %broadcast_in_dim.37.seg_ref, bf16[24,384,128]{2,1,0:T(8,128)(2,1)S(1)} %kv.2.refs_0_.refs_1_, ...), custom_call_target="tpu_custom_call" | custom-call | flops 7247757312 | bytes 20000000 | tf_op jit(solution)/shard_map/attention/pallas_call | solution.py:533
  272.9 0.0 copy-start.16
  272.9 2.3 copy-done.16
  275.3 4.8 %proj_add.3.x_ref = bf16[768,1536]{1,0:T(8,128)(2,1)S(1)} custom-call(bf16[768,1536]{1,0:T(8,128)(2,1)S(1)} %attention.1.a_ref, bf16[1536,1536]{1,0:T(8,128)(2,1)S(1)} %bitcast.9, bf16[384,1536]{1,0:T(8,128)(2,1)S(1)} %mlp.3.refs_0_, bf16[384,1536]{1,0:T(8,128)(2,1)S(1)} %copy-done.7), custom_call_target="tpu_custom_call" | custom-call | flops 3623878656 | bytes 11796480 | tf_op jit(solution)/shard_map/proj_add/pallas_call | solution.py:307
  280.1 51.9 %mlp.5 = bf16[768,1536]{1,0:T(8,128)(2,1)} custom-call(bf16[768,1536]{1,0:T(8,128)(2,1)S(1)} %proj_add.3.x_ref, f32[4,1536]{1,0:T(4,128)S(1)} %copy-done.9, bf16[2,1536,12288]{2,1,0:T(8,128)(2,1)} %wu_ref.5, bf16[2,1536,12288]{2,1,0:T(8,128)(2,1)} %wu_ref.5, bf16[2,6144,1536]{2,1,0:T(8,128)(2,1)} %wd_ref.5), custom_call_target="tpu_custom_call" | custom-call | flops 43486543872 | bytes 56623104 | tf_op jit(solution)/shard_map/mlp/pallas_call | solution.py:344
  (40 shorter events, 0.1 us)
Async XLA Ops:
  0.8 21.3 %collective-permute-start.2 = (s32[4]{0:T(128)S(1)}, s32[4]{0:T(128)S(1)}, u32[]{:S(2)}, u32[]{:S(2)}) collective-permute-start(s32[4]{0:T(128)S(1)} %convert_reduce_fusion), channel_id=1, source_target_pairs={{0,3},{4,7}} | collective-permute-start | bytes 56 | tf_op jit(solution)/shard_map/ppermute | solution.py:566
  1.5 20.6 %collective-permute-start.1 = (s32[4]{0:T(128)S(1)}, s32[4]{0:T(128)S(1)}, u32[]{:S(2)}, u32[]{:S(2)}) collective-permute-start(s32[4]{0:T(128)S(1)} %convert_reduce_fusion), channel_id=1, source_target_pairs={{0,2},{1,3},{4,6},{5,7}} | collective-permute-start | bytes 56 | tf_op jit(solution)/shard_map/ppermute | solution.py:566
  2.8 19.4 %collective-permute-start = (s32[4]{0:T(128)S(1)}, s32[4]{0:T(128)S(1)}, u32[]{:S(2)}, u32[]{:S(2)}) collective-permute-start(s32[4]{0:T(128)S(1)} %convert_reduce_fusion), channel_id=1, source_target_pairs={{0,1},{1,2},{2,3},{4,5},{5,6},{6,7}} | collective-permute-start | bytes 56 | tf_op jit(solution)/shard_map/ppermute | solution.py:566
  6.6 0.7 copy-start.8
  7.4 1.7 copy-start.17
  9.0 13.2 %copy-start.23 = (s32[768]{0:T(1024)S(1)}, s32[768]{0:T(1024)}, u32[]{:S(2)}) copy-start(s32[768]{0:T(1024)} %param.12) | copy-start | bytes 9220
  20.7 1.4 copy-start.4
  22.1 7.1 %copy-start.2 = (bf16[768,3072]{1,0:T(8,128)(2,1)}, bf16[768,3072]{1,0:T(8,128)(2,1)S(1)}, u32[]{:S(2)}) copy-start(bf16[768,3072]{1,0:T(8,128)(2,1)S(1)} %get-tuple-element.36.x_ref) | copy-start | bytes 14155780
  22.1 7.1 %copy-start.10 = (f32[768,128]{1,0:T(8,128)}, f32[768,128]{1,0:T(8,128)S(1)}, u32[]{:S(2)}) copy-start(f32[768,128]{1,0:T(8,128)S(1)} %get-tuple-element.38.dt_ref) | copy-start | bytes 1179652
  22.1 7.1 %copy-start.12 = (f32[768,128]{1,0:T(8,128)}, f32[768,128]{1,0:T(8,128)S(1)}, u32[]{:S(2)}) copy-start(f32[768,128]{1,0:T(8,128)S(1)} %get-tuple-element.39.cum_ref) | copy-start | bytes 1179652
  29.2 5.3 %collective-permute-start.3 = (f32[128,3072]{1,0:T(8,128)S(1)}, f32[128,3072]{1,0:T(8,128)}, u32[]{:S(2)}, u32[]{:S(2)}) collective-permute-start(f32[128,3072]{1,0:T(8,128)S(1)} %get-tuple-element.41), channel_id=1, source_target_pairs={{0,1},{1,0},{2,3},{3,2},{4,5},{5,4},{6,7},{7,6}} | collective-permute-start | bytes 4718600 | tf_op jit(solution)/shard_map/ppermute | solution.py:585
  33.2 1.3 collective-permute-start.4
  34.6 3.6 %copy-start.20 = (f32[768,64]{1,0:T(8,128)S(1)}, f32[768,64]{1,0:T(8,128)}, u32[]{:S(2)}) copy-start(f32[768,64]{1,0:T(8,128)} %get-tuple-element.65) | copy-start | bytes 589828
  34.6 3.6 %copy-start.21 = (f32[768,64]{1,0:T(8,128)S(1)}, f32[768,64]{1,0:T(8,128)}, u32[]{:S(2)}) copy-start(f32[768,64]{1,0:T(8,128)} %get-tuple-element.66) | copy-start | bytes 589828
  34.6 3.6 %copy-start.22 = (f32[768,64]{1,0:T(8,128)S(1)}, f32[768,64]{1,0:T(8,128)}, u32[]{:S(2)}) copy-start(f32[768,64]{1,0:T(8,128)} %get-tuple-element.67) | copy-start | bytes 589828
  36.4 2.9 copy-start.5
  36.5 21.8 %collective-permute-start.5 = (f32[64,3072]{1,0:T(8,128)S(1)}, f32[64,3072]{1,0:T(8,128)S(1)}, u32[]{:S(2)}, u32[]{:S(2)}) collective-permute-start(f32[64,3072]{1,0:T(8,128)S(1)} %slice_select_fusion), channel_id=1, source_target_pairs={{0,2},{1,3},{4,6},{5,7}} | collective-permute-start | bytes 2359304 | tf_op jit(solution)/shard_map/ppermute | solution.py:591
  49.8 3.6 %copy-start.1 = (f32[768,3072]{1,0:T(8,128)}, f32[768,3072]{1,0:T(8,128)S(1)}, u32[]{:S(2)}) copy-start(f32[768,3072]{1,0:T(8,128)S(1)} %z_proj.1.z_ref) | copy-start | bytes 28311556
  58.3 2.3 collective-permute-start.6
  59.2 3.1 copy-start.11
  59.2 3.1 copy-start.13
  59.2 3.1 copy-start.19
  62.3 2.3 copy-start.3
  64.6 17.2 %copy-start.18 = (bf16[768,1536]{1,0:T(8,128)(2,1)S(1)}, bf16[768,1536]{1,0:T(8,128)(2,1)}, u32[]{:S(2)}) copy-start(bf16[768,1536]{1,0:T(8,128)(2,1)} %refs_0_.1) | copy-start | bytes 7077892
  81.9 10.0 %copy-start.9 = (f32[4,1536]{1,0:T(4,128)S(1)}, f32[4,1536]{1,0:T(4,128)}, u32[]{:S(2)}) copy-start(f32[4,1536]{1,0:T(4,128)} %gain_ref.7) | copy-start | bytes 73732
  119.6 28.0 %copy-start.14 = (f32[768,128]{1,0:T(8,128)S(1)}, f32[768,128]{1,0:T(8,128)}, u32[]{:S(2)}) copy-start(f32[768,128]{1,0:T(8,128)} %get-tuple-element.49.refs_3_) | copy-start | bytes 1179652
  119.6 28.0 %copy-start.15 = (f32[768,128]{1,0:T(8,128)S(1)}, f32[768,128]{1,0:T(8,128)}, u32[]{:S(2)}) copy-start(f32[768,128]{1,0:T(8,128)} %get-tuple-element.50.refs_4_) | copy-start | bytes 1179652
  147.5 18.4 %copy-start.6 = (bf16[384,1536]{1,0:T(8,128)(2,1)}, bf16[384,1536]{1,0:T(8,128)(2,1)S(1)}, u32[]{:S(2)}) copy-start(bf16[384,1536]{1,0:T(8,128)(2,1)S(1)} %mlp.4.refs_1_) | copy-start | bytes 3538948
  164.4 38.6 %copy-start = (bf16[24,768,128]{2,1,0:T(8,128)(2,1)}, bf16[24,768,128]{2,1,0:T(8,128)(2,1)S(1)}, u32[]{:S(2)}) copy-start(bf16[24,768,128]{2,1,0:T(8,128)(2,1)S(1)} %get-tuple-element.58.refs_10_.refs_11_) | copy-start | bytes 14155780
  164.5 71.2 %collective-permute-start.11 = (bf16[24,768,128]{2,1,0:T(8,128)(2,1)S(1)}, bf16[24,768,128]{2,1,0:T(8,128)(2,1)}, u32[]{:S(2)}, u32[]{:S(2)}) collective-permute-start(bf16[24,768,128]{2,1,0:T(8,128)(2,1)S(1)} %get-tuple-element.58.refs_10_.refs_11_), channel_id=1, source_target_pairs={{0,1},{1,0},{2,3},{3,2},{4,5},{5,4},{6,7},{7,6}} | collective-permute-start | bytes 14155784 | tf_op jit(solution)/shard_map/ppermute | solution.py:610
  164.6 30.7 %collective-permute-start.7 = (bf16[384,1536]{1,0:T(8,128)(2,1)S(1)}, bf16[384,1536]{1,0:T(8,128)(2,1)S(1)}, u32[]{:S(2)}, u32[]{:S(2)}) collective-permute-start(bf16[384,1536]{1,0:T(8,128)(2,1)S(1)} %mlp.3.refs_0_), channel_id=1, source_target_pairs={{0,2},{1,3},{4,6},{5,7}} | collective-permute-start | bytes 3538952 | tf_op jit(solution)/shard_map/ppermute | solution.py:604
  165.9 54.1 %collective-permute-start.8 = (bf16[384,1536]{1,0:T(8,128)(2,1)S(1)}, bf16[384,1536]{1,0:T(8,128)(2,1)S(1)}, u32[]{:S(2)}, u32[]{:S(2)}) collective-permute-start(bf16[384,1536]{1,0:T(8,128)(2,1)S(1)} %mlp.4.refs_1_), channel_id=1, source_target_pairs={{0,2},{1,3},{4,6},{5,7}} | collective-permute-start | bytes 3538952 | tf_op jit(solution)/shard_map/ppermute | solution.py:607
  227.8 45.1 %copy-start.7 = (bf16[384,1536]{1,0:T(8,128)(2,1)S(1)}, bf16[384,1536]{1,0:T(8,128)(2,1)}, u32[]{:S(2)}) copy-start(bf16[384,1536]{1,0:T(8,128)(2,1)} %copy-done.6) | copy-start | bytes 3538948
  227.8 4.6 %collective-permute-start.10 = (bf16[24,384,128]{2,1,0:T(8,128)(2,1)S(1)}, bf16[24,384,128]{2,1,0:T(8,128)(2,1)S(1)}, u32[]{:S(2)}, u32[]{:S(2)}) collective-permute-start(bf16[24,384,128]{2,1,0:T(8,128)(2,1)S(1)} %kv.3.refs_2_.refs_3_), channel_id=1, source_target_pairs={{0,1},{1,0},{2,3},{3,2},{4,5},{5,4},{6,7},{7,6}} | collective-permute-start | bytes 7077896 | tf_op jit(solution)/shard_map/ppermute | solution.py:616
  227.8 7.9 %collective-permute-start.9 = (bf16[24,384,128]{2,1,0:T(8,128)(2,1)S(1)}, bf16[24,384,128]{2,1,0:T(8,128)(2,1)S(1)}, u32[]{:S(2)}, u32[]{:S(2)}) collective-permute-start(bf16[24,384,128]{2,1,0:T(8,128)(2,1)S(1)} %kv.2.refs_0_.refs_1_), channel_id=1, source_target_pairs={{0,1},{1,0},{2,3},{3,2},{4,5},{5,4},{6,7},{7,6}} | collective-permute-start | bytes 7077896 | tf_op jit(solution)/shard_map/ppermute | solution.py:613
  272.9 2.3 copy-start.16

commit v3 on v2

--- a/solution.py
+++ b/solution.py
@@ -12,6 +12,7 @@
 CHUNK = 64
 NORM_EPS = 1e-6
 ROPE_BASE = 10000.0
+LANES = 128
 F32 = jnp.float32
 BF16 = jnp.bfloat16
 NT = (((1,), (1,)), ((), ()))
@@ -81,8 +82,8 @@
         jax.ShapeDtypeStruct((tokens, dim), BF16),
         jax.ShapeDtypeStruct((tokens, inner), BF16),
         jax.ShapeDtypeStruct((tokens, 256), BF16),
-        jax.ShapeDtypeStruct((tokens, 128), F32),
-        jax.ShapeDtypeStruct((tokens, 128), F32),
+        jax.ShapeDtypeStruct((tokens, LANES), F32),
+        jax.ShapeDtypeStruct((tokens, LANES), F32),
     )
     return pl.pallas_call(
         functools.partial(in_proj_kernel, n_heads),
@@ -91,14 +92,14 @@
             full_spec((tokens, dim)),
             full_spec(gains.shape),
             pl.BlockSpec((tile, dim), lambda i: (jnp.where(i == 0, last, i - 1), 0)),
-            full_spec((8, 128)),
+            full_spec((8, LANES)),
         ],
         out_specs=(
             full_spec((tokens, dim)),
             pl.BlockSpec((tokens, tile), lambda i: (0, jnp.maximum(i - 1, 0))),
             full_spec((tokens, 256)),
-            full_spec((tokens, 128)),
-            full_spec((tokens, 128)),
+            full_spec((tokens, LANES)),
+            full_spec((tokens, LANES)),
         ),
         out_shape=out_shape,
         compiler_params=params(("arbitrary",), 40),
@@ -122,7 +123,7 @@
         in_specs=[full_spec((tokens, dim)), pl.BlockSpec((tile, dim), lambda i: (i + first, 0))],
         out_specs=pl.BlockSpec((tokens, tile), lambda i: (0, i)),
         out_shape=jax.ShapeDtypeStruct((tokens, inner), F32),
-        compiler_params=params(("arbitrary",), 40),
+        compiler_params=params(("arbitrary",), 60),
         cost_estimate=cost(2 * tokens * dim * inner, 21e6),
         name="z_proj",
     )(hid, w_in_t)
@@ -149,7 +150,7 @@
 
 
 def step_weights(sc_ref, seg_ref, dt, cum2):
-    row = lax.broadcasted_iota(jnp.int32, (STEP, 128), 0)
+    row = lax.broadcasted_iota(jnp.int32, (STEP, LANES), 0)
     start = doc_start(seg_ref[...], sc_ref, N_SRC) - (sc_ref[N_SRC - 1] + pl.program_id(0) * STEP)
     upper = row < CHUNK
     last = lambda v: jnp.where(upper, v[CHUNK - 1:CHUNK, :], v[STEP - 1:STEP, :])
@@ -163,7 +164,7 @@
 
 
 def b_transposed(bc_ref, c):
-    return bc_ref[half_rows(c), :128].astype(F32).T.astype(BF16)
+    return bc_ref[half_rows(c), :LANES].astype(F32).T.astype(BF16)
 
 
 def ssd_state_kernel(sc_ref, x_ref, bc_ref, dt_ref, cum_ref, seg_ref, end_ref, decay_ref, e_ref, xp_ref, xw_ref):
@@ -175,9 +176,9 @@
 
     cum2 = cum_ref[...] * LOG2E
     rel, end_w = step_weights(sc_ref, seg_ref, dt_ref[...], cum2)
-    lane = lax.broadcasted_iota(jnp.int32, (STEP, 128), 1)
+    lane = lax.broadcasted_iota(jnp.int32, (STEP, LANES), 1)
     carry = jnp.where((rel < 0) & (lane < 64), jnp.exp2(cum2), 0.0)
-    ends = [jnp.broadcast_to(carry[r:r + 1, :], (8, 128)) for r in (CHUNK - 1, STEP - 1)]
+    ends = [jnp.broadcast_to(carry[r:r + 1, :], (8, LANES)) for r in (CHUNK - 1, STEP - 1)]
     xp_ref[...] = dot(split3(jnp.concatenate([end_w] + ends, axis=0)), e_ref[...])
     xw_ref[...] = (x_ref[...].astype(F32) * xp_ref[:STEP, :]).astype(BF16)
     add = [dot(b_transposed(bc_ref, c), xw_ref[half_rows(c), :]) for c in range(2)]
@@ -192,9 +193,9 @@
     return pl.pallas_call(
         ssd_state_kernel,
         grid=(tokens // STEP,),
-        in_specs=[SMEM_SPEC, row(inner), row(256), row(128), row(128), row(128)],
-        out_specs=(full_spec((128, inner)), full_spec((1, inner))),
-        out_shape=(jax.ShapeDtypeStruct((128, inner), F32), jax.ShapeDtypeStruct((1, inner), F32)),
+        in_specs=[SMEM_SPEC, row(inner), row(256), row(LANES), row(LANES), row(LANES)],
+        out_specs=(full_spec((LANES, inner)), full_spec((1, inner))),
+        out_shape=(jax.ShapeDtypeStruct((LANES, inner), F32), jax.ShapeDtypeStruct((1, inner), F32)),
         scratch_shapes=[pltpu.VMEM((256, inner), BF16), pltpu.VMEM((STEP + 16, inner), F32), pltpu.VMEM((STEP, inner), BF16)],
         compiler_params=params(("arbitrary",), 40),
         cost_estimate=cost(2 * tokens * 256 * inner, 8e6),
@@ -202,12 +203,19 @@
     )(scalars, xs, bc, dt, cum, seg_wide)
 
 
-def ssd_full_kernel(sc_ref, x_ref, bc_ref, dt_ref, cum_ref, seg_ref, z_ref, hin_ref, skip_ref, gain_ref, out_ref,
-                    state_ref, y_ref, e_ref, xp_ref, xw_ref, turn_ref, pack_ref):
+def ssd_full_kernel(sc_ref, x_ref, bc_ref, dt_ref, cum_ref, seg_ref, z_ref, got_ref, other_ref, pair_ref, pdecay_ref, head_ref, gain_ref, out_ref,
+                    skip_ref, state_ref, y_ref, e_ref, xp_ref, xw_ref, turn_ref, pack_ref):
     @pl.when(pl.program_id(0) == 0)
     def _():
-        state_ref[...] = hin_ref[...]
+        odd = sc_ref[N_SRC + 10] == 1
+        decay = jnp.where(odd, jnp.where(sc_ref[N_SRC + 11] == 1, pdecay_ref[...], 0.0), 1.0)
+        half = got_ref.shape[0]
+        for k, same, turned in ((0, got_ref, other_ref), (1, other_ref, got_ref)):
+            rows = slice(k * half, (k + 1) * half)
+            chip_in = jnp.where(odd, turned[...], same[...])
+            state_ref[rows, :] = decay * chip_in + jnp.where(odd, pair_ref[rows, :], 0.0)
         fill_spread(e_ref)
+        skip_ref[...] = dot(split3(head_ref[...]), e_ref[...])
 
     inner = x_ref.shape[1]
     n_heads = inner // 64
@@ -226,36 +234,36 @@
         pack_ref[0, k] = jnp.where(left, even, pltpu.roll(odd, 64, 1))
         pack_ref[1, k] = jnp.where(left, pltpu.roll(even, 64, 1), odd)
 
-    row_id = lax.broadcasted_iota(jnp.int32, (CHUNK, 128), 0)
-    lane_id = lax.broadcasted_iota(jnp.int32, (CHUNK, 128), 1)
+    row_id = lax.broadcasted_iota(jnp.int32, (CHUNK, LANES), 0)
+    lane_id = lax.broadcasted_iota(jnp.int32, (CHUNK, LANES), 1)
     left = lane_id < 64
     src = jnp.where(left, lane_id, lane_id - 64)
     for c in range(2):
         rows = half_rows(c)
         state = state_ref[...]
         opens = rel[rows] < 0
-        c_open = jnp.where(opens, bc_ref[rows, 128:].astype(F32), 0.0).astype(BF16)
+        c_open = jnp.where(opens, bc_ref[rows, LANES:].astype(F32), 0.0).astype(BF16)
         carried = dot(c_open, state.astype(BF16))
         carry_x = jnp.exp2(xp_ref[rows, :])
         keep = jnp.where(opens[CHUNK - 1:CHUNK, :], 1.0, 0.0)
-        dec = carry_x[CHUNK - 1:CHUNK, :] * jnp.concatenate([keep] * (inner // 128), axis=1)
-        y_ref[rows, :] = carried * carry_x + skip_ref[...] * x_ref[rows, :].astype(F32)
+        dec = carry_x[CHUNK - 1:CHUNK, :] * jnp.concatenate([keep] * (inner // LANES), axis=1)
+        y_ref[rows, :] = carried * carry_x + skip_ref[2:3, :] * x_ref[rows, :].astype(F32)
         state_ref[...] = dec * state + dot(b_transposed(bc_ref, c), xw_ref[rows, :])
 
     for c in range(2):
         rows = half_rows(c)
         visible = (src >= rel[rows]) & (src <= row_id)
-        b_blk = bc_ref[rows, :128]
-        scores = dot(bc_ref[rows, 128:], jnp.concatenate([b_blk, b_blk], axis=0), NT)
+        b_blk = bc_ref[rows, :LANES]
+        scores = dot(bc_ref[rows, LANES:], jnp.concatenate([b_blk, b_blk], axis=0), NT)
         scores = jnp.where(visible, scores, 0.0)
-        left16 = lax.broadcasted_iota(jnp.int32, (CHUNK, 128), 1) < 64
-        zero = jnp.zeros((CHUNK, 128), BF16)
+        left16 = lax.broadcasted_iota(jnp.int32, (CHUNK, LANES), 1) < 64
+        zero = jnp.zeros((CHUNK, LANES), BF16)
         for g in range(inner // 256):
             cols = slice(g * 256, (g + 1) * 256)
             mixes, diag = [], []
             for k in range(2):
                 pair = 2 * g + k
-                sub = slice(pair * 128, (pair + 1) * 128)
+                sub = slice(pair * LANES, (pair + 1) * LANES)
                 cum_s = pack_ref[c, 0, pair:pair + 1, :]
                 dt_s = pack_ref[c, 1, pair:pair + 1, :]
                 decay = jnp.exp2(jnp.minimum(xp_ref[rows, sub] - cum_s, 0.0))
@@ -270,27 +278,28 @@
     out_ref[...] = (y * inv * gain_ref[...] * z_ref[...]).astype(BF16)
 
 
-def ssd_full(scalars, xs, bc, dt, cum, seg_wide, z, h_in, skip, gain):
+def ssd_full(scalars, xs, bc, dt, cum, seg_wide, z, got, other, pair_state, pair_decay, head_pad, gain):
     tokens, inner = xs.shape
     row = lambda width: pl.BlockSpec((STEP, width), lambda i: (i, 0))
     return pl.pallas_call(
         ssd_full_kernel,
         grid=(tokens // STEP,),
         in_specs=[
-            SMEM_SPEC, row(inner), row(256), row(128), row(128), row(128),
-            row(inner), full_spec((128, inner)), full_spec((1, inner)), full_spec((1, inner)),
+            SMEM_SPEC, row(inner), row(256), row(LANES), row(LANES), row(LANES),
+            row(inner), full_spec(got.shape), full_spec(got.shape), full_spec((LANES, inner)), full_spec((1, inner)), full_spec((8, LANES)),
+            full_spec((1, inner)),
         ],
         out_specs=row(inner),
         out_shape=jax.ShapeDtypeStruct((tokens, inner), BF16),
         scratch_shapes=[
-            pltpu.VMEM((128, inner), F32), pltpu.VMEM((STEP, inner), F32), pltpu.VMEM((256, inner), BF16),
-            pltpu.VMEM((2 * STEP, inner), F32), pltpu.VMEM((STEP, inner), BF16), pltpu.VMEM((2, 128, STEP), F32),
-            pltpu.VMEM((2, 2, inner // 128, STEP), F32),
+            pltpu.VMEM((8, inner), F32), pltpu.VMEM((LANES, inner), F32), pltpu.VMEM((STEP, inner), F32), pltpu.VMEM((256, inner), BF16),
+            pltpu.VMEM((2 * STEP, inner), F32), pltpu.VMEM((STEP, inner), BF16), pltpu.VMEM((2, LANES, STEP), F32),
+            pltpu.VMEM((2, 2, inner // LANES, STEP), F32),
         ],
-        compiler_params=params(("arbitrary",), 40),
+        compiler_params=params(("arbitrary",), 44),
         cost_estimate=cost(12e9, 20e6),
         name="ssd_full",
-    )(scalars, xs, bc, dt, cum, seg_wide, z, h_in, skip, gain)
+    )(scalars, xs, bc, dt, cum, seg_wide, z, got, other, pair_state, pair_decay, head_pad, gain)
 
 
 def proj_add_kernel(a_ref, w_ref, *refs):
@@ -310,7 +319,7 @@
         in_specs=[full_spec((tokens, depth)), col(depth)] + [col(r.shape[0]) for r in res],
         out_specs=col(tokens),
         out_shape=jax.ShapeDtypeStruct((tokens, dim), BF16),
-        compiler_params=params(("arbitrary",), 40),
+        compiler_params=params(("arbitrary",), 44),
         cost_estimate=cost(2 * tokens * depth * dim, 2 * (tokens * depth + depth * dim + 2 * tokens * dim)),
         name="proj_add",
     )(a, w, *res)
@@ -354,7 +363,7 @@
         out_specs=full_spec((tokens, dim)),
         out_shape=jax.ShapeDtypeStruct((tokens, dim), BF16),
         scratch_shapes=[pltpu.VMEM((tokens, dim), BF16), pltpu.VMEM((tokens, dim), F32)],
-        compiler_params=params(("arbitrary",), 40),
+        compiler_params=params(("arbitrary",), 44),
         cost_estimate=cost(6 * tokens * dim * ff, 6 * dim * ff),
         name="mlp",
     )(x_rows, gains, mlp_up, mlp_up, mlp_down)
@@ -453,10 +462,10 @@
     start = doc_start(seg_ref[...], sc_ref, N_SRC)
 
     def lanes(x, width):
-        return jnp.concatenate([x] * (width // 128), axis=1)
+        return jnp.concatenate([x] * (width // LANES), axis=1)
 
     def fold(x):
-        return sum(x[:, i:i + 128] for i in range(128, x.shape[1], 128)) + x[:, :128]
+        return sum(x[:, i:i + LANES] for i in range(LANES, x.shape[1], LANES)) + x[:, :LANES]
 
     def weights(h, k_ref, rows, bias):
         s = dot(q_ref[h], k_ref[h, rows, :], NT) + bias
@@ -469,7 +478,7 @@
     bias_ref[...] = jnp.where((col_id + q0 >= lanes(start, BLOCK)) & (col_id <= row_id), 0.0, NEG)
     for h in every:
         s, top = weights(h, k_ref, rows, bias_ref[...])
-        m_new = jnp.broadcast_to(top, (BLOCK, 128))
+        m_new = jnp.broadcast_to(top, (BLOCK, LANES))
         p = jnp.exp2((s - lanes(m_new, BLOCK)) * scale)
         m_ref[h] = m_new
         l_ref[h] = fold(p)
@@ -522,7 +531,7 @@
     groups = n_heads // per
     in_specs = [
         pl.BlockSpec((per, BLOCK, head_dim), lambda h, j, sc: (h, j, 0)),
-        pl.BlockSpec((BLOCK, 128), lambda h, j, sc: (j, 0)),
+        pl.BlockSpec((BLOCK, LANES), lambda h, j, sc: (j, 0)),
     ]
     args = [q, seg_wide]
     for kv in kv_list:
@@ -537,7 +546,7 @@
             grid=(groups, tokens // BLOCK),
             in_specs=in_specs,
             out_specs=pl.BlockSpec((BLOCK, per * head_dim), lambda h, j, sc: (j, h)),
-            scratch_shapes=[pltpu.VMEM((per, BLOCK, 128), F32)] * 2
+            scratch_shapes=[pltpu.VMEM((per, BLOCK, LANES), F32)] * 2
             + [pltpu.VMEM((per, BLOCK, head_dim), F32), pltpu.VMEM((BLOCK, BLOCK), F32)],
         ),
         out_shape=jax.ShapeDtypeStruct((tokens, n_heads * head_dim), BF16),
@@ -562,43 +571,53 @@
         n_heads = ssm_head.shape[1]
         n_query, head_dim = w_attn_out.shape[:2]
 
+        odd = (dev % 2) == 1
         counts = jnp.sum((seg_ids[None, :] <= jnp.arange(4, dtype=jnp.int32)[:, None]).astype(jnp.int32), axis=1)
-        earlier = [lax.ppermute(counts, 'sp', [(d, d + k) for d in range(n_dev - k)]) for k in range(1, n_dev)]
-        seg_wide = jnp.broadcast_to(seg_ids[:, None], (tokens, 128))
-        head_pad = jnp.pad(ssm_head, ((0, 5), (0, 128 - n_heads)))
-        skip = jnp.repeat(ssm_head[2:3], inner // n_heads, axis=1)
+        ends = jnp.stack([seg_ids[0], seg_ids[tokens - 1]])
+        seg_wide = jnp.broadcast_to(seg_ids[:, None], (tokens, LANES))
+        head_pad = jnp.pad(ssm_head, ((0, 5), (0, LANES - n_heads)))
         w_in_t = w_in.T
         hid, xs, bc, dt, cum = in_proj(x_rows, norm_gains, w_in_t, head_pad, inner, n_heads)
+        local = jnp.pad(jnp.where(counts > 0, counts + 1, 0), (N_SRC, 8))
+        local = jnp.where(jnp.arange(16) == N_SRC - 1, 1, local)
+        state_end, decay = ssd_state(local, xs, bc, dt, cum, seg_wide)
+
+        pair_state = lax.ppermute(state_end, 'sp', swap_perm)
+        pair_decay = lax.ppermute(decay, 'sp', swap_perm)
+        info, decay = lax.optimization_barrier((jnp.concatenate([counts, ends, ends]), decay))
+        pair_info = lax.ppermute(info, 'sp', swap_perm)
+        joins = jnp.where(odd, seg_ids[0] == pair_info[5], pair_info[4] == seg_ids[tokens - 1])
+        half = state_end.shape[0] // 2
+        first = jnp.where(odd, half, 0)
+        own_half = lax.dynamic_slice_in_dim(state_end, first, half, 0)
+        pair_half = lax.dynamic_slice_in_dim(pair_state, first, half, 0)
+        odd_decay = jnp.where(joins, jnp.where(odd, decay, pair_decay), 0.0)
+        mine = odd_decay * jnp.where(odd, pair_half, own_half) + jnp.where(odd, own_half, pair_half)
+        mine, hid = lax.optimization_barrier((mine, hid))
+        got = lax.ppermute(mine, 'sp', cross_perm)
+        slot8 = jnp.arange(8, dtype=jnp.int32)
+        chip_info = jnp.where(slot8 < 4, info + pair_info, jnp.where(odd, info, pair_info))
+        far_info = lax.ppermute(chip_info, 'sp', cross_perm)
+        z = z_proj(hid, w_in_t, inner)
+        pos = (dev * tokens + jnp.arange(tokens)).astype(F32)
+        cos, sin = rope_tables(pos, head_dim)
+        cos_far, sin_far = rope_tables(pos - 2.0 * tokens, head_dim)
+        got, z, cos, sin, cos_far, sin_far = lax.optimization_barrier((got, z, cos, sin, cos_far, sin_far))
+        other = lax.ppermute(got, 'sp', swap_perm)
+
         first_pos = dev * tokens
         far = jnp.int32(1 << 24)
         pair_pos = (dev ^ 1) * tokens
-        earlier, cum = lax.optimization_barrier((earlier, cum))
-        doc_starts = counts + sum(earlier)
+        doc_starts = counts + jnp.where(odd, pair_info[:4], 0) + far_info[:4]
         slot = jnp.arange(4, dtype=jnp.int32)
         bases = jnp.where(slot == 3, first_pos, pair_pos)
         bases = jnp.where(slot >= 2, bases, jnp.where(dev >= 2, jnp.where(slot == 0, first_pos, pair_pos) - 2 * tokens, far))
         edge_seg = jnp.pad(seg_ids[::BLOCK], (0, 8 - tokens // BLOCK))
+        edge_seg = jnp.where(jnp.arange(8) == 6, odd.astype(jnp.int32), edge_seg)
+        edge_seg = jnp.where(jnp.arange(8) == 7, (pair_info[4] == far_info[5]).astype(jnp.int32), edge_seg)
         scalars = jnp.concatenate([bases, doc_starts, edge_seg])
-        state_end, decay = ssd_state(scalars, xs, bc, dt, cum, seg_wide)
-
-        odd = (dev % 2) == 1
-        pair_state = lax.ppermute(state_end, 'sp', swap_perm)
-        pair_decay = lax.ppermute(decay, 'sp', swap_perm)
-        chip_state = jnp.where(odd, decay * pair_state + state_end, pair_decay * state_end + pair_state)
-        half = state_end.shape[0] // 2
-        mine = jnp.where(odd, chip_state[half:], chip_state[:half])
-        mine, hid = lax.optimization_barrier((mine, hid))
-        got = lax.ppermute(mine, 'sp', cross_perm)
-        z = z_proj(hid, w_in_t, inner)
-        pos = (first_pos + jnp.arange(tokens)).astype(F32)
-        cos, sin = rope_tables(pos, head_dim)
-        cos_far, sin_far = rope_tables(pos - 2.0 * tokens, head_dim)
-        got, z, cos, sin, cos_far, sin_far = lax.optimization_barrier((got, z, cos, sin, cos_far, sin_far))
-        other = lax.ppermute(got, 'sp', swap_perm)
-        chip_in = jnp.where(odd, jnp.concatenate([other, got], axis=0), jnp.concatenate([got, other], axis=0))
-        h_in = jnp.where(odd, pair_decay * chip_in + pair_state, chip_in)
-
-        gated = ssd_full(scalars, xs, bc, dt, cum, seg_wide, z, h_in, skip, y_gain[None, :])
+
+        gated = ssd_full(scalars, xs, bc, dt, cum, seg_wide, z, got, other, pair_state, pair_decay, head_pad, y_gain[None, :])
         x_one = proj_add(gated, w_out, [x_rows])
         x_a = mlp(x_one, norm_gains, mlp_up, mlp_down, 0, 0, 2)
         far_a = lax.ppermute(x_a, 'sp', cross_perm)

time: 333 us -> 338 us (1.015)
  Pallas kernels: 238 us -> 244 us
  waiting for transfers between devices: 59.3 us -> 64.3 us
  local copies, waits for them, and re-layouts: 14.6 us -> 10.3 us
  between operations: 0.52 us -> 3.91 us
    unnamed x48 -> x28, local copies, waits for them, and re-layouts: 12.2 us -> 5.11 us
    ppermute x3 -> x2, waiting for transfers between devices: 0.01 us -> 3.98 us  [the longest x1 3.98 us: layers(): far_info = lax.ppermute(chip_info, 'sp', cross_perm)]
    select_n x3 -> x5, other arithmetic: 3.55 us -> 0.12 us  [the longest x1 0.08 us: layers(): local = jnp.where(jnp.arange(16) == N_SRC - 1, 1, local)]
  transfers between devices with their start and end apart: 12 -> 11, of which waited for: 7 -> 6; matrix products, arithmetic and copies ran while one was open for 2% -> 3% of each run, Pallas kernels for 11% -> 8%
where the time goes in v3:
time: 338 us; the launch traced here: 337 us
  Pallas kernels  244 us (72%)
  waiting for transfers between devices  64.3 us (19%)
  local copies, waits for them, and re-layouts  10.3 us (3%)
  other arithmetic  7.97 us (2%)
  starting transfers between devices  6.41 us (2%)
  between operations  3.91 us (1%)
    pallas_call x3, Pallas kernels, mlp(): pl.pallas_call(functools.partial(mlp_kernel, layer), grid=(n_ff,), in_spe...  107 us
    pallas_call x1, Pallas kernels, attention(): pl.pallas_call(attn_kernel, grid_spec=pltpu.PrefetchScalarGridSpec(num_sc...  37.2 us
    pallas_call x3, Pallas kernels, qkv_proj(): pl.pallas_call(functools.partial(qkv_kernel, n_q, n_rot, len(parts)), gri...  32.4 us
    ppermute x1, waiting for transfers between devices, layers(): far_a = lax.ppermute(x_a, 'sp', cross_perm)  28.1 us
    pallas_call x1, Pallas kernels, ssd_full(): pl.pallas_call(ssd_full_kernel, grid=(tokens // STEP,), in_specs=[SMEM_SP...  19.2 us
    ppermute x1, waiting for transfers between devices, layers(): far_b = lax.ppermute(x_b, 'sp', cross_perm)  17.1 us
    pallas_call x2, Pallas kernels, proj_add(): pl.pallas_call(proj_add_kernel, grid=(dim // tile,), in_specs=[full_spec(...  15.7 us
    pallas_call x1, Pallas kernels, z_proj(): pl.pallas_call(z_proj_kernel, grid=(inner // tile,), in_specs=[full_spec(...  12.8 us
  transfers between devices with their start and end apart: 11, of which 6 were waited for; matrix products, arithmetic and copies ran while one was open for 3% of the time, Pallas kernels for 8%

profile of v3, /device:TPU:2, one launch (start us, length us, event | category | flops | bytes accessed | tf_op | source)
XLA Modules:
  0.0 336.9 jit_solution(16469364621265725543)
XLA Ops:
  0.0 0.8 convert_reduce_fusion
  0.8 0.1 compare_select_fusion.4.sc_ref
  0.9 0.7 pad.13.head_ref
  1.6 0.7 copy-done.5
  2.3 1.7 copy-done.7
  4.0 11.7 %in_proj.1 = (bf16[768,1536]{1,0:T(8,128)(2,1)S(1)}, bf16[768,3072]{1,0:T(8,128)(2,1)S(1)}, bf16[768,256]{1,0:T(8,128)(2,1)S(1)}, f32[768,128]{1,0:T(8,128)S(1)}, f32[768,128]{1,0:T(8,128)S(1)}) custom-call(bf16[768,1536]{1,0:T(8,128)(2,1)S(1)} %copy-done.7, f32[4,1536]{1,0:T(4,128)S(1)} %copy-done.5, bf16[6448,1536]{1,0:T(8,128)(2,1)} %bitcast.12, ...), custom_call_target="tpu_custom_call" | custom-call | flops 9663676416 | bytes 16000000 | tf_op jit(solution)/shard_map/in_proj/pallas_call | solution.py:88
  15.7 0.0 copy-start.2
  15.7 1.4 copy-done.2
  17.1 0.2 broadcast_in_dim.52.seg_ref
  17.2 7.8 %ssd_state.1 = (f32[128,3072]{1,0:T(8,128)}, f32[1,3072]{1,0:T(1,128)S(1)}) custom-call(s32[16]{0:T(128)S(1)} %compare_select_fusion.4.sc_ref, bf16[768,3072]{1,0:T(8,128)(2,1)S(1)} %get-tuple-element.30.x_ref, bf16[768,256]{1,0:T(8,128)(2,1)S(1)} %get-tuple-element.31.bc_ref, f32[768,128]{1,0:T(8,128)S(1)} %get-tuple-element.32.dt_ref, ...), custom_call_target="tpu_custom_call" | custom-call | flops 1207959552 | bytes 8000000 | tf_op jit(solution)/shard_map/ssd_state/pallas_call | solution.py:193
  25.0 0.0 copy-done.1
  25.0 0.0 collective-permute-start.2
  25.0 0.5 collective-permute-start.3
  25.5 0.6 fusion.5
  26.1 2.5 concatenate.19
  28.6 0.0 collective-permute-start
  28.6 3.9 %fusion.1 = (f32[768,64]{1,0:T(8,128)S(1)}, f32[768,64]{1,0:T(8,128)S(1)}, f32[768,64]{1,0:T(8,128)S(1)}, f32[768,64]{1,0:T(8,128)}, f32[768,64]{1,0:T(8,128)}, /*index=5*/f32[768,64]{1,0:T(8,128)}) fusion(f32[64]{0:T(128)S(1)} %multiply_power_fusion, f32[768]{0:T(1024)S(1)} %broadcast_add_fusion, f32[768]{0:T(1024)S(1)} %add_convert_fusion), kind=kLoop, calls=%fused_computation.10 | loop fusion | flops 196608 | bytes 1186048 | tf_op jit(solution)/shard_map/neg | solution.py:377
  32.6 0.3 pad_maximum_fusion.2
  32.8 0.0 collective-permute-done
  32.8 0.6 fusion.6
  35.8 0.0 copy-start.10
  35.8 0.0 copy-start.11
  35.8 0.0 copy-start.12
  35.8 0.0 collective-permute-done.2.pdecay_ref
  35.8 0.0 collective-permute-done.3.pair_ref
  35.8 2.5 select_add_fusion
  38.3 1.3 collective-permute-start.4
  39.6 0.0 copy-done.10
  39.6 0.0 copy-done.11
  39.6 0.3 pad_maximum_fusion
  39.9 0.0 copy-start.9
  39.9 12.8 %z_proj.1.z_ref = f32[768,3072]{1,0:T(8,128)} custom-call(bf16[768,1536]{1,0:T(8,128)(2,1)} %copy-done.2, bf16[6448,1536]{1,0:T(8,128)(2,1)} %bitcast.13), custom_call_target="tpu_custom_call" | custom-call | flops 7247757312 | bytes 21000000 | tf_op jit(solution)/shard_map/z_proj/pallas_call | solution.py:120
  52.8 7.7 %collective-permute-done.4.got_ref = f32[64,3072]{1,0:T(8,128)} collective-permute-done((f32[64,3072]{1,0:T(8,128)}, f32[64,3072]{1,0:T(8,128)}, u32[]{:S(2)}, u32[]{:S(2)}) %collective-permute-start.4) | collective-permute-done | bytes 786464 | tf_op jit(solution)/shard_map/ppermute | solution.py:597
  60.5 0.0 collective-permute-start.5
  60.5 0.1 slice.33
  60.6 1.5 collective-permute-start.1
  62.1 4.0 %collective-permute-done.1 = s32[8]{0:T(128)S(1)} collective-permute-done((s32[8]{0:T(128)S(1)}, s32[8]{0:T(128)S(1)}, u32[]{:S(2)}, u32[]{:S(2)}) %collective-permute-start.1) | collective-permute-done | bytes 64 | tf_op jit(solution)/shard_map/ppermute | solution.py:600
  66.0 0.6 slice.32
  67.9 0.1 pad_add_fusion.sc_ref
  67.9 0.0 collective-permute-done.5.other_ref
  68.0 19.2 %ssd_full.1.a_ref = bf16[768,3072]{1,0:T(8,128)(2,1)S(1)} custom-call(s32[16]{0:T(128)S(1)} %pad_add_fusion.sc_ref, bf16[768,3072]{1,0:T(8,128)(2,1)} %copy-done.1, bf16[768,256]{1,0:T(8,128)(2,1)S(1)} %get-tuple-element.31.bc_ref, f32[768,128]{1,0:T(8,128)S(1)} %get-tuple-element.32.dt_ref, f32[768,128]{1,0:T(8,128)S(1)} %get-tuple-element.33.cum_ref, ...), custom_call_target="tpu_custom_call" | custom-call | flops 12000000000 | bytes 20000000 | tf_op jit(solution)/shard_map/ssd_full/pallas_call | solution.py:284
  87.1 0.0 copy-start.6
  87.2 9.9 %proj_add.2.x_ref = bf16[768,1536]{1,0:T(8,128)(2,1)S(1)} custom-call(bf16[768,3072]{1,0:T(8,128)(2,1)S(1)} %ssd_full.1.a_ref, bf16[3072,1536]{1,0:T(8,128)(2,1)} %w_ref.1, bf16[768,1536]{1,0:T(8,128)(2,1)S(1)} %copy-done.8), custom_call_target="tpu_custom_call" | custom-call | flops 7247757312 | bytes 18874368 | tf_op jit(solution)/shard_map/proj_add/pallas_call | solution.py:316
  97.1 27.7 %mlp.3.refs_0_ = bf16[384,1536]{1,0:T(8,128)(2,1)S(1)} custom-call(bf16[768,1536]{1,0:T(8,128)(2,1)S(1)} %proj_add.2.x_ref, f32[4,1536]{1,0:T(4,128)S(1)} %copy-done.6, bf16[2,1536,12288]{2,1,0:T(8,128)(2,1)} %wu_ref.5, bf16[2,1536,12288]{2,1,0:T(8,128)(2,1)} %wu_ref.5, bf16[2,6144,1536]{2,1,0:T(8,128)(2,1)} %wd_ref.5), custom_call_target="tpu_custom_call" | custom-call | flops 21743271936 | bytes 56623104 | tf_op jit(solution)/shard_map/mlp/pallas_call | solution.py:353
  124.8 27.7 %mlp.4.refs_1_ = bf16[384,1536]{1,0:T(8,128)(2,1)S(1)} custom-call(bf16[768,1536]{1,0:T(8,128)(2,1)S(1)} %proj_add.2.x_ref, f32[4,1536]{1,0:T(4,128)S(1)} %copy-done.6, bf16[2,1536,12288]{2,1,0:T(8,128)(2,1)} %wu_ref.5, bf16[2,1536,12288]{2,1,0:T(8,128)(2,1)} %wu_ref.5, bf16[2,6144,1536]{2,1,0:T(8,128)(2,1)} %wd_ref.5), custom_call_target="tpu_custom_call" | custom-call | flops 21743271936 | bytes 56623104 | tf_op jit(solution)/shard_map/mlp/pallas_call | solution.py:353
  152.5 0.0 copy-start.3
  152.6 16.9 %qkv.1 = (bf16[12,768,128]{2,1,0:T(8,128)(2,1)S(1)}, bf16[24,768,128]{2,1,0:T(8,128)(2,1)S(1)}) custom-call(bf16[384,1536]{1,0:T(8,128)(2,1)S(1)} %mlp.3.refs_0_, bf16[384,1536]{1,0:T(8,128)(2,1)S(1)} %mlp.4.refs_1_, f32[4,1536]{1,0:T(4,128)S(1)} %copy-done.6, f32[768,128]{1,0:T(8,128)S(1)} %get-tuple-element.45.refs_3_, ...), custom_call_target="tpu_custom_call" | custom-call | flops 10871635968 | bytes 22155776 | tf_op jit(solution)/shard_map/qkv/pallas_call | solution.py:425
  169.5 0.0 collective-permute-start.10
  169.5 1.3 collective-permute-start.6
  170.8 1.3 collective-permute-start.7
  172.1 28.1 %collective-permute-done.6.refs_0_ = bf16[384,1536]{1,0:T(8,128)(2,1)S(1)} collective-permute-done((bf16[384,1536]{1,0:T(8,128)(2,1)S(1)}, bf16[384,1536]{1,0:T(8,128)(2,1)S(1)}, u32[]{:S(2)}, u32[]{:S(2)}) %collective-permute-start.6) | collective-permute-done | bytes 1179680 | tf_op jit(solution)/shard_map/ppermute | solution.py:623
  200.3 7.7 %kv.2.refs_0_.refs_1_ = bf16[24,384,128]{2,1,0:T(8,128)(2,1)S(1)} custom-call(bf16[384,1536]{1,0:T(8,128)(2,1)S(1)} %collective-permute-done.6.refs_0_, f32[4,1536]{1,0:T(4,128)S(1)} %copy-done.6, f32[768,128]{1,0:T(8,128)S(1)} %get-tuple-element.50.refs_2_, f32[768,128]{1,0:T(8,128)S(1)} %get-tuple-element.51.refs_3_, bf16[36,1536,128]{2,1,0:T(8,128)(2,1)} %bitcast.10), custom_call_target="tpu_custom_call" | custom-call | flops 3623878656 | bytes 17437184 | tf_op jit(solution)/shard_map/kv/pallas_call | solution.py:425
  208.0 17.1 %collective-permute-done.7.refs_0_ = bf16[384,1536]{1,0:T(8,128)(2,1)S(1)} collective-permute-done((bf16[384,1536]{1,0:T(8,128)(2,1)S(1)}, bf16[384,1536]{1,0:T(8,128)(2,1)S(1)}, u32[]{:S(2)}, u32[]{:S(2)}) %collective-permute-start.7) | collective-permute-done | bytes 1179680 | tf_op jit(solution)/shard_map/ppermute | solution.py:626
  225.1 7.7 %kv.3.refs_2_.refs_3_ = bf16[24,384,128]{2,1,0:T(8,128)(2,1)S(1)} custom-call(bf16[384,1536]{1,0:T(8,128)(2,1)S(1)} %collective-permute-done.7.refs_0_, f32[4,1536]{1,0:T(4,128)S(1)} %copy-done.6, f32[768,128]{1,0:T(8,128)S(1)} %get-tuple-element.50.refs_2_, f32[768,128]{1,0:T(8,128)S(1)} %get-tuple-element.51.refs_3_, bf16[36,1536,128]{2,1,0:T(8,128)(2,1)} %bitcast.11), custom_call_target="tpu_custom_call" | custom-call | flops 3623878656 | bytes 17437184 | tf_op jit(solution)/shard_map/kv/pallas_call | solution.py:425
  232.8 0.0 collective-permute-start.9
  232.8 0.5 collective-permute-start.8
  233.3 4.0 %collective-permute-done.9.refs_6_.refs_7_ = bf16[24,384,128]{2,1,0:T(8,128)(2,1)S(1)} collective-permute-done((bf16[24,384,128]{2,1,0:T(8,128)(2,1)S(1)}, bf16[24,384,128]{2,1,0:T(8,128)(2,1)S(1)}, u32[]{:S(2)}, u32[]{:S(2)}) %collective-permute-start.9) | collective-permute-done | bytes 2359328 | tf_op jit(solution)/shard_map/ppermute | solution.py:635
  237.4 3.4 %collective-permute-done.8.refs_4_.refs_5_ = bf16[24,384,128]{2,1,0:T(8,128)(2,1)S(1)} collective-permute-done((bf16[24,384,128]{2,1,0:T(8,128)(2,1)S(1)}, bf16[24,384,128]{2,1,0:T(8,128)(2,1)S(1)}, u32[]{:S(2)}, u32[]{:S(2)}) %collective-permute-start.8) | collective-permute-done | bytes 2359328 | tf_op jit(solution)/shard_map/ppermute | solution.py:632
  240.7 0.0 collective-permute-done.10.refs_8_.refs_9_
  240.7 37.2 %attention.1.a_ref = bf16[768,1536]{1,0:T(8,128)(2,1)S(1)} custom-call(s32[16]{0:T(128)S(1)} %pad_add_fusion.sc_ref, bf16[12,768,128]{2,1,0:T(8,128)(2,1)S(1)} %get-tuple-element.48.q_ref, s32[768,128]{1,0:T(8,128)S(1)} %broadcast_in_dim.52.seg_ref, bf16[24,384,128]{2,1,0:T(8,128)(2,1)S(1)} %kv.2.refs_0_.refs_1_, ...), custom_call_target="tpu_custom_call" | custom-call | flops 7247757312 | bytes 20000000 | tf_op jit(solution)/shard_map/attention/pallas_call | solution.py:542
  277.9 0.0 copy-start.4
  277.9 1.3 copy-done.4
  279.2 5.8 %proj_add.3.x_ref = bf16[768,1536]{1,0:T(8,128)(2,1)S(1)} custom-call(bf16[768,1536]{1,0:T(8,128)(2,1)S(1)} %attention.1.a_ref, bf16[1536,1536]{1,0:T(8,128)(2,1)} %bitcast.15, bf16[384,1536]{1,0:T(8,128)(2,1)S(1)} %mlp.3.refs_0_, bf16[384,1536]{1,0:T(8,128)(2,1)S(1)} %copy-done.4), custom_call_target="tpu_custom_call" | custom-call | flops 3623878656 | bytes 11796480 | tf_op jit(solution)/shard_map/proj_add/pallas_call | solution.py:316
  285.0 51.9 %mlp.5 = bf16[768,1536]{1,0:T(8,128)(2,1)} custom-call(bf16[768,1536]{1,0:T(8,128)(2,1)S(1)} %proj_add.3.x_ref, f32[4,1536]{1,0:T(4,128)S(1)} %copy-done.6, bf16[2,1536,12288]{2,1,0:T(8,128)(2,1)} %wu_ref.5, bf16[2,1536,12288]{2,1,0:T(8,128)(2,1)} %wu_ref.5, bf16[2,6144,1536]{2,1,0:T(8,128)(2,1)} %wd_ref.5), custom_call_target="tpu_custom_call" | custom-call | flops 43486543872 | bytes 56623104 | tf_op jit(solution)/shard_map/mlp/pallas_call | solution.py:353
  (22 shorter events, 0.1 us)
Async XLA Ops:
  1.6 0.7 copy-start.5
  2.3 1.7 copy-start.7
  4.0 13.1 %copy-start.13 = (s32[768]{0:T(1024)S(1)}, s32[768]{0:T(1024)}, u32[]{:S(2)}) copy-start(s32[768]{0:T(1024)} %param.12) | copy-start | bytes 9220
  15.7 1.4 copy-start.2
  17.1 8.0 %copy-start.1 = (bf16[768,3072]{1,0:T(8,128)(2,1)}, bf16[768,3072]{1,0:T(8,128)(2,1)S(1)}, u32[]{:S(2)}) copy-start(bf16[768,3072]{1,0:T(8,128)(2,1)S(1)} %get-tuple-element.30.x_ref) | copy-start | bytes 14155780
  25.0 10.8 %collective-permute-start.2 = (f32[1,3072]{1,0:T(1,128)S(1)}, f32[1,3072]{1,0:T(1,128)S(1)}, u32[]{:S(2)}, u32[]{:S(2)}) collective-permute-start(f32[1,3072]{1,0:T(1,128)S(1)} %get-tuple-element.36), channel_id=1, source_target_pairs={{0,1},{1,0},{2,3},{3,2},{4,5},{5,4},{6,7},{7,6}} | collective-permute-start | bytes 36872 | tf_op jit(solution)/shard_map/ppermute | solution.py:586
  25.0 10.8 %collective-permute-start.3 = (f32[128,3072]{1,0:T(8,128)}, f32[128,3072]{1,0:T(8,128)}, u32[]{:S(2)}, u32[]{:S(2)}) collective-permute-start(f32[128,3072]{1,0:T(8,128)} %get-tuple-element.37), channel_id=1, source_target_pairs={{0,1},{1,0},{2,3},{3,2},{4,5},{5,4},{6,7},{7,6}} | collective-permute-start | bytes 4718600 | tf_op jit(solution)/shard_map/ppermute | solution.py:585
  28.6 4.2 %collective-permute-start = (s32[8]{0:T(128)S(1)}, s32[8]{0:T(128)S(1)}, u32[]{:S(2)}, u32[]{:S(2)}) collective-permute-start(s32[8]{0:T(128)S(1)} %concatenate.19), channel_id=1, source_target_pairs={{0,1},{1,0},{2,3},{3,2},{4,5},{5,4},{6,7},{7,6}} | collective-permute-start | bytes 104 | tf_op jit(solution)/shard_map/ppermute | solution.py:588
  35.8 3.9 %copy-start.10 = (f32[768,64]{1,0:T(8,128)S(1)}, f32[768,64]{1,0:T(8,128)}, u32[]{:S(2)}) copy-start(f32[768,64]{1,0:T(8,128)} %get-tuple-element.63) | copy-start | bytes 589828
  35.8 3.9 %copy-start.11 = (f32[768,64]{1,0:T(8,128)S(1)}, f32[768,64]{1,0:T(8,128)}, u32[]{:S(2)}) copy-start(f32[768,64]{1,0:T(8,128)} %get-tuple-element.64) | copy-start | bytes 589828
  35.8 3.9 %copy-start.12 = (f32[768,64]{1,0:T(8,128)S(1)}, f32[768,64]{1,0:T(8,128)}, u32[]{:S(2)}) copy-start(f32[768,64]{1,0:T(8,128)} %get-tuple-element.65) | copy-start | bytes 589828
  38.3 22.1 %collective-permute-start.4 = (f32[64,3072]{1,0:T(8,128)}, f32[64,3072]{1,0:T(8,128)}, u32[]{:S(2)}, u32[]{:S(2)}) collective-permute-start(f32[64,3072]{1,0:T(8,128)} %select_add_fusion), channel_id=1, source_target_pairs={{0,2},{1,3},{4,6},{5,7}} | collective-permute-start | bytes 2359304 | tf_op jit(solution)/shard_map/ppermute | solution.py:597
  39.9 28.0 %copy-start.9 = (f32[3072]{0:T(1024)S(1)}, f32[3072]{0:T(1024)}, u32[]{:S(2)}) copy-start(f32[3072]{0:T(1024)} %param.16) | copy-start | bytes 36868
  60.5 7.5 %collective-permute-start.5 = (f32[64,3072]{1,0:T(8,128)}, f32[64,3072]{1,0:T(8,128)}, u32[]{:S(2)}, u32[]{:S(2)}) collective-permute-start(f32[64,3072]{1,0:T(8,128)} %collective-permute-done.4.got_ref), channel_id=1, source_target_pairs={{0,1},{1,0},{2,3},{3,2},{4,5},{5,4},{6,7},{7,6}} | collective-permute-start | bytes 2359304 | tf_op jit(solution)/shard_map/ppermute | solution.py:606
  60.6 5.5 %collective-permute-start.1 = (s32[8]{0:T(128)S(1)}, s32[8]{0:T(128)S(1)}, u32[]{:S(2)}, u32[]{:S(2)}) collective-permute-start(s32[8]{0:T(128)S(1)} %compare_select_fusion.2), channel_id=1, source_target_pairs={{0,2},{1,3},{4,6},{5,7}} | collective-permute-start | bytes 104 | tf_op jit(solution)/shard_map/ppermute | solution.py:600
  68.0 19.2 %copy-start.8 = (bf16[768,1536]{1,0:T(8,128)(2,1)S(1)}, bf16[768,1536]{1,0:T(8,128)(2,1)}, u32[]{:S(2)}) copy-start(bf16[768,1536]{1,0:T(8,128)(2,1)} %refs_0_.1) | copy-start | bytes 7077892
  87.1 9.9 %copy-start.6 = (f32[4,1536]{1,0:T(4,128)S(1)}, f32[4,1536]{1,0:T(4,128)}, u32[]{:S(2)}) copy-start(f32[4,1536]{1,0:T(4,128)} %gain_ref.7) | copy-start | bytes 73732
  152.5 18.3 %copy-start.3 = (bf16[384,1536]{1,0:T(8,128)(2,1)}, bf16[384,1536]{1,0:T(8,128)(2,1)S(1)}, u32[]{:S(2)}) copy-start(bf16[384,1536]{1,0:T(8,128)(2,1)S(1)} %mlp.4.refs_1_) | copy-start | bytes 3538948
  169.5 38.5 %copy-start = (bf16[24,768,128]{2,1,0:T(8,128)(2,1)}, bf16[24,768,128]{2,1,0:T(8,128)(2,1)S(1)}, u32[]{:S(2)}) copy-start(bf16[24,768,128]{2,1,0:T(8,128)(2,1)S(1)} %get-tuple-element.54.refs_10_.refs_11_) | copy-start | bytes 14155780
  169.5 71.2 %collective-permute-start.10 = (bf16[24,768,128]{2,1,0:T(8,128)(2,1)S(1)}, bf16[24,768,128]{2,1,0:T(8,128)(2,1)}, u32[]{:S(2)}, u32[]{:S(2)}) collective-permute-start(bf16[24,768,128]{2,1,0:T(8,128)(2,1)S(1)} %get-tuple-element.54.refs_10_.refs_11_), channel_id=1, source_target_pairs={{0,1},{1,0},{2,3},{3,2},{4,5},{5,4},{6,7},{7,6}} | collective-permute-start | bytes 14155784 | tf_op jit(solution)/shard_map/ppermute | solution.py:629
  169.5 30.7 %collective-permute-start.6 = (bf16[384,1536]{1,0:T(8,128)(2,1)S(1)}, bf16[384,1536]{1,0:T(8,128)(2,1)S(1)}, u32[]{:S(2)}, u32[]{:S(2)}) collective-permute-start(bf16[384,1536]{1,0:T(8,128)(2,1)S(1)} %mlp.3.refs_0_), channel_id=1, source_target_pairs={{0,2},{1,3},{4,6},{5,7}} | collective-permute-start | bytes 3538952 | tf_op jit(solution)/shard_map/ppermute | solution.py:623
  170.8 54.2 %collective-permute-start.7 = (bf16[384,1536]{1,0:T(8,128)(2,1)S(1)}, bf16[384,1536]{1,0:T(8,128)(2,1)S(1)}, u32[]{:S(2)}, u32[]{:S(2)}) collective-permute-start(bf16[384,1536]{1,0:T(8,128)(2,1)S(1)} %mlp.4.refs_1_), channel_id=1, source_target_pairs={{0,2},{1,3},{4,6},{5,7}} | collective-permute-start | bytes 3538952 | tf_op jit(solution)/shard_map/ppermute | solution.py:626
  232.8 4.6 %collective-permute-start.9 = (bf16[24,384,128]{2,1,0:T(8,128)(2,1)S(1)}, bf16[24,384,128]{2,1,0:T(8,128)(2,1)S(1)}, u32[]{:S(2)}, u32[]{:S(2)}) collective-permute-start(bf16[24,384,128]{2,1,0:T(8,128)(2,1)S(1)} %kv.3.refs_2_.refs_3_), channel_id=1, source_target_pairs={{0,1},{1,0},{2,3},{3,2},{4,5},{5,4},{6,7},{7,6}} | collective-permute-start | bytes 7077896 | tf_op jit(solution)/shard_map/ppermute | solution.py:635
  232.8 7.9 %collective-permute-start.8 = (bf16[24,384,128]{2,1,0:T(8,128)(2,1)S(1)}, bf16[24,384,128]{2,1,0:T(8,128)(2,1)S(1)}, u32[]{:S(2)}, u32[]{:S(2)}) collective-permute-start(bf16[24,384,128]{2,1,0:T(8,128)(2,1)S(1)} %kv.2.refs_0_.refs_1_), channel_id=1, source_target_pairs={{0,1},{1,0},{2,3},{3,2},{4,5},{5,4},{6,7},{7,6}} | collective-permute-start | bytes 7077896 | tf_op jit(solution)/shard_map/ppermute | solution.py:632
  277.9 1.3 copy-start.4

commit v4 on v3

--- a/solution.py
+++ b/solution.py
@@ -102,7 +102,7 @@
             full_spec((tokens, LANES)),
         ),
         out_shape=out_shape,
-        compiler_params=params(("arbitrary",), 40),
+        compiler_params=params(("arbitrary",), 52),
         cost_estimate=cost(2 * tokens * dim * (inner + tile), 16e6),
         name="in_proj",
     )(x_rows, gains, w_in_t, head_pad)
@@ -123,7 +123,7 @@
         in_specs=[full_spec((tokens, dim)), pl.BlockSpec((tile, dim), lambda i: (i + first, 0))],
         out_specs=pl.BlockSpec((tokens, tile), lambda i: (0, i)),
         out_shape=jax.ShapeDtypeStruct((tokens, inner), F32),
-        compiler_params=params(("arbitrary",), 60),
+        compiler_params=params(("arbitrary",), 56),
         cost_estimate=cost(2 * tokens * dim * inner, 21e6),
         name="z_proj",
     )(hid, w_in_t)
@@ -197,7 +197,7 @@
         out_specs=(full_spec((LANES, inner)), full_spec((1, inner))),
         out_shape=(jax.ShapeDtypeStruct((LANES, inner), F32), jax.ShapeDtypeStruct((1, inner), F32)),
         scratch_shapes=[pltpu.VMEM((256, inner), BF16), pltpu.VMEM((STEP + 16, inner), F32), pltpu.VMEM((STEP, inner), BF16)],
-        compiler_params=params(("arbitrary",), 40),
+        compiler_params=params(("arbitrary",), 52),
         cost_estimate=cost(2 * tokens * 256 * inner, 8e6),
         name="ssd_state",
     )(scalars, xs, bc, dt, cum, seg_wide)
@@ -207,8 +207,11 @@
                     skip_ref, state_ref, y_ref, e_ref, xp_ref, xw_ref, turn_ref, pack_ref):
     @pl.when(pl.program_id(0) == 0)
     def _():
-        odd = sc_ref[N_SRC + 10] == 1
-        decay = jnp.where(odd, jnp.where(sc_ref[N_SRC + 11] == 1, pdecay_ref[...], 0.0), 1.0)
+        odd = sc_ref[N_SRC + 7] == 1
+        starts_there = jnp.int32(0)
+        for k in range(N_SRC):
+            starts_there += (sc_ref[N_SRC + k] == sc_ref[2]).astype(jnp.int32)
+        decay = jnp.where(odd, jnp.where(starts_there == 0, pdecay_ref[...], 0.0), 1.0)
         half = got_ref.shape[0]
         for k, same, turned in ((0, got_ref, other_ref), (1, other_ref, got_ref)):
             rows = slice(k * half, (k + 1) * half)
@@ -452,7 +455,7 @@
 
 def attn_kernel(sc_ref, q_ref, seg_ref, *refs):
     far_refs, near_refs = refs[:8], refs[8:12]
-    o_ref, m_ref, l_ref, acc_ref, bias_ref = refs[12:]
+    o_ref, m_ref, l_ref, acc_ref = refs[12:]
     j = pl.program_id(1)
     heads, _, head_dim = q_ref.shape
     every = range(heads)
@@ -475,14 +478,15 @@
     rows = pl.ds(pl.multiple_of(j * BLOCK, BLOCK), BLOCK)
     col_id = lax.broadcasted_iota(jnp.int32, (BLOCK, BLOCK), 1)
     row_id = lax.broadcasted_iota(jnp.int32, (BLOCK, BLOCK), 0)
-    bias_ref[...] = jnp.where((col_id + q0 >= lanes(start, BLOCK)) & (col_id <= row_id), 0.0, NEG)
+    bias = jnp.where((col_id + q0 >= lanes(start, BLOCK)) & (col_id <= row_id), 0.0, NEG)
+    scored = [weights(h, k_ref, rows, bias) for h in every]
+    tops = [jnp.broadcast_to(top, (BLOCK, LANES)) for _, top in scored]
+    p = [jnp.exp2((scored[h][0] - lanes(tops[h], BLOCK)) * scale) for h in every]
+    acc = [dot(p[h].astype(BF16), v_ref[h, rows, :]) for h in every]
     for h in every:
-        s, top = weights(h, k_ref, rows, bias_ref[...])
-        m_new = jnp.broadcast_to(top, (BLOCK, LANES))
-        p = jnp.exp2((s - lanes(m_new, BLOCK)) * scale)
-        m_ref[h] = m_new
-        l_ref[h] = fold(p)
-        acc_ref[h] = dot(p.astype(BF16), v_ref[h, rows, :])
+        m_ref[h] = tops[h]
+        l_ref[h] = fold(p[h])
+        acc_ref[h] = acc[h]
 
     def update(k_ref, v_ref, rows, width, first_col):
         col = lax.broadcasted_iota(jnp.int32, (BLOCK, width), 1) + first_col
@@ -547,7 +551,7 @@
             in_specs=in_specs,
             out_specs=pl.BlockSpec((BLOCK, per * head_dim), lambda h, j, sc: (j, h)),
             scratch_shapes=[pltpu.VMEM((per, BLOCK, LANES), F32)] * 2
-            + [pltpu.VMEM((per, BLOCK, head_dim), F32), pltpu.VMEM((BLOCK, BLOCK), F32)],
+            + [pltpu.VMEM((per, BLOCK, head_dim), F32)],
         ),
         out_shape=jax.ShapeDtypeStruct((tokens, n_heads * head_dim), BF16),
         compiler_params=params(("arbitrary", "arbitrary"), 40),
@@ -560,6 +564,7 @@
     n_dev = mesh.shape['sp']
     swap_perm = [(d, d ^ 1) for d in range(n_dev)]
     cross_perm = [(d, d + 2) for d in range(n_dev - 2)]
+    turned_perm = [(d, (d ^ 1) + 2) for d in range(n_dev - 2)]
     row_spec = P(('dp', 'sp'), None)
     tok_spec = P(('dp', 'sp'))
     replicated = P()
@@ -573,20 +578,24 @@
 
         odd = (dev % 2) == 1
         counts = jnp.sum((seg_ids[None, :] <= jnp.arange(4, dtype=jnp.int32)[:, None]).astype(jnp.int32), axis=1)
-        ends = jnp.stack([seg_ids[0], seg_ids[tokens - 1]])
         seg_wide = jnp.broadcast_to(seg_ids[:, None], (tokens, LANES))
         head_pad = jnp.pad(ssm_head, ((0, 5), (0, LANES - n_heads)))
         w_in_t = w_in.T
         hid, xs, bc, dt, cum = in_proj(x_rows, norm_gains, w_in_t, head_pad, inner, n_heads)
+        counts, cum = lax.optimization_barrier((counts, cum))
+        got_counts = []
+        for perm in (swap_perm, cross_perm, turned_perm):
+            got_counts.append(lax.ppermute(counts, 'sp', perm))
+        pair_counts, *far_counts = got_counts
         local = jnp.pad(jnp.where(counts > 0, counts + 1, 0), (N_SRC, 8))
         local = jnp.where(jnp.arange(16) == N_SRC - 1, 1, local)
         state_end, decay = ssd_state(local, xs, bc, dt, cum, seg_wide)
 
         pair_state = lax.ppermute(state_end, 'sp', swap_perm)
         pair_decay = lax.ppermute(decay, 'sp', swap_perm)
-        info, decay = lax.optimization_barrier((jnp.concatenate([counts, ends, ends]), decay))
-        pair_info = lax.ppermute(info, 'sp', swap_perm)
-        joins = jnp.where(odd, seg_ids[0] == pair_info[5], pair_info[4] == seg_ids[tokens - 1])
+        even_counts = jnp.where(odd, pair_counts, counts)
+        odd_counts = jnp.where(odd, counts, pair_counts)
+        joins = jnp.sum((even_counts < tokens).astype(jnp.int32) - (odd_counts == 0).astype(jnp.int32)) == 0
         half = state_end.shape[0] // 2
         first = jnp.where(odd, half, 0)
         own_half = lax.dynamic_slice_in_dim(state_end, first, half, 0)
@@ -595,9 +604,6 @@
         mine = odd_decay * jnp.where(odd, pair_half, own_half) + jnp.where(odd, own_half, pair_half)
         mine, hid = lax.optimization_barrier((mine, hid))
         got = lax.ppermute(mine, 'sp', cross_perm)
-        slot8 = jnp.arange(8, dtype=jnp.int32)
-        chip_info = jnp.where(slot8 < 4, info + pair_info, jnp.where(odd, info, pair_info))
-        far_info = lax.ppermute(chip_info, 'sp', cross_perm)
         z = z_proj(hid, w_in_t, inner)
         pos = (dev * tokens + jnp.arange(tokens)).astype(F32)
         cos, sin = rope_tables(pos, head_dim)
@@ -608,14 +614,13 @@
         first_pos = dev * tokens
         far = jnp.int32(1 << 24)
         pair_pos = (dev ^ 1) * tokens
-        doc_starts = counts + jnp.where(odd, pair_info[:4], 0) + far_info[:4]
+        doc_starts = counts + jnp.where(odd, pair_counts, 0) + far_counts[0] + far_counts[1]
         slot = jnp.arange(4, dtype=jnp.int32)
         bases = jnp.where(slot == 3, first_pos, pair_pos)
         bases = jnp.where(slot >= 2, bases, jnp.where(dev >= 2, jnp.where(slot == 0, first_pos, pair_pos) - 2 * tokens, far))
-        edge_seg = jnp.pad(seg_ids[::BLOCK], (0, 8 - tokens // BLOCK))
-        edge_seg = jnp.where(jnp.arange(8) == 6, odd.astype(jnp.int32), edge_seg)
-        edge_seg = jnp.where(jnp.arange(8) == 7, (pair_info[4] == far_info[5]).astype(jnp.int32), edge_seg)
-        scalars = jnp.concatenate([bases, doc_starts, edge_seg])
+        edge_seg = jnp.pad(seg_ids[::BLOCK], (0, 4 - tokens // BLOCK))
+        edge_seg = jnp.where(slot == 3, odd.astype(jnp.int32), edge_seg)
+        scalars = jnp.concatenate([bases, doc_starts, edge_seg, jnp.zeros_like(slot)])
 
         gated = ssd_full(scalars, xs, bc, dt, cum, seg_wide, z, got, other, pair_state, pair_decay, head_pad, y_gain[None, :])
         x_one = proj_add(gated, w_out, [x_rows])

time: 338 us -> 332 us (0.982)
  local copies, waits for them, and re-layouts: 10.3 us -> 2.98 us
  transfers between devices with their start and end apart: 11 -> 12, of which waited for: 6 -> 8; matrix products, arithmetic and copies ran while one was open for 3% -> 1% of each run, Pallas kernels for 8% -> 8%
where the time goes in v4:
time: 332 us
  Pallas kernels  246 us (74%)
  waiting for transfers between devices  66.2 us (20%)
  starting transfers between devices  7.83 us (2%)
  other arithmetic  7.73 us (2%)
    pallas_call x3, Pallas kernels, mlp(): pl.pallas_call(functools.partial(mlp_kernel, layer), grid=(n_ff,), in_spe...  108 us
    pallas_call x1, Pallas kernels, attention(): pl.pallas_call(attn_kernel, grid_spec=pltpu.PrefetchScalarGridSpec(num_sc...  35.2 us
    pallas_call x3, Pallas kernels, qkv_proj(): pl.pallas_call(functools.partial(qkv_kernel, n_q, n_rot, len(parts)), gri...  32.3 us
    ppermute x1, waiting for transfers between devices, layers(): far_a = lax.ppermute(x_a, 'sp', cross_perm)  28.1 us
    pallas_call x1, Pallas kernels, ssd_full(): pl.pallas_call(ssd_full_kernel, grid=(tokens // STEP,), in_specs=[SMEM_SP...  19.2 us
    ppermute x1, waiting for transfers between devices, layers(): far_b = lax.ppermute(x_b, 'sp', cross_perm)  16.9 us
    pallas_call x2, Pallas kernels, proj_add(): pl.pallas_call(proj_add_kernel, grid=(dim // tile,), in_specs=[full_spec(...  15.8 us
    pallas_call x1, Pallas kernels, in_proj(): pl.pallas_call(functools.partial(in_proj_kernel, n_heads), grid=(n_x + 1,...  14.1 us
  transfers between devices with their start and end apart: 12, of which 8 were waited for; matrix products, arithmetic and copies ran while one was open for 1% of the time, Pallas kernels for 8%

profile of v4, /device:TPU:2, one launch (start us, length us, event | category | flops | bytes accessed | tf_op | source)
XLA Modules:
  0.0 331.5 jit_solution(9020713057597894741)
XLA Ops:
  0.0 0.8 convert_reduce_fusion
  0.8 0.7 pad.12.head_ref
  1.5 0.7 copy-done.3
  2.2 14.1 %in_proj.1 = (bf16[768,1536]{1,0:T(8,128)(2,1)}, bf16[768,3072]{1,0:T(8,128)(2,1)}, bf16[768,256]{1,0:T(8,128)(2,1)S(1)}, f32[768,128]{1,0:T(8,128)S(1)}, f32[768,128]{1,0:T(8,128)S(1)}) custom-call(bf16[768,1536]{1,0:T(8,128)(2,1)} %refs_0_.1, f32[4,1536]{1,0:T(4,128)S(1)} %copy-done.3, bf16[6448,1536]{1,0:T(8,128)(2,1)} %bitcast.9, f32[8,128]{1,0:T(8,128)S(1)} %pad.12.head_ref), custom_call_target="tpu_custom_call" | custom-call | flops 9663676416 | bytes 16000000 | tf_op jit(solution)/shard_map/in_proj/pallas_call | solution.py:88
  16.3 1.3 collective-permute-start.2
  17.6 1.3 collective-permute-start.1
  18.9 0.0 collective-permute-start
  18.9 2.2 collective-permute-done.2
  21.2 1.9 collective-permute-done.1
  23.1 0.0 collective-permute-done
  23.1 0.7 fusion.7
  23.8 0.1 compare_select_fusion.1.sc_ref
  23.9 0.0 copy-done.10
  23.9 0.2 broadcast_in_dim.49.seg_ref
  24.0 8.7 %ssd_state.1 = (f32[128,3072]{1,0:T(8,128)}, f32[1,3072]{1,0:T(1,128)S(1)}) custom-call(s32[16]{0:T(128)S(1)} %compare_select_fusion.1.sc_ref, bf16[768,3072]{1,0:T(8,128)(2,1)} %get-tuple-element.32.x_ref, bf16[768,256]{1,0:T(8,128)(2,1)S(1)} %get-tuple-element.33.bc_ref, f32[768,128]{1,0:T(8,128)S(1)} %get-tuple-element.34.dt_ref, ...), custom_call_target="tpu_custom_call" | custom-call | flops 1207959552 | bytes 8000000 | tf_op jit(solution)/shard_map/ssd_state/pallas_call | solution.py:193
  32.7 0.0 collective-permute-start.4
  32.8 3.9 %fusion.1 = (f32[768,64]{1,0:T(8,128)S(1)}, f32[768,64]{1,0:T(8,128)S(1)}, f32[768,64]{1,0:T(8,128)S(1)}, f32[768,64]{1,0:T(8,128)}, f32[768,64]{1,0:T(8,128)}, /*index=5*/f32[768,64]{1,0:T(8,128)}) fusion(f32[64]{0:T(128)S(1)} %multiply_power_fusion, f32[768]{0:T(1024)S(1)} %broadcast_add_fusion, f32[768]{0:T(1024)S(1)} %add_convert_fusion), kind=kLoop, calls=%fused_computation.10 | loop fusion | flops 196608 | bytes 1186048 | tf_op jit(solution)/shard_map/neg | solution.py:380
  36.7 0.5 collective-permute-start.3
  37.2 0.3 pad_maximum_fusion.2
  38.1 0.0 copy-start.7
  38.1 0.0 copy-start.8
  38.2 0.0 copy-start.9
  38.2 0.0 collective-permute-done.3.pdecay_ref
  38.2 0.0 collective-permute-done.4.pair_ref
  38.2 1.6 select_add_fusion
  39.8 1.5 collective-permute-start.5
  41.3 0.0 copy-done.7
  41.3 0.0 copy-done.8
  41.3 0.0 copy-done.9
  41.3 0.3 pad_maximum_fusion
  41.6 0.0 copy-start.6
  41.6 12.7 %z_proj.1.z_ref = f32[768,3072]{1,0:T(8,128)} custom-call(bf16[768,1536]{1,0:T(8,128)(2,1)} %get-tuple-element.40.h_ref, bf16[6448,1536]{1,0:T(8,128)(2,1)} %bitcast.10), custom_call_target="tpu_custom_call" | custom-call | flops 7247757312 | bytes 21000000 | tf_op jit(solution)/shard_map/z_proj/pallas_call | solution.py:120
  54.2 7.2 %collective-permute-done.5.got_ref = f32[64,3072]{1,0:T(8,128)} collective-permute-done((f32[64,3072]{1,0:T(8,128)S(1)}, f32[64,3072]{1,0:T(8,128)}, u32[]{:S(2)}, u32[]{:S(2)}) %collective-permute-start.5) | collective-permute-done | bytes 786464 | tf_op jit(solution)/shard_map/ppermute | solution.py:606
  61.4 0.0 collective-permute-start.6
  61.4 0.1 slice.3
  61.5 0.1 pad_add_fusion.sc_ref
  61.6 2.4 collective-permute-done.6.other_ref
  64.1 0.0 copy-done.6
  64.1 19.2 %ssd_full.1.a_ref = bf16[768,3072]{1,0:T(8,128)(2,1)S(1)} custom-call(s32[16]{0:T(128)S(1)} %pad_add_fusion.sc_ref, bf16[768,3072]{1,0:T(8,128)(2,1)} %get-tuple-element.32.x_ref, bf16[768,256]{1,0:T(8,128)(2,1)S(1)} %get-tuple-element.33.bc_ref, f32[768,128]{1,0:T(8,128)S(1)} %get-tuple-element.34.dt_ref, f32[768,128]{1,0:T(8,128)S(1)} %get-tuple-element.35.cum_ref, ...), custom_call_target="tpu_custom_call" | custom-call | flops 12000000000 | bytes 20000000 | tf_op jit(solution)/shard_map/ssd_full/pallas_call | solution.py:287
  83.2 0.0 copy-done.5
  83.3 0.0 copy-start.4
  83.3 10.0 %proj_add.2.x_ref = bf16[768,1536]{1,0:T(8,128)(2,1)S(1)} custom-call(bf16[768,3072]{1,0:T(8,128)(2,1)S(1)} %ssd_full.1.a_ref, bf16[3072,1536]{1,0:T(8,128)(2,1)} %w_ref.1, bf16[768,1536]{1,0:T(8,128)(2,1)S(1)} %copy-done.5), custom_call_target="tpu_custom_call" | custom-call | flops 7247757312 | bytes 18874368 | tf_op jit(solution)/shard_map/proj_add/pallas_call | solution.py:319
  93.2 0.0 copy-done.4
  93.3 27.8 %mlp.3.refs_0_ = bf16[384,1536]{1,0:T(8,128)(2,1)S(1)} custom-call(bf16[768,1536]{1,0:T(8,128)(2,1)S(1)} %proj_add.2.x_ref, f32[4,1536]{1,0:T(4,128)S(1)} %copy-done.4, bf16[2,1536,12288]{2,1,0:T(8,128)(2,1)} %wu_ref.5, bf16[2,1536,12288]{2,1,0:T(8,128)(2,1)} %wu_ref.5, bf16[2,6144,1536]{2,1,0:T(8,128)(2,1)} %wd_ref.5), custom_call_target="tpu_custom_call" | custom-call | flops 21743271936 | bytes 56623104 | tf_op jit(solution)/shard_map/mlp/pallas_call | solution.py:356
  121.1 28.0 %mlp.4.refs_1_ = bf16[384,1536]{1,0:T(8,128)(2,1)S(1)} custom-call(bf16[768,1536]{1,0:T(8,128)(2,1)S(1)} %proj_add.2.x_ref, f32[4,1536]{1,0:T(4,128)S(1)} %copy-done.4, bf16[2,1536,12288]{2,1,0:T(8,128)(2,1)} %wu_ref.5, bf16[2,1536,12288]{2,1,0:T(8,128)(2,1)} %wu_ref.5, bf16[2,6144,1536]{2,1,0:T(8,128)(2,1)} %wd_ref.5), custom_call_target="tpu_custom_call" | custom-call | flops 21743271936 | bytes 56623104 | tf_op jit(solution)/shard_map/mlp/pallas_call | solution.py:356
  149.1 0.0 copy-start.1
  149.1 16.8 %qkv.1 = (bf16[12,768,128]{2,1,0:T(8,128)(2,1)S(1)}, bf16[24,768,128]{2,1,0:T(8,128)(2,1)S(1)}) custom-call(bf16[384,1536]{1,0:T(8,128)(2,1)S(1)} %mlp.3.refs_0_, bf16[384,1536]{1,0:T(8,128)(2,1)S(1)} %mlp.4.refs_1_, f32[4,1536]{1,0:T(4,128)S(1)} %copy-done.4, f32[768,128]{1,0:T(8,128)S(1)} %get-tuple-element.45.refs_3_, ...), custom_call_target="tpu_custom_call" | custom-call | flops 10871635968 | bytes 22155776 | tf_op jit(solution)/shard_map/qkv/pallas_call | solution.py:428
  166.0 0.2 collective-permute-start.11
  166.2 1.3 collective-permute-start.7
  167.5 1.3 collective-permute-start.8
  168.8 28.1 %collective-permute-done.7.refs_0_ = bf16[384,1536]{1,0:T(8,128)(2,1)S(1)} collective-permute-done((bf16[384,1536]{1,0:T(8,128)(2,1)S(1)}, bf16[384,1536]{1,0:T(8,128)(2,1)S(1)}, u32[]{:S(2)}, u32[]{:S(2)}) %collective-permute-start.7) | collective-permute-done | bytes 1179680 | tf_op jit(solution)/shard_map/ppermute | solution.py:628
  196.9 7.7 %kv.2.refs_0_.refs_1_ = bf16[24,384,128]{2,1,0:T(8,128)(2,1)S(1)} custom-call(bf16[384,1536]{1,0:T(8,128)(2,1)S(1)} %collective-permute-done.7.refs_0_, f32[4,1536]{1,0:T(4,128)S(1)} %copy-done.4, f32[768,128]{1,0:T(8,128)S(1)} %get-tuple-element.50.refs_2_, f32[768,128]{1,0:T(8,128)S(1)} %get-tuple-element.51.refs_3_, bf16[36,1536,128]{2,1,0:T(8,128)(2,1)} %bitcast.7), custom_call_target="tpu_custom_call" | custom-call | flops 3623878656 | bytes 17437184 | tf_op jit(solution)/shard_map/kv/pallas_call | solution.py:428
  204.6 16.9 %collective-permute-done.8.refs_0_ = bf16[384,1536]{1,0:T(8,128)(2,1)S(1)} collective-permute-done((bf16[384,1536]{1,0:T(8,128)(2,1)S(1)}, bf16[384,1536]{1,0:T(8,128)(2,1)S(1)}, u32[]{:S(2)}, u32[]{:S(2)}) %collective-permute-start.8) | collective-permute-done | bytes 1179680 | tf_op jit(solution)/shard_map/ppermute | solution.py:631
  221.6 7.7 %kv.3.refs_2_.refs_3_ = bf16[24,384,128]{2,1,0:T(8,128)(2,1)S(1)} custom-call(bf16[384,1536]{1,0:T(8,128)(2,1)S(1)} %collective-permute-done.8.refs_0_, f32[4,1536]{1,0:T(4,128)S(1)} %copy-done.4, f32[768,128]{1,0:T(8,128)S(1)} %get-tuple-element.50.refs_2_, f32[768,128]{1,0:T(8,128)S(1)} %get-tuple-element.51.refs_3_, bf16[36,1536,128]{2,1,0:T(8,128)(2,1)} %bitcast.8), custom_call_target="tpu_custom_call" | custom-call | flops 3623878656 | bytes 17437184 | tf_op jit(solution)/shard_map/kv/pallas_call | solution.py:428
  229.3 0.0 collective-permute-start.10
  229.3 0.5 collective-permute-start.9
  229.8 4.0 %collective-permute-done.10.refs_6_.refs_7_ = bf16[24,384,128]{2,1,0:T(8,128)(2,1)S(1)} collective-permute-done((bf16[24,384,128]{2,1,0:T(8,128)(2,1)S(1)}, bf16[24,384,128]{2,1,0:T(8,128)(2,1)S(1)}, u32[]{:S(2)}, u32[]{:S(2)}) %collective-permute-start.10) | collective-permute-done | bytes 2359328 | tf_op jit(solution)/shard_map/ppermute | solution.py:640
  233.8 3.4 %collective-permute-done.9.refs_4_.refs_5_ = bf16[24,384,128]{2,1,0:T(8,128)(2,1)S(1)} collective-permute-done((bf16[24,384,128]{2,1,0:T(8,128)(2,1)S(1)}, bf16[24,384,128]{2,1,0:T(8,128)(2,1)S(1)}, u32[]{:S(2)}, u32[]{:S(2)}) %collective-permute-start.9) | collective-permute-done | bytes 2359328 | tf_op jit(solution)/shard_map/ppermute | solution.py:637
  237.2 0.0 collective-permute-done.11.refs_8_.refs_9_
  237.2 35.2 %attention.1.a_ref = bf16[768,1536]{1,0:T(8,128)(2,1)S(1)} custom-call(s32[16]{0:T(128)S(1)} %pad_add_fusion.sc_ref, bf16[12,768,128]{2,1,0:T(8,128)(2,1)S(1)} %get-tuple-element.48.q_ref, s32[768,128]{1,0:T(8,128)S(1)} %broadcast_in_dim.49.seg_ref, bf16[24,384,128]{2,1,0:T(8,128)(2,1)S(1)} %kv.2.refs_0_.refs_1_, ...), custom_call_target="tpu_custom_call" | custom-call | flops 7247757312 | bytes 20000000 | tf_op jit(solution)/shard_map/attention/pallas_call | solution.py:546
  272.4 0.0 copy-start.2
  272.4 1.3 copy-done.2
  273.7 5.8 %proj_add.3.x_ref = bf16[768,1536]{1,0:T(8,128)(2,1)S(1)} custom-call(bf16[768,1536]{1,0:T(8,128)(2,1)S(1)} %attention.1.a_ref, bf16[1536,1536]{1,0:T(8,128)(2,1)} %bitcast.12, bf16[384,1536]{1,0:T(8,128)(2,1)S(1)} %mlp.3.refs_0_, bf16[384,1536]{1,0:T(8,128)(2,1)S(1)} %copy-done.2), custom_call_target="tpu_custom_call" | custom-call | flops 3623878656 | bytes 11796480 | tf_op jit(solution)/shard_map/proj_add/pallas_call | solution.py:319
  279.5 52.0 %mlp.5 = bf16[768,1536]{1,0:T(8,128)(2,1)} custom-call(bf16[768,1536]{1,0:T(8,128)(2,1)S(1)} %proj_add.3.x_ref, f32[4,1536]{1,0:T(4,128)S(1)} %copy-done.4, bf16[2,1536,12288]{2,1,0:T(8,128)(2,1)} %wu_ref.5, bf16[2,1536,12288]{2,1,0:T(8,128)(2,1)} %wu_ref.5, bf16[2,6144,1536]{2,1,0:T(8,128)(2,1)} %wd_ref.5), custom_call_target="tpu_custom_call" | custom-call | flops 43486543872 | bytes 56623104 | tf_op jit(solution)/shard_map/mlp/pallas_call | solution.py:356
  (12 shorter events, 0.1 us)
Async XLA Ops:
  1.5 0.7 copy-start.3
  2.2 21.6 %copy-start.10 = (s32[768]{0:T(1024)S(1)}, s32[768]{0:T(1024)}, u32[]{:S(2)}) copy-start(s32[768]{0:T(1024)} %param.12) | copy-start | bytes 9220
  16.3 4.9 %collective-permute-start.2 = (s32[4]{0:T(128)S(1)}, s32[4]{0:T(128)S(1)}, u32[]{:S(2)}, u32[]{:S(2)}) collective-permute-start(s32[4]{0:T(128)S(1)} %convert_reduce_fusion), channel_id=1, source_target_pairs={{0,3},{1,2},{4,7},{5,6}} | collective-permute-start | bytes 56 | tf_op jit(solution)/shard_map/ppermute | solution.py:588
  17.6 5.5 %collective-permute-start.1 = (s32[4]{0:T(128)S(1)}, s32[4]{0:T(128)S(1)}, u32[]{:S(2)}, u32[]{:S(2)}) collective-permute-start(s32[4]{0:T(128)S(1)} %convert_reduce_fusion), channel_id=1, source_target_pairs={{0,2},{1,3},{4,6},{5,7}} | collective-permute-start | bytes 56 | tf_op jit(solution)/shard_map/ppermute | solution.py:588
  18.9 4.2 %collective-permute-start = (s32[4]{0:T(128)S(1)}, s32[4]{0:T(128)S(1)}, u32[]{:S(2)}, u32[]{:S(2)}) collective-permute-start(s32[4]{0:T(128)S(1)} %convert_reduce_fusion), channel_id=1, source_target_pairs={{0,1},{1,0},{2,3},{3,2},{4,5},{5,4},{6,7},{7,6}} | collective-permute-start | bytes 56 | tf_op jit(solution)/shard_map/ppermute | solution.py:588
  32.7 5.5 %collective-permute-start.4 = (f32[128,3072]{1,0:T(8,128)}, f32[128,3072]{1,0:T(8,128)}, u32[]{:S(2)}, u32[]{:S(2)}) collective-permute-start(f32[128,3072]{1,0:T(8,128)} %get-tuple-element.37), channel_id=1, source_target_pairs={{0,1},{1,0},{2,3},{3,2},{4,5},{5,4},{6,7},{7,6}} | collective-permute-start | bytes 4718600 | tf_op jit(solution)/shard_map/ppermute | solution.py:594
  36.7 1.5 collective-permute-start.3
  38.1 3.1 copy-start.7
  38.1 3.1 copy-start.8
  38.2 3.1 copy-start.9
  39.8 21.6 %collective-permute-start.5 = (f32[64,3072]{1,0:T(8,128)S(1)}, f32[64,3072]{1,0:T(8,128)}, u32[]{:S(2)}, u32[]{:S(2)}) collective-permute-start(f32[64,3072]{1,0:T(8,128)S(1)} %select_add_fusion), channel_id=1, source_target_pairs={{0,2},{1,3},{4,6},{5,7}} | collective-permute-start | bytes 2359304 | tf_op jit(solution)/shard_map/ppermute | solution.py:606
  41.6 22.5 %copy-start.6 = (f32[3072]{0:T(1024)S(1)}, f32[3072]{0:T(1024)}, u32[]{:S(2)}) copy-start(f32[3072]{0:T(1024)} %param.16) | copy-start | bytes 36868
  61.4 2.6 collective-permute-start.6
  64.1 19.2 %copy-start.5 = (bf16[768,1536]{1,0:T(8,128)(2,1)S(1)}, bf16[768,1536]{1,0:T(8,128)(2,1)}, u32[]{:S(2)}) copy-start(bf16[768,1536]{1,0:T(8,128)(2,1)} %refs_0_.1) | copy-start | bytes 7077892
  83.3 10.0 %copy-start.4 = (f32[4,1536]{1,0:T(4,128)S(1)}, f32[4,1536]{1,0:T(4,128)}, u32[]{:S(2)}) copy-start(f32[4,1536]{1,0:T(4,128)} %gain_ref.7) | copy-start | bytes 73732
  149.1 18.3 %copy-start.1 = (bf16[384,1536]{1,0:T(8,128)(2,1)}, bf16[384,1536]{1,0:T(8,128)(2,1)S(1)}, u32[]{:S(2)}) copy-start(bf16[384,1536]{1,0:T(8,128)(2,1)S(1)} %mlp.4.refs_1_) | copy-start | bytes 3538948
  166.0 38.6 %copy-start = (bf16[24,768,128]{2,1,0:T(8,128)(2,1)}, bf16[24,768,128]{2,1,0:T(8,128)(2,1)S(1)}, u32[]{:S(2)}) copy-start(bf16[24,768,128]{2,1,0:T(8,128)(2,1)S(1)} %get-tuple-element.54.refs_10_.refs_11_) | copy-start | bytes 14155780
  166.0 71.2 %collective-permute-start.11 = (bf16[24,768,128]{2,1,0:T(8,128)(2,1)S(1)}, bf16[24,768,128]{2,1,0:T(8,128)(2,1)}, u32[]{:S(2)}, u32[]{:S(2)}) collective-permute-start(bf16[24,768,128]{2,1,0:T(8,128)(2,1)S(1)} %get-tuple-element.54.refs_10_.refs_11_), channel_id=1, source_target_pairs={{0,1},{1,0},{2,3},{3,2},{4,5},{5,4},{6,7},{7,6}} | collective-permute-start | bytes 14155784 | tf_op jit(solution)/shard_map/ppermute | solution.py:634
  166.2 30.7 %collective-permute-start.7 = (bf16[384,1536]{1,0:T(8,128)(2,1)S(1)}, bf16[384,1536]{1,0:T(8,128)(2,1)S(1)}, u32[]{:S(2)}, u32[]{:S(2)}) collective-permute-start(bf16[384,1536]{1,0:T(8,128)(2,1)S(1)} %mlp.3.refs_0_), channel_id=1, source_target_pairs={{0,2},{1,3},{4,6},{5,7}} | collective-permute-start | bytes 3538952 | tf_op jit(solution)/shard_map/ppermute | solution.py:628
  167.5 54.1 %collective-permute-start.8 = (bf16[384,1536]{1,0:T(8,128)(2,1)S(1)}, bf16[384,1536]{1,0:T(8,128)(2,1)S(1)}, u32[]{:S(2)}, u32[]{:S(2)}) collective-permute-start(bf16[384,1536]{1,0:T(8,128)(2,1)S(1)} %mlp.4.refs_1_), channel_id=1, source_target_pairs={{0,2},{1,3},{4,6},{5,7}} | collective-permute-start | bytes 3538952 | tf_op jit(solution)/shard_map/ppermute | solution.py:631
  229.3 4.6 %collective-permute-start.10 = (bf16[24,384,128]{2,1,0:T(8,128)(2,1)S(1)}, bf16[24,384,128]{2,1,0:T(8,128)(2,1)S(1)}, u32[]{:S(2)}, u32[]{:S(2)}) collective-permute-start(bf16[24,384,128]{2,1,0:T(8,128)(2,1)S(1)} %kv.3.refs_2_.refs_3_), channel_id=1, source_target_pairs={{0,1},{1,0},{2,3},{3,2},{4,5},{5,4},{6,7},{7,6}} | collective-permute-start | bytes 7077896 | tf_op jit(solution)/shard_map/ppermute | solution.py:640
  229.3 7.9 %collective-permute-start.9 = (bf16[24,384,128]{2,1,0:T(8,128)(2,1)S(1)}, bf16[24,384,128]{2,1,0:T(8,128)(2,1)S(1)}, u32[]{:S(2)}, u32[]{:S(2)}) collective-permute-start(bf16[24,384,128]{2,1,0:T(8,128)(2,1)S(1)} %kv.2.refs_0_.refs_1_), channel_id=1, source_target_pairs={{0,1},{1,0},{2,3},{3,2},{4,5},{5,4},{6,7},{7,6}} | collective-permute-start | bytes 7077896 | tf_op jit(solution)/shard_map/ppermute | solution.py:637
  272.4 1.3 copy-start.2

commit v5 on v4

--- a/solution.py
+++ b/solution.py
@@ -366,7 +366,7 @@
         out_specs=full_spec((tokens, dim)),
         out_shape=jax.ShapeDtypeStruct((tokens, dim), BF16),
         scratch_shapes=[pltpu.VMEM((tokens, dim), BF16), pltpu.VMEM((tokens, dim), F32)],
-        compiler_params=params(("arbitrary",), 44),
+        compiler_params=params(("arbitrary",), 40),
         cost_estimate=cost(6 * tokens * dim * ff, 6 * dim * ff),
         name="mlp",
     )(x_rows, gains, mlp_up, mlp_up, mlp_down)
@@ -434,14 +434,14 @@
         out_specs=tuple(out_specs),
         out_shape=tuple(out_shape),
         scratch_shapes=[pltpu.VMEM((tokens, dim), BF16)],
-        compiler_params=params(("arbitrary",), 40),
+        compiler_params=params(("arbitrary",), 24),
         cost_estimate=cost(2 * tokens * dim * steps * per * head_dim, 2 * dim * steps * per * head_dim + 8e6),
         name="qkv" if with_q else "kv",
     )(*parts, gains, cos, sin, w_heads)
 
 
 BLOCK = 256
-HEAD_GROUP = 4
+HEAD_GROUP = 6
 N_SRC = 4
 NEG = -1e30
 
@@ -582,17 +582,15 @@
         head_pad = jnp.pad(ssm_head, ((0, 5), (0, LANES - n_heads)))
         w_in_t = w_in.T
         hid, xs, bc, dt, cum = in_proj(x_rows, norm_gains, w_in_t, head_pad, inner, n_heads)
-        counts, cum = lax.optimization_barrier((counts, cum))
-        got_counts = []
-        for perm in (swap_perm, cross_perm, turned_perm):
-            got_counts.append(lax.ppermute(counts, 'sp', perm))
-        pair_counts, *far_counts = got_counts
         local = jnp.pad(jnp.where(counts > 0, counts + 1, 0), (N_SRC, 8))
         local = jnp.where(jnp.arange(16) == N_SRC - 1, 1, local)
         state_end, decay = ssd_state(local, xs, bc, dt, cum, seg_wide)
 
         pair_state = lax.ppermute(state_end, 'sp', swap_perm)
         pair_decay = lax.ppermute(decay, 'sp', swap_perm)
+        counts, decay = lax.optimization_barrier((counts, decay))
+        pair_counts = lax.ppermute(counts, 'sp', swap_perm)
+        far_counts = [lax.ppermute(counts, 'sp', perm) for perm in (cross_perm, turned_perm)]
         even_counts = jnp.where(odd, pair_counts, counts)
         odd_counts = jnp.where(odd, counts, pair_counts)
         joins = jnp.sum((even_counts < tokens).astype(jnp.int32) - (odd_counts == 0).astype(jnp.int32)) == 0

time: 332 us -> 331 us (level); the launches traced: 332 us -> 326 us
  Pallas kernels: 246 us -> 237 us
  other arithmetic: 7.73 us -> 13 us
  waiting for transfers between devices: 66.2 us -> 62.2 us
    pallas_call x3, Pallas kernels: 32.3 us -> 25.9 us  [qkv_proj(): pl.pallas_call(functools.partial(qkv_kernel, n_q, n_rot, len(parts)), gri...]
    ppermute x3, waiting for transfers between devices: 4.12 us -> 0.01 us  [the longest x2 0.01 us: layers(): lax.ppermute(counts, 'sp', perm)]
  transfers between devices with their start and end apart: 12 -> 12, of which waited for: 8 -> 5; matrix products, arithmetic and copies ran while one was open for 1% -> 3% of each run, Pallas kernels for 8% -> 7%
where the time goes in v5:
time: 331 us; the launch traced here: 326 us
  Pallas kernels  237 us (72%)
  waiting for transfers between devices  62.2 us (19%)
  other arithmetic  13 us (4%)
  starting transfers between devices  8.35 us (3%)
  local copies, waits for them, and re-layouts  3.65 us (1%)
    pallas_call x3, Pallas kernels, mlp(): pl.pallas_call(functools.partial(mlp_kernel, layer), grid=(n_ff,), in_spe...  109 us
    pallas_call x1, Pallas kernels, attention(): pl.pallas_call(attn_kernel, grid_spec=pltpu.PrefetchScalarGridSpec(num_sc...  32.8 us
    ppermute x1, waiting for transfers between devices, layers(): far_a = lax.ppermute(x_a, 'sp', cross_perm)  28.1 us
    pallas_call x3, Pallas kernels, qkv_proj(): pl.pallas_call(functools.partial(qkv_kernel, n_q, n_rot, len(parts)), gri...  25.9 us
    ppermute x1, waiting for transfers between devices, layers(): far_b = lax.ppermute(x_b, 'sp', cross_perm)  18.7 us
    pallas_call x1, Pallas kernels, ssd_full(): pl.pallas_call(ssd_full_kernel, grid=(tokens // STEP,), in_specs=[SMEM_SP...  18.7 us
    pallas_call x2, Pallas kernels, proj_add(): pl.pallas_call(proj_add_kernel, grid=(dim // tile,), in_specs=[full_spec(...  15.8 us
    pallas_call x1, Pallas kernels, in_proj(): pl.pallas_call(functools.partial(in_proj_kernel, n_heads), grid=(n_x + 1,...  14.1 us
  transfers between devices with their start and end apart: 12, of which 5 were waited for; matrix products, arithmetic and copies ran while one was open for 3% of the time, Pallas kernels for 7%

profile of v5, /device:TPU:2, one launch (start us, length us, event | category | flops | bytes accessed | tf_op | source)
XLA Modules:
  0.0 326.0 jit_solution(7172583555830032224)
XLA Ops:
  0.0 1.4 convert_reduce_fusion
  1.4 0.7 compare_select_fusion
  2.1 0.1 compare_select_fusion.1.sc_ref
  2.1 0.7 pad.13.head_ref
  2.8 0.7 copy-done.6
  3.6 14.1 %in_proj.1 = (bf16[768,1536]{1,0:T(8,128)(2,1)}, bf16[768,3072]{1,0:T(8,128)(2,1)}, bf16[768,256]{1,0:T(8,128)(2,1)S(1)}, f32[768,128]{1,0:T(8,128)S(1)}, f32[768,128]{1,0:T(8,128)S(1)}) custom-call(bf16[768,1536]{1,0:T(8,128)(2,1)} %refs_0_.1, f32[4,1536]{1,0:T(4,128)S(1)} %copy-done.6, bf16[6448,1536]{1,0:T(8,128)(2,1)} %bitcast.11, f32[8,128]{1,0:T(8,128)S(1)} %pad.13.head_ref), custom_call_target="tpu_custom_call" | custom-call | flops 9663676416 | bytes 16000000 | tf_op jit(solution)/shard_map/in_proj/pallas_call | solution.py:88
  17.7 0.0 copy-done.17
  17.7 0.2 broadcast_in_dim.49.seg_ref
  17.8 8.7 %ssd_state.1 = (f32[128,3072]{1,0:T(8,128)}, f32[1,3072]{1,0:T(1,128)}) custom-call(s32[16]{0:T(128)S(1)} %compare_select_fusion.1.sc_ref, bf16[768,3072]{1,0:T(8,128)(2,1)} %get-tuple-element.30.x_ref, bf16[768,256]{1,0:T(8,128)(2,1)S(1)} %get-tuple-element.31.bc_ref, f32[768,128]{1,0:T(8,128)S(1)} %get-tuple-element.32.dt_ref, ...), custom_call_target="tpu_custom_call" | custom-call | flops 1207959552 | bytes 8000000 | tf_op jit(solution)/shard_map/ssd_state/pallas_call | solution.py:193
  26.6 1.3 collective-permute-start.2
  27.9 1.3 collective-permute-start.1
  29.2 0.0 collective-permute-start
  29.2 0.5 collective-permute-start.3
  29.7 0.0 collective-permute-start.4
  29.7 3.9 %fusion.1 = (f32[768,64]{1,0:T(8,128)S(1)}, f32[768,64]{1,0:T(8,128)S(1)}, f32[768,64]{1,0:T(8,128)S(1)}, f32[768,64]{1,0:T(8,128)}, f32[768,64]{1,0:T(8,128)}, /*index=5*/f32[768,64]{1,0:T(8,128)}) fusion(f32[64]{0:T(128)S(1)} %multiply_power_fusion, f32[768]{0:T(1024)S(1)} %broadcast_add_fusion, f32[768]{0:T(1024)S(1)} %add_convert_fusion), kind=kLoop, calls=%fused_computation.10 | loop fusion | flops 196608 | bytes 1186048 | tf_op jit(solution)/shard_map/neg | solution.py:380
  33.6 1.0 pad_maximum_fusion.2
  34.7 0.0 collective-permute-done.2
  34.7 0.0 collective-permute-done.1
  34.7 0.0 collective-permute-done
  34.7 2.0 fusion.7
  37.4 0.0 collective-permute-done.3.pdecay_ref
  37.4 0.0 collective-permute-done.4.pair_ref
  37.4 1.3 select_add_fusion
  38.8 1.6 collective-permute-start.5
  40.4 0.0 copy-done.14
  40.4 0.0 copy-done.15
  40.4 0.0 copy-done.16
  40.4 1.2 pad_maximum_fusion
  41.6 12.8 %z_proj.1.z_ref = f32[768,3072]{1,0:T(8,128)} custom-call(bf16[768,1536]{1,0:T(8,128)(2,1)} %get-tuple-element.40.h_ref, bf16[6448,1536]{1,0:T(8,128)(2,1)} %bitcast.12), custom_call_target="tpu_custom_call" | custom-call | flops 7247757312 | bytes 21000000 | tf_op jit(solution)/shard_map/z_proj/pallas_call | solution.py:120
  54.3 7.9 %collective-permute-done.5.got_ref = f32[64,3072]{1,0:T(8,128)} collective-permute-done((f32[64,3072]{1,0:T(8,128)S(1)}, f32[64,3072]{1,0:T(8,128)}, u32[]{:S(2)}, u32[]{:S(2)}) %collective-permute-start.5) | collective-permute-done | bytes 786464 | tf_op jit(solution)/shard_map/ppermute | solution.py:604
  62.2 0.1 collective-permute-start.6
  62.3 1.3 slice.3
  63.6 0.7 compare_select_fusion.3
  64.3 0.7 pad_add_fusion.sc_ref
  65.0 0.0 collective-permute-done.6.other_ref
  65.0 0.7 copy-done.13
  65.7 18.7 %ssd_full.1.a_ref = bf16[768,3072]{1,0:T(8,128)(2,1)S(1)} custom-call(s32[16]{0:T(128)S(1)} %pad_add_fusion.sc_ref, bf16[768,3072]{1,0:T(8,128)(2,1)} %get-tuple-element.30.x_ref, bf16[768,256]{1,0:T(8,128)(2,1)S(1)} %get-tuple-element.31.bc_ref, f32[768,128]{1,0:T(8,128)S(1)} %get-tuple-element.32.dt_ref, f32[768,128]{1,0:T(8,128)S(1)} %get-tuple-element.33.cum_ref, ...), custom_call_target="tpu_custom_call" | custom-call | flops 12000000000 | bytes 20000000 | tf_op jit(solution)/shard_map/ssd_full/pallas_call | solution.py:287
  84.4 0.0 copy-start.7
  84.4 10.0 %proj_add.2.x_ref = bf16[768,1536]{1,0:T(8,128)(2,1)S(1)} custom-call(bf16[768,3072]{1,0:T(8,128)(2,1)S(1)} %ssd_full.1.a_ref, bf16[3072,1536]{1,0:T(8,128)(2,1)} %w_ref.1, bf16[768,1536]{1,0:T(8,128)(2,1)S(1)} %copy-done.12), custom_call_target="tpu_custom_call" | custom-call | flops 7247757312 | bytes 18874368 | tf_op jit(solution)/shard_map/proj_add/pallas_call | solution.py:319
  94.4 0.0 slice-start
  94.4 0.0 slice-start.1
  94.5 27.9 %mlp.3.refs_0_ = bf16[384,1536]{1,0:T(8,128)(2,1)S(1)} custom-call(bf16[768,1536]{1,0:T(8,128)(2,1)S(1)} %proj_add.2.x_ref, f32[4,1536]{1,0:T(4,128)S(1)} %copy-done.7, bf16[2,1536,12288]{2,1,0:T(8,128)(2,1)} %wu_ref.5, bf16[2,1536,12288]{2,1,0:T(8,128)(2,1)} %wu_ref.5, bf16[2,6144,1536]{2,1,0:T(8,128)(2,1)} %wd_ref.5), custom_call_target="tpu_custom_call" | custom-call | flops 21743271936 | bytes 56623104 | tf_op jit(solution)/shard_map/mlp/pallas_call | solution.py:356
  122.4 0.0 copy-start.2
  122.4 0.0 slice-start.2
  122.4 0.0 slice-start.3
  122.4 0.0 copy-start.8
  122.4 29.0 %mlp.4.refs_1_ = bf16[384,1536]{1,0:T(8,128)(2,1)S(1)} custom-call(bf16[768,1536]{1,0:T(8,128)(2,1)S(1)} %proj_add.2.x_ref, f32[4,1536]{1,0:T(4,128)S(1)} %copy-done.7, bf16[2,1536,12288]{2,1,0:T(8,128)(2,1)} %wu_ref.5, bf16[2,1536,12288]{2,1,0:T(8,128)(2,1)} %wu_ref.5, bf16[2,6144,1536]{2,1,0:T(8,128)(2,1)} %wd_ref.5), custom_call_target="tpu_custom_call" | custom-call | flops 21743271936 | bytes 56623104 | tf_op jit(solution)/shard_map/mlp/pallas_call | solution.py:356
  151.5 14.7 %qkv.1 = (bf16[12,768,128]{2,1,0:T(8,128)(2,1)S(1)}, bf16[24,768,128]{2,1,0:T(8,128)(2,1)S(1)}) custom-call(bf16[384,1536]{1,0:T(8,128)(2,1)S(1)} %mlp.3.refs_0_, bf16[384,1536]{1,0:T(8,128)(2,1)S(1)} %mlp.4.refs_1_, f32[4,1536]{1,0:T(4,128)S(1)} %copy-done.7, f32[768,128]{1,0:T(8,128)S(1)} %copy-done.8, f32[768,128]{1,0:T(8,128)S(1)} %copy-done.9, ...), custom_call_target="tpu_custom_call" | custom-call | flops 10871635968 | bytes 22155776 | tf_op jit(solution)/shard_map/qkv/pallas_call | solution.py:428
  166.3 0.4 collective-permute-start.11
  166.7 1.3 collective-permute-start.7
  168.0 1.3 collective-permute-start.8
  169.3 28.1 %collective-permute-done.7.refs_0_ = bf16[384,1536]{1,0:T(8,128)(2,1)S(1)} collective-permute-done((bf16[384,1536]{1,0:T(8,128)(2,1)S(1)}, bf16[384,1536]{1,0:T(8,128)(2,1)S(1)}, u32[]{:S(2)}, u32[]{:S(2)}) %collective-permute-start.7) | collective-permute-done | bytes 1179680 | tf_op jit(solution)/shard_map/ppermute | solution.py:626
  197.4 5.7 %kv.2.refs_0_.refs_1_ = bf16[24,384,128]{2,1,0:T(8,128)(2,1)S(1)} custom-call(bf16[384,1536]{1,0:T(8,128)(2,1)S(1)} %collective-permute-done.7.refs_0_, f32[4,1536]{1,0:T(4,128)S(1)} %copy-done.7, f32[768,128]{1,0:T(8,128)S(1)} %get-tuple-element.50.refs_2_, f32[768,128]{1,0:T(8,128)S(1)} %copy-done.1, bf16[36,1536,128]{2,1,0:T(8,128)(2,1)S(1)} %bitcast.8), custom_call_target="tpu_custom_call" | custom-call | flops 3623878656 | bytes 17437184 | tf_op jit(solution)/shard_map/kv/pallas_call | solution.py:428
  203.1 18.7 %collective-permute-done.8.refs_0_ = bf16[384,1536]{1,0:T(8,128)(2,1)S(1)} collective-permute-done((bf16[384,1536]{1,0:T(8,128)(2,1)S(1)}, bf16[384,1536]{1,0:T(8,128)(2,1)S(1)}, u32[]{:S(2)}, u32[]{:S(2)}) %collective-permute-start.8) | collective-permute-done | bytes 1179680 | tf_op jit(solution)/shard_map/ppermute | solution.py:629
  221.8 5.5 %kv.3.refs_2_.refs_3_ = bf16[24,384,128]{2,1,0:T(8,128)(2,1)S(1)} custom-call(bf16[384,1536]{1,0:T(8,128)(2,1)S(1)} %collective-permute-done.8.refs_0_, f32[4,1536]{1,0:T(4,128)S(1)} %copy-done.7, f32[768,128]{1,0:T(8,128)S(1)} %get-tuple-element.50.refs_2_, f32[768,128]{1,0:T(8,128)S(1)} %copy-done.1, bf16[36,1536,128]{2,1,0:T(8,128)(2,1)S(1)} %bitcast.9), custom_call_target="tpu_custom_call" | custom-call | flops 3623878656 | bytes 17437184 | tf_op jit(solution)/shard_map/kv/pallas_call | solution.py:428
  227.3 0.0 copy-start.3
  227.4 0.0 collective-permute-start.10
  227.4 0.5 collective-permute-start.9
  227.9 4.0 %collective-permute-done.10.refs_6_.refs_7_ = bf16[24,384,128]{2,1,0:T(8,128)(2,1)S(1)} collective-permute-done((bf16[24,384,128]{2,1,0:T(8,128)(2,1)S(1)}, bf16[24,384,128]{2,1,0:T(8,128)(2,1)S(1)}, u32[]{:S(2)}, u32[]{:S(2)}) %collective-permute-start.10) | collective-permute-done | bytes 2359328 | tf_op jit(solution)/shard_map/ppermute | solution.py:638
  231.9 3.4 %collective-permute-done.9.refs_4_.refs_5_ = bf16[24,384,128]{2,1,0:T(8,128)(2,1)S(1)} collective-permute-done((bf16[24,384,128]{2,1,0:T(8,128)(2,1)S(1)}, bf16[24,384,128]{2,1,0:T(8,128)(2,1)S(1)}, u32[]{:S(2)}, u32[]{:S(2)}) %collective-permute-start.9) | collective-permute-done | bytes 2359328 | tf_op jit(solution)/shard_map/ppermute | solution.py:635
  235.3 0.0 collective-permute-done.11.refs_8_.refs_9_
  235.3 32.8 %attention.1.a_ref = bf16[768,1536]{1,0:T(8,128)(2,1)S(1)} custom-call(s32[16]{0:T(128)S(1)} %copy-done.11, bf16[12,768,128]{2,1,0:T(8,128)(2,1)S(1)} %get-tuple-element.48.q_ref, s32[768,128]{1,0:T(8,128)S(1)} %broadcast_in_dim.49.seg_ref, bf16[24,384,128]{2,1,0:T(8,128)(2,1)S(1)} %kv.2.refs_0_.refs_1_, bf16[24,384,128]{2,1,0:T(8,128)(2,1)S(1)} %kv.2.refs_0_.refs_1_, ...), custom_call_target="tpu_custom_call" | custom-call | flops 7247757312 | bytes 20000000 | tf_op jit(solution)/shard_map/attention/pallas_call | solution.py:546
  268.1 5.8 %proj_add.3.x_ref = bf16[768,1536]{1,0:T(8,128)(2,1)S(1)} custom-call(bf16[768,1536]{1,0:T(8,128)(2,1)S(1)} %attention.1.a_ref, bf16[1536,1536]{1,0:T(8,128)(2,1)} %bitcast.14, bf16[384,1536]{1,0:T(8,128)(2,1)S(1)} %copy-done.3, bf16[384,1536]{1,0:T(8,128)(2,1)S(1)} %copy-done.5), custom_call_target="tpu_custom_call" | custom-call | flops 3623878656 | bytes 11796480 | tf_op jit(solution)/shard_map/proj_add/pallas_call | solution.py:319
  273.9 51.8 %mlp.5 = bf16[768,1536]{1,0:T(8,128)(2,1)} custom-call(bf16[768,1536]{1,0:T(8,128)(2,1)S(1)} %proj_add.3.x_ref, f32[4,1536]{1,0:T(4,128)S(1)} %copy-done.7, bf16[2,1536,12288]{2,1,0:T(8,128)(2,1)} %wu_ref.5, bf16[2,1536,12288]{2,1,0:T(8,128)(2,1)} %wu_ref.5, bf16[2,6144,1536]{2,1,0:T(8,128)(2,1)} %wd_ref.5), custom_call_target="tpu_custom_call" | custom-call | flops 43486543872 | bytes 56623104 | tf_op jit(solution)/shard_map/mlp/pallas_call | solution.py:356
  (36 shorter events, 0.1 us)
Async XLA Ops:
  2.8 0.7 copy-start.6
  3.6 14.1 %copy-start.17 = (s32[768]{0:T(1024)S(1)}, s32[768]{0:T(1024)}, u32[]{:S(2)}) copy-start(s32[768]{0:T(1024)} %param.12) | copy-start | bytes 9220
  26.6 8.1 %collective-permute-start.2 = (s32[4]{0:T(128)}, s32[4]{0:T(128)}, u32[]{:S(2)}, u32[]{:S(2)}) collective-permute-start(s32[4]{0:T(128)} %convert_reduce_fusion), channel_id=1, source_target_pairs={{0,3},{1,2},{4,7},{5,6}} | collective-permute-start | bytes 56 | tf_op jit(solution)/shard_map/ppermute | solution.py:593
  27.9 6.8 %collective-permute-start.1 = (s32[4]{0:T(128)}, s32[4]{0:T(128)}, u32[]{:S(2)}, u32[]{:S(2)}) collective-permute-start(s32[4]{0:T(128)} %convert_reduce_fusion), channel_id=1, source_target_pairs={{0,2},{1,3},{4,6},{5,7}} | collective-permute-start | bytes 56 | tf_op jit(solution)/shard_map/ppermute | solution.py:593
  29.2 5.5 %collective-permute-start = (s32[4]{0:T(128)}, s32[4]{0:T(128)}, u32[]{:S(2)}, u32[]{:S(2)}) collective-permute-start(s32[4]{0:T(128)} %convert_reduce_fusion), channel_id=1, source_target_pairs={{0,1},{1,0},{2,3},{3,2},{4,5},{5,4},{6,7},{7,6}} | collective-permute-start | bytes 56 | tf_op jit(solution)/shard_map/ppermute | solution.py:592
  29.2 8.2 %collective-permute-start.3 = (f32[1,3072]{1,0:T(1,128)}, f32[1,3072]{1,0:T(1,128)S(1)}, u32[]{:S(2)}, u32[]{:S(2)}) collective-permute-start(f32[1,3072]{1,0:T(1,128)} %get-tuple-element.36), channel_id=1, source_target_pairs={{0,1},{1,0},{2,3},{3,2},{4,5},{5,4},{6,7},{7,6}} | collective-permute-start | bytes 36872 | tf_op jit(solution)/shard_map/ppermute | solution.py:590
  29.7 7.7 %collective-permute-start.4 = (f32[128,3072]{1,0:T(8,128)}, f32[128,3072]{1,0:T(8,128)S(1)}, u32[]{:S(2)}, u32[]{:S(2)}) collective-permute-start(f32[128,3072]{1,0:T(8,128)} %get-tuple-element.37), channel_id=1, source_target_pairs={{0,1},{1,0},{2,3},{3,2},{4,5},{5,4},{6,7},{7,6}} | collective-permute-start | bytes 4718600 | tf_op jit(solution)/shard_map/ppermute | solution.py:589
  37.3 3.0 copy-start.14
  37.4 3.0 copy-start.15
  37.4 3.0 copy-start.16
  38.8 23.5 %collective-permute-start.5 = (f32[64,3072]{1,0:T(8,128)S(1)}, f32[64,3072]{1,0:T(8,128)}, u32[]{:S(2)}, u32[]{:S(2)}) collective-permute-start(f32[64,3072]{1,0:T(8,128)S(1)} %select_add_fusion), channel_id=1, source_target_pairs={{0,2},{1,3},{4,6},{5,7}} | collective-permute-start | bytes 2359304 | tf_op jit(solution)/shard_map/ppermute | solution.py:604
  62.2 2.8 collective-permute-start.6
  65.0 19.4 %copy-start.10 = (s32[16]{0:T(128)}, s32[16]{0:T(128)S(1)}, u32[]{:S(2)}) copy-start(s32[16]{0:T(128)S(1)} %pad_add_fusion.sc_ref) | copy-start | bytes 196
  65.0 0.7 copy-start.13
  65.7 18.7 %copy-start.12 = (bf16[768,1536]{1,0:T(8,128)(2,1)S(1)}, bf16[768,1536]{1,0:T(8,128)(2,1)}, u32[]{:S(2)}) copy-start(bf16[768,1536]{1,0:T(8,128)(2,1)} %refs_0_.1) | copy-start | bytes 7077892
  84.4 10.0 %copy-start.7 = (f32[4,1536]{1,0:T(4,128)S(1)}, f32[4,1536]{1,0:T(4,128)}, u32[]{:S(2)}) copy-start(f32[4,1536]{1,0:T(4,128)} %gain_ref.7) | copy-start | bytes 73732
  94.4 57.0 %slice-start = ((s8[14155776]{0:T(1024)(128)(4,1)}), s8[4194304]{0:T(1024)(128)(4,1)S(1)}, s32[]{:S(2)}) async-start(s8[14155776]{0:T(1024)(128)(4,1)} %bitcast.5), calls=%async_computation | async-start | bytes 8388608
  94.4 57.0 %slice-start.1 = ((s8[14155776]{0:T(1024)(128)(4,1)}), s8[4194304]{0:T(1024)(128)(4,1)S(1)}, s32[]{:S(2)}) async-start(s8[14155776]{0:T(1024)(128)(4,1)} %bitcast.5), calls=%async_computation.1 | async-start | bytes 8388608
  122.4 44.3 %copy-start.2 = (bf16[384,1536]{1,0:T(8,128)(2,1)}, bf16[384,1536]{1,0:T(8,128)(2,1)S(1)}, u32[]{:S(2)}) copy-start(bf16[384,1536]{1,0:T(8,128)(2,1)S(1)} %mlp.3.refs_0_) | copy-start | bytes 3538948
  122.4 29.1 %slice-start.2 = ((s8[14155776]{0:T(1024)(128)(4,1)}), s8[4194304]{0:T(1024)(128)(4,1)S(1)}, s32[]{:S(2)}) async-start(s8[14155776]{0:T(1024)(128)(4,1)} %bitcast.5), calls=%async_computation.2 | async-start | bytes 8388608
  122.4 29.1 %slice-start.3 = ((s8[14155776]{0:T(1024)(128)(4,1)}), s8[1572864]{0:T(1024)(128)(4,1)S(1)}, s32[]{:S(2)}) async-start(s8[14155776]{0:T(1024)(128)(4,1)} %bitcast.5), calls=%async_computation.3 | async-start | bytes 3145728
  122.4 29.1 %copy-start.8 = (f32[768,128]{1,0:T(8,128)S(1)}, f32[768,128]{1,0:T(8,128)}, u32[]{:S(2)}) copy-start(f32[768,128]{1,0:T(8,128)} %get-tuple-element.45.refs_3_) | copy-start | bytes 1179652
  122.4 29.1 %copy-start.9 = (f32[768,128]{1,0:T(8,128)S(1)}, f32[768,128]{1,0:T(8,128)}, u32[]{:S(2)}) copy-start(f32[768,128]{1,0:T(8,128)} %get-tuple-element.46.refs_4_) | copy-start | bytes 1179652
  151.5 16.5 %copy-start.4 = (bf16[384,1536]{1,0:T(8,128)(2,1)}, bf16[384,1536]{1,0:T(8,128)(2,1)S(1)}, u32[]{:S(2)}) copy-start(bf16[384,1536]{1,0:T(8,128)(2,1)S(1)} %mlp.4.refs_1_) | copy-start | bytes 3538948
  151.5 45.9 %copy-start.1 = (f32[768,128]{1,0:T(8,128)S(1)}, f32[768,128]{1,0:T(8,128)}, u32[]{:S(2)}) copy-start(f32[768,128]{1,0:T(8,128)} %get-tuple-element.51.refs_3_) | copy-start | bytes 1179652
  166.3 36.8 %copy-start = (bf16[24,768,128]{2,1,0:T(8,128)(2,1)}, bf16[24,768,128]{2,1,0:T(8,128)(2,1)S(1)}, u32[]{:S(2)}) copy-start(bf16[24,768,128]{2,1,0:T(8,128)(2,1)S(1)} %get-tuple-element.54.refs_10_.refs_11_) | copy-start | bytes 14155780
  166.3 69.0 %collective-permute-start.11 = (bf16[24,768,128]{2,1,0:T(8,128)(2,1)S(1)}, bf16[24,768,128]{2,1,0:T(8,128)(2,1)}, u32[]{:S(2)}, u32[]{:S(2)}) collective-permute-start(bf16[24,768,128]{2,1,0:T(8,128)(2,1)S(1)} %get-tuple-element.54.refs_10_.refs_11_), channel_id=1, source_target_pairs={{0,1},{1,0},{2,3},{3,2},{4,5},{5,4},{6,7},{7,6}} | collective-permute-start | bytes 14155784 | tf_op jit(solution)/shard_map/ppermute | solution.py:632
  166.7 30.7 %collective-permute-start.7 = (bf16[384,1536]{1,0:T(8,128)(2,1)S(1)}, bf16[384,1536]{1,0:T(8,128)(2,1)S(1)}, u32[]{:S(2)}, u32[]{:S(2)}) collective-permute-start(bf16[384,1536]{1,0:T(8,128)(2,1)S(1)} %mlp.3.refs_0_), channel_id=1, source_target_pairs={{0,2},{1,3},{4,6},{5,7}} | collective-permute-start | bytes 3538952 | tf_op jit(solution)/shard_map/ppermute | solution.py:626
  168.0 53.8 %collective-permute-start.8 = (bf16[384,1536]{1,0:T(8,128)(2,1)S(1)}, bf16[384,1536]{1,0:T(8,128)(2,1)S(1)}, u32[]{:S(2)}, u32[]{:S(2)}) collective-permute-start(bf16[384,1536]{1,0:T(8,128)(2,1)S(1)} %mlp.4.refs_1_), channel_id=1, source_target_pairs={{0,2},{1,3},{4,6},{5,7}} | collective-permute-start | bytes 3538952 | tf_op jit(solution)/shard_map/ppermute | solution.py:629
  203.1 32.2 %copy-start.11 = (s32[16]{0:T(128)S(1)}, s32[16]{0:T(128)}, u32[]{:S(2)}) copy-start(s32[16]{0:T(128)} %copy-done.10) | copy-start | bytes 196
  227.3 40.7 %copy-start.3 = (bf16[384,1536]{1,0:T(8,128)(2,1)S(1)}, bf16[384,1536]{1,0:T(8,128)(2,1)}, u32[]{:S(2)}) copy-start(bf16[384,1536]{1,0:T(8,128)(2,1)} %copy-done.2) | copy-start | bytes 3538948
  227.4 40.7 %copy-start.5 = (bf16[384,1536]{1,0:T(8,128)(2,1)S(1)}, bf16[384,1536]{1,0:T(8,128)(2,1)}, u32[]{:S(2)}) copy-start(bf16[384,1536]{1,0:T(8,128)(2,1)} %copy-done.4) | copy-start | bytes 3538948
  227.4 4.6 %collective-permute-start.10 = (bf16[24,384,128]{2,1,0:T(8,128)(2,1)S(1)}, bf16[24,384,128]{2,1,0:T(8,128)(2,1)S(1)}, u32[]{:S(2)}, u32[]{:S(2)}) collective-permute-start(bf16[24,384,128]{2,1,0:T(8,128)(2,1)S(1)} %kv.3.refs_2_.refs_3_), channel_id=1, source_target_pairs={{0,1},{1,0},{2,3},{3,2},{4,5},{5,4},{6,7},{7,6}} | collective-permute-start | bytes 7077896 | tf_op jit(solution)/shard_map/ppermute | solution.py:638
  227.4 7.9 %collective-permute-start.9 = (bf16[24,384,128]{2,1,0:T(8,128)(2,1)S(1)}, bf16[24,384,128]{2,1,0:T(8,128)(2,1)S(1)}, u32[]{:S(2)}, u32[]{:S(2)}) collective-permute-start(bf16[24,384,128]{2,1,0:T(8,128)(2,1)S(1)} %kv.2.refs_0_.refs_1_), channel_id=1, source_target_pairs={{0,1},{1,0},{2,3},{3,2},{4,5},{5,4},{6,7},{7,6}} | collective-permute-start | bytes 7077896 | tf_op jit(solution)/shard_map/ppermute | solution.py:635

commit v6 on v5

--- a/solution.py
+++ b/solution.py
@@ -347,11 +347,10 @@
         out_ref[...] = (x_ref[...].astype(F32) + acc_ref[...]).astype(BF16)
 
 
-def mlp(x_rows, gains, mlp_up, mlp_down, layer, part, parts):
-    tokens, dim = x_rows.shape
-    tokens //= parts
+def mlp(x_rows, gains, mlp_up, mlp_down, layer, tokens, part):
+    dim = x_rows.shape[1]
     ff = mlp_down.shape[1]
-    tile = 512 * parts
+    tile = 512 if tokens == x_rows.shape[0] else 1024
     n_ff = ff // tile
     return pl.pallas_call(
         functools.partial(mlp_kernel, layer),
@@ -434,7 +433,7 @@
         out_specs=tuple(out_specs),
         out_shape=tuple(out_shape),
         scratch_shapes=[pltpu.VMEM((tokens, dim), BF16)],
-        compiler_params=params(("arbitrary",), 24),
+        compiler_params=params(("arbitrary",), 40),
         cost_estimate=cost(2 * tokens * dim * steps * per * head_dim, 2 * dim * steps * per * head_dim + 8e6),
         name="qkv" if with_q else "kv",
     )(*parts, gains, cos, sin, w_heads)
@@ -518,7 +517,7 @@
     for i in range(4):
         k_ref, v_ref = far_refs[2 * i], far_refs[2 * i + 1]
         width = k_ref.shape[1]
-        base = sc_ref[i // 2] + (i % 2) * width
+        base = sc_ref[i // 2] + (i % 2) * far_refs[0].shape[1]
 
         @pl.when((base < q0) & (first_start < base + width))
         def _(k_ref=k_ref, v_ref=v_ref, base=base, width=width):
@@ -622,10 +621,10 @@
 
         gated = ssd_full(scalars, xs, bc, dt, cum, seg_wide, z, got, other, pair_state, pair_decay, head_pad, y_gain[None, :])
         x_one = proj_add(gated, w_out, [x_rows])
-        x_a = mlp(x_one, norm_gains, mlp_up, mlp_down, 0, 0, 2)
+        x_a = mlp(x_one, norm_gains, mlp_up, mlp_down, 0, 2 * BLOCK, 0)
         far_a = lax.ppermute(x_a, 'sp', cross_perm)
         x_one, x_a = lax.optimization_barrier((x_one, x_a))
-        x_b = mlp(x_one, norm_gains, mlp_up, mlp_down, 0, 1, 2)
+        x_b = mlp(x_one, norm_gains, mlp_up, mlp_down, 0, BLOCK, 2)
         far_b = lax.ppermute(x_b, 'sp', cross_perm)
         w_heads = w_qkv.transpose(1, 0, 2)
         q, kv = qkv_proj([x_a, x_b], norm_gains, cos, sin, 0, w_heads, n_query, True)
@@ -634,10 +633,10 @@
         kv_far_a, = qkv_proj([far_a], norm_gains, cos_far, sin_far, 0, w_heads, n_query, False)
         kv_fp_a = lax.ppermute(kv_far_a, 'sp', swap_perm)
         far_b, kv_far_a = lax.optimization_barrier((far_b, kv_far_a))
-        kv_far_b, = qkv_proj([far_b], norm_gains, cos_far, sin_far, 1, w_heads, n_query, False)
+        kv_far_b, = qkv_proj([far_b], norm_gains, cos_far, sin_far, 2, w_heads, n_query, False)
         kv_fp_b = lax.ppermute(kv_far_b, 'sp', swap_perm)
         attn = attention(scalars, q, seg_wide, [kv_far_a, kv_far_b, kv_fp_a, kv_fp_b, kv_pair, kv])
         x_three = proj_add(attn, w_attn_out.reshape(n_query * head_dim, dim), [x_a, x_b])
-        return mlp(x_three, norm_gains, mlp_up, mlp_down, 1, 0, 1)
+        return mlp(x_three, norm_gains, mlp_up, mlp_down, 1, tokens, 0)
 
     return jax.shard_map(layers, mesh=mesh, in_specs=(row_spec, tok_spec) + (replicated,) * 9, out_specs=row_spec, check_vma=False)

time: 331 us -> 304 us (0.918)
  waiting for transfers between devices: 62.2 us -> 34.1 us
  Pallas kernels: 237 us -> 245 us
  other arithmetic: 13 us -> 7.63 us
    ppermute x1, waiting for transfers between devices: 28.1 us -> 0.01 us  [layers(): far_a = lax.ppermute(x_a, 'sp', cross_perm)]
    pallas_call x3, Pallas kernels: 25.9 us -> 33.6 us  [qkv_proj(): pl.pallas_call(functools.partial(qkv_kernel, n_q, n_rot, len(parts)), gri...]
    ppermute x1, waiting for transfers between devices: 3.37 us -> 0.01 us  [layers(): kv_fp_a = lax.ppermute(kv_far_a, 'sp', swap_perm)]
  transfers between devices with their start and end apart: 12 -> 12, of which waited for: 5 -> 4; matrix products, arithmetic and copies ran while one was open for 3% -> 2% of each run, Pallas kernels for 7% -> 23%
where the time goes in v6:
time: 304 us; the launch traced here: 298 us
  Pallas kernels  245 us (81%)
  waiting for transfers between devices  34.1 us (11%)
  starting transfers between devices  8.31 us (3%)
  other arithmetic  7.63 us (3%)
    pallas_call x3, Pallas kernels, mlp(): pl.pallas_call(functools.partial(mlp_kernel, layer), grid=(n_ff,), in_spe...  110 us
    pallas_call x3, Pallas kernels, qkv_proj(): pl.pallas_call(functools.partial(qkv_kernel, n_q, n_rot, len(parts)), gri...  33.6 us
    pallas_call x1, Pallas kernels, attention(): pl.pallas_call(attn_kernel, grid_spec=pltpu.PrefetchScalarGridSpec(num_sc...  30.6 us
    ppermute x1, waiting for transfers between devices, layers(): far_b = lax.ppermute(x_b, 'sp', cross_perm)  20.6 us
    pallas_call x1, Pallas kernels, ssd_full(): pl.pallas_call(ssd_full_kernel, grid=(tokens // STEP,), in_specs=[SMEM_SP...  19.2 us
    pallas_call x2, Pallas kernels, proj_add(): pl.pallas_call(proj_add_kernel, grid=(dim // tile,), in_specs=[full_spec(...  15.8 us
    pallas_call x1, Pallas kernels, in_proj(): pl.pallas_call(functools.partial(in_proj_kernel, n_heads), grid=(n_x + 1,...  14.2 us
    pallas_call x1, Pallas kernels, z_proj(): pl.pallas_call(z_proj_kernel, grid=(inner // tile,), in_specs=[full_spec(...  12.7 us
  transfers between devices with their start and end apart: 12, of which 4 were waited for; matrix products, arithmetic and copies ran while one was open for 2% of the time, Pallas kernels for 23%

profile of v6, /device:TPU:2, one launch (start us, length us, event | category | flops | bytes accessed | tf_op | source)
XLA Modules:
  0.0 298.0 jit_solution(15884621571767449663)
XLA Ops:
  0.0 0.8 convert_reduce_fusion
  0.8 0.1 compare_select_fusion.1.sc_ref
  0.9 0.7 pad.13.head_ref
  1.6 0.7 copy-done.5
  2.3 14.2 %in_proj.1 = (bf16[768,1536]{1,0:T(8,128)(2,1)}, bf16[768,3072]{1,0:T(8,128)(2,1)}, bf16[768,256]{1,0:T(8,128)(2,1)S(1)}, f32[768,128]{1,0:T(8,128)S(1)}, f32[768,128]{1,0:T(8,128)S(1)}) custom-call(bf16[768,1536]{1,0:T(8,128)(2,1)} %refs_0_.1, f32[4,1536]{1,0:T(4,128)S(1)} %copy-done.5, bf16[6448,1536]{1,0:T(8,128)(2,1)} %bitcast.9, f32[8,128]{1,0:T(8,128)S(1)} %pad.13.head_ref), custom_call_target="tpu_custom_call" | custom-call | flops 9663676416 | bytes 16000000 | tf_op jit(solution)/shard_map/in_proj/pallas_call | solution.py:88
  16.5 0.0 copy-done.12
  16.5 0.2 broadcast_in_dim.49.seg_ref
  16.6 8.7 %ssd_state.1 = (f32[128,3072]{1,0:T(8,128)}, f32[1,3072]{1,0:T(1,128)S(1)}) custom-call(s32[16]{0:T(128)S(1)} %compare_select_fusion.1.sc_ref, bf16[768,3072]{1,0:T(8,128)(2,1)} %get-tuple-element.30.x_ref, bf16[768,256]{1,0:T(8,128)(2,1)S(1)} %get-tuple-element.31.bc_ref, f32[768,128]{1,0:T(8,128)S(1)} %get-tuple-element.32.dt_ref, ...), custom_call_target="tpu_custom_call" | custom-call | flops 1207959552 | bytes 8000000 | tf_op jit(solution)/shard_map/ssd_state/pallas_call | solution.py:193
  25.3 1.3 collective-permute-start.2
  26.6 1.3 collective-permute-start.1
  27.9 0.0 collective-permute-start
  28.0 0.5 collective-permute-start.3
  28.5 0.0 collective-permute-start.4
  28.5 3.9 %fusion.1 = (f32[768,64]{1,0:T(8,128)S(1)}, f32[768,64]{1,0:T(8,128)S(1)}, f32[768,64]{1,0:T(8,128)S(1)}, f32[768,64]{1,0:T(8,128)}, f32[768,64]{1,0:T(8,128)}, /*index=5*/f32[768,64]{1,0:T(8,128)}) fusion(f32[64]{0:T(128)S(1)} %multiply_power_fusion, f32[768]{0:T(1024)S(1)} %broadcast_add_fusion, f32[768]{0:T(1024)S(1)} %add_convert_fusion), kind=kLoop, calls=%fused_computation.10 | loop fusion | flops 196608 | bytes 1186048 | tf_op jit(solution)/shard_map/neg | solution.py:379
  32.4 0.3 pad_maximum_fusion.2
  32.7 0.0 collective-permute-done.2
  32.7 0.0 collective-permute-done.1
  32.7 0.0 collective-permute-done
  32.7 0.6 fusion.7
  33.9 0.0 copy-start.9
  33.9 0.0 copy-start.10
  33.9 0.0 copy-start.11
  33.9 0.0 collective-permute-done.3.pdecay_ref
  34.0 0.0 collective-permute-done.4.pair_ref
  34.0 1.6 select_add_fusion
  35.5 1.6 collective-permute-start.5
  37.1 0.0 copy-done.9
  37.1 0.0 copy-done.10
  37.1 0.0 copy-done.11
  37.2 0.3 pad_maximum_fusion
  37.4 0.0 copy-start.8
  37.4 12.7 %z_proj.1.z_ref = f32[768,3072]{1,0:T(8,128)} custom-call(bf16[768,1536]{1,0:T(8,128)(2,1)} %get-tuple-element.40.h_ref, bf16[6448,1536]{1,0:T(8,128)(2,1)} %bitcast.10), custom_call_target="tpu_custom_call" | custom-call | flops 7247757312 | bytes 21000000 | tf_op jit(solution)/shard_map/z_proj/pallas_call | solution.py:120
  50.1 7.6 %collective-permute-done.5.got_ref = f32[64,3072]{1,0:T(8,128)} collective-permute-done((f32[64,3072]{1,0:T(8,128)S(1)}, f32[64,3072]{1,0:T(8,128)}, u32[]{:S(2)}, u32[]{:S(2)}) %collective-permute-start.5) | collective-permute-done | bytes 786464 | tf_op jit(solution)/shard_map/ppermute | solution.py:603
  57.7 0.0 collective-permute-start.6
  57.7 0.1 slice.3
  57.8 0.1 pad_add_fusion.sc_ref
  57.9 2.4 collective-permute-done.6.other_ref
  60.4 19.2 %ssd_full.1.a_ref = bf16[768,3072]{1,0:T(8,128)(2,1)S(1)} custom-call(s32[16]{0:T(128)S(1)} %pad_add_fusion.sc_ref, bf16[768,3072]{1,0:T(8,128)(2,1)} %get-tuple-element.30.x_ref, bf16[768,256]{1,0:T(8,128)(2,1)S(1)} %get-tuple-element.31.bc_ref, f32[768,128]{1,0:T(8,128)S(1)} %get-tuple-element.32.dt_ref, f32[768,128]{1,0:T(8,128)S(1)} %get-tuple-element.33.cum_ref, ...), custom_call_target="tpu_custom_call" | custom-call | flops 12000000000 | bytes 20000000 | tf_op jit(solution)/shard_map/ssd_full/pallas_call | solution.py:287
  79.6 0.0 copy-done.7
  79.6 0.0 copy-start.6
  79.6 10.0 %proj_add.2.x_ref = bf16[768,1536]{1,0:T(8,128)(2,1)S(1)} custom-call(bf16[768,3072]{1,0:T(8,128)(2,1)S(1)} %ssd_full.1.a_ref, bf16[3072,1536]{1,0:T(8,128)(2,1)} %w_ref.1, bf16[768,1536]{1,0:T(8,128)(2,1)S(1)} %copy-done.7), custom_call_target="tpu_custom_call" | custom-call | flops 7247757312 | bytes 18874368 | tf_op jit(solution)/shard_map/proj_add/pallas_call | solution.py:319
  89.6 35.4 %mlp.3.refs_0_ = bf16[512,1536]{1,0:T(8,128)(2,1)S(1)} custom-call(bf16[768,1536]{1,0:T(8,128)(2,1)S(1)} %proj_add.2.x_ref, f32[4,1536]{1,0:T(4,128)S(1)} %copy-done.6, bf16[2,1536,12288]{2,1,0:T(8,128)(2,1)} %wu_ref.5, bf16[2,1536,12288]{2,1,0:T(8,128)(2,1)} %wu_ref.5, bf16[2,6144,1536]{2,1,0:T(8,128)(2,1)} %wd_ref.5), custom_call_target="tpu_custom_call" | custom-call | flops 28991029248 | bytes 56623104 | tf_op jit(solution)/shard_map/mlp/pallas_call | solution.py:355
  124.9 0.0 copy-start.1
  125.0 1.8 collective-permute-start.7
  126.8 22.9 %mlp.4.refs_1_ = bf16[256,1536]{1,0:T(8,128)(2,1)S(1)} custom-call(bf16[768,1536]{1,0:T(8,128)(2,1)S(1)} %proj_add.2.x_ref, f32[4,1536]{1,0:T(4,128)S(1)} %copy-done.6, bf16[2,1536,12288]{2,1,0:T(8,128)(2,1)} %wu_ref.5, bf16[2,1536,12288]{2,1,0:T(8,128)(2,1)} %wu_ref.5, bf16[2,6144,1536]{2,1,0:T(8,128)(2,1)} %wd_ref.5), custom_call_target="tpu_custom_call" | custom-call | flops 14495514624 | bytes 56623104 | tf_op jit(solution)/shard_map/mlp/pallas_call | solution.py:355
  149.7 0.0 copy-start.3
  149.7 0.0 copy-done.1
  149.7 16.7 %qkv.1 = (bf16[12,768,128]{2,1,0:T(8,128)(2,1)S(1)}, bf16[24,768,128]{2,1,0:T(8,128)(2,1)S(1)}) custom-call(bf16[512,1536]{1,0:T(8,128)(2,1)S(1)} %mlp.3.refs_0_, bf16[256,1536]{1,0:T(8,128)(2,1)S(1)} %mlp.4.refs_1_, f32[4,1536]{1,0:T(4,128)S(1)} %copy-done.6, f32[768,128]{1,0:T(8,128)S(1)} %get-tuple-element.45.refs_3_, ...), custom_call_target="tpu_custom_call" | custom-call | flops 10871635968 | bytes 22155776 | tf_op jit(solution)/shard_map/qkv/pallas_call | solution.py:427
  166.4 0.0 copy-start
  166.4 0.2 collective-permute-start.11
  166.5 0.0 collective-permute-done.7.refs_0_
  166.5 10.3 %kv.2.refs_0_.refs_1_ = bf16[24,512,128]{2,1,0:T(8,128)(2,1)S(1)} custom-call(bf16[512,1536]{1,0:T(8,128)(2,1)S(1)} %collective-permute-done.7.refs_0_, f32[4,1536]{1,0:T(4,128)S(1)} %copy-done.6, f32[768,128]{1,0:T(8,128)S(1)} %get-tuple-element.50.refs_2_, f32[768,128]{1,0:T(8,128)S(1)} %get-tuple-element.51.refs_3_, bf16[36,1536,128]{2,1,0:T(8,128)(2,1)} %bitcast.7), custom_call_target="tpu_custom_call" | custom-call | flops 4831838208 | bytes 17437184 | tf_op jit(solution)/shard_map/kv/pallas_call | solution.py:427
  176.9 0.1 collective-permute-start.9
  177.0 1.5 collective-permute-start.8
  178.5 20.6 %collective-permute-done.8.refs_0_ = bf16[256,1536]{1,0:T(8,128)(2,1)S(1)} collective-permute-done((bf16[256,1536]{1,0:T(8,128)(2,1)S(1)}, bf16[256,1536]{1,0:T(8,128)(2,1)S(1)}, u32[]{:S(2)}, u32[]{:S(2)}) %collective-permute-start.8) | collective-permute-done | bytes 786464 | tf_op jit(solution)/shard_map/ppermute | solution.py:628
  199.1 6.6 %kv.3.refs_2_.refs_3_ = bf16[24,256,128]{2,1,0:T(8,128)(2,1)S(1)} custom-call(bf16[256,1536]{1,0:T(8,128)(2,1)S(1)} %collective-permute-done.8.refs_0_, f32[4,1536]{1,0:T(4,128)S(1)} %copy-done.6, f32[768,128]{1,0:T(8,128)S(1)} %get-tuple-element.50.refs_2_, f32[768,128]{1,0:T(8,128)S(1)} %get-tuple-element.51.refs_3_, bf16[36,1536,128]{2,1,0:T(8,128)(2,1)} %bitcast.8), custom_call_target="tpu_custom_call" | custom-call | flops 2415919104 | bytes 17437184 | tf_op jit(solution)/shard_map/kv/pallas_call | solution.py:427
  205.7 0.0 copy-start.2
  205.7 0.0 collective-permute-start.10
  205.8 3.4 %collective-permute-done.10.refs_6_.refs_7_ = bf16[24,256,128]{2,1,0:T(8,128)(2,1)S(1)} collective-permute-done((bf16[24,256,128]{2,1,0:T(8,128)(2,1)S(1)}, bf16[24,256,128]{2,1,0:T(8,128)(2,1)S(1)}, u32[]{:S(2)}, u32[]{:S(2)}) %collective-permute-start.10) | collective-permute-done | bytes 1572896 | tf_op jit(solution)/shard_map/ppermute | solution.py:637
  209.2 0.0 collective-permute-done.9.refs_4_.refs_5_
  209.2 0.0 collective-permute-done.11.refs_8_.refs_9_
  209.2 30.6 %attention.1.a_ref = bf16[768,1536]{1,0:T(8,128)(2,1)S(1)} custom-call(s32[16]{0:T(128)S(1)} %pad_add_fusion.sc_ref, bf16[12,768,128]{2,1,0:T(8,128)(2,1)S(1)} %get-tuple-element.48.q_ref, s32[768,128]{1,0:T(8,128)S(1)} %broadcast_in_dim.49.seg_ref, bf16[24,512,128]{2,1,0:T(8,128)(2,1)S(1)} %kv.2.refs_0_.refs_1_, ...), custom_call_target="tpu_custom_call" | custom-call | flops 7247757312 | bytes 20000000 | tf_op jit(solution)/shard_map/attention/pallas_call | solution.py:545
  239.8 5.8 %proj_add.3.x_ref = bf16[768,1536]{1,0:T(8,128)(2,1)S(1)} custom-call(bf16[768,1536]{1,0:T(8,128)(2,1)S(1)} %attention.1.a_ref, bf16[1536,1536]{1,0:T(8,128)(2,1)} %bitcast.12, bf16[512,1536]{1,0:T(8,128)(2,1)S(1)} %copy-done.2, bf16[256,1536]{1,0:T(8,128)(2,1)S(1)} %copy-done.4), custom_call_target="tpu_custom_call" | custom-call | flops 3623878656 | bytes 11796480 | tf_op jit(solution)/shard_map/proj_add/pallas_call | solution.py:319
  245.7 52.1 %mlp.5 = bf16[768,1536]{1,0:T(8,128)(2,1)} custom-call(bf16[768,1536]{1,0:T(8,128)(2,1)S(1)} %proj_add.3.x_ref, f32[4,1536]{1,0:T(4,128)S(1)} %copy-done.6, bf16[2,1536,12288]{2,1,0:T(8,128)(2,1)} %wu_ref.5, bf16[2,1536,12288]{2,1,0:T(8,128)(2,1)} %wu_ref.5, bf16[2,6144,1536]{2,1,0:T(8,128)(2,1)} %wd_ref.5), custom_call_target="tpu_custom_call" | custom-call | flops 43486543872 | bytes 56623104 | tf_op jit(solution)/shard_map/mlp/pallas_call | solution.py:355
  (17 shorter events, 0.1 us)
Async XLA Ops:
  1.6 0.7 copy-start.5
  2.3 14.2 %copy-start.12 = (s32[768]{0:T(1024)S(1)}, s32[768]{0:T(1024)}, u32[]{:S(2)}) copy-start(s32[768]{0:T(1024)} %param.12) | copy-start | bytes 9220
  25.3 7.4 %collective-permute-start.2 = (s32[4]{0:T(128)S(1)}, s32[4]{0:T(128)S(1)}, u32[]{:S(2)}, u32[]{:S(2)}) collective-permute-start(s32[4]{0:T(128)S(1)} %convert_reduce_fusion), channel_id=1, source_target_pairs={{0,3},{1,2},{4,7},{5,6}} | collective-permute-start | bytes 56 | tf_op jit(solution)/shard_map/ppermute | solution.py:592
  26.6 6.1 %collective-permute-start.1 = (s32[4]{0:T(128)S(1)}, s32[4]{0:T(128)S(1)}, u32[]{:S(2)}, u32[]{:S(2)}) collective-permute-start(s32[4]{0:T(128)S(1)} %convert_reduce_fusion), channel_id=1, source_target_pairs={{0,2},{1,3},{4,6},{5,7}} | collective-permute-start | bytes 56 | tf_op jit(solution)/shard_map/ppermute | solution.py:592
  27.9 4.8 %collective-permute-start = (s32[4]{0:T(128)S(1)}, s32[4]{0:T(128)S(1)}, u32[]{:S(2)}, u32[]{:S(2)}) collective-permute-start(s32[4]{0:T(128)S(1)} %convert_reduce_fusion), channel_id=1, source_target_pairs={{0,1},{1,0},{2,3},{3,2},{4,5},{5,4},{6,7},{7,6}} | collective-permute-start | bytes 56 | tf_op jit(solution)/shard_map/ppermute | solution.py:591
  28.0 6.0 %collective-permute-start.3 = (f32[1,3072]{1,0:T(1,128)S(1)}, f32[1,3072]{1,0:T(1,128)S(1)}, u32[]{:S(2)}, u32[]{:S(2)}) collective-permute-start(f32[1,3072]{1,0:T(1,128)S(1)} %get-tuple-element.36), channel_id=1, source_target_pairs={{0,1},{1,0},{2,3},{3,2},{4,5},{5,4},{6,7},{7,6}} | collective-permute-start | bytes 36872 | tf_op jit(solution)/shard_map/ppermute | solution.py:589
  28.5 5.5 %collective-permute-start.4 = (f32[128,3072]{1,0:T(8,128)}, f32[128,3072]{1,0:T(8,128)}, u32[]{:S(2)}, u32[]{:S(2)}) collective-permute-start(f32[128,3072]{1,0:T(8,128)} %get-tuple-element.37), channel_id=1, source_target_pairs={{0,1},{1,0},{2,3},{3,2},{4,5},{5,4},{6,7},{7,6}} | collective-permute-start | bytes 4718600 | tf_op jit(solution)/shard_map/ppermute | solution.py:588
  33.9 3.2 %copy-start.9 = (f32[768,64]{1,0:T(8,128)S(1)}, f32[768,64]{1,0:T(8,128)}, u32[]{:S(2)}) copy-start(f32[768,64]{1,0:T(8,128)} %get-tuple-element.63) | copy-start | bytes 589828
  33.9 3.2 %copy-start.10 = (f32[768,64]{1,0:T(8,128)S(1)}, f32[768,64]{1,0:T(8,128)}, u32[]{:S(2)}) copy-start(f32[768,64]{1,0:T(8,128)} %get-tuple-element.64) | copy-start | bytes 589828
  33.9 3.2 %copy-start.11 = (f32[768,64]{1,0:T(8,128)S(1)}, f32[768,64]{1,0:T(8,128)}, u32[]{:S(2)}) copy-start(f32[768,64]{1,0:T(8,128)} %get-tuple-element.65) | copy-start | bytes 589828
  35.5 22.2 %collective-permute-start.5 = (f32[64,3072]{1,0:T(8,128)S(1)}, f32[64,3072]{1,0:T(8,128)}, u32[]{:S(2)}, u32[]{:S(2)}) collective-permute-start(f32[64,3072]{1,0:T(8,128)S(1)} %select_add_fusion), channel_id=1, source_target_pairs={{0,2},{1,3},{4,6},{5,7}} | collective-permute-start | bytes 2359304 | tf_op jit(solution)/shard_map/ppermute | solution.py:603
  37.4 22.9 %copy-start.8 = (f32[3072]{0:T(1024)S(1)}, f32[3072]{0:T(1024)}, u32[]{:S(2)}) copy-start(f32[3072]{0:T(1024)} %param.16) | copy-start | bytes 36868
  57.7 2.6 collective-permute-start.6
  60.4 19.2 %copy-start.7 = (bf16[768,1536]{1,0:T(8,128)(2,1)S(1)}, bf16[768,1536]{1,0:T(8,128)(2,1)}, u32[]{:S(2)}) copy-start(bf16[768,1536]{1,0:T(8,128)(2,1)} %refs_0_.1) | copy-start | bytes 7077892
  79.6 10.0 %copy-start.6 = (f32[4,1536]{1,0:T(4,128)S(1)}, f32[4,1536]{1,0:T(4,128)}, u32[]{:S(2)}) copy-start(f32[4,1536]{1,0:T(4,128)} %gain_ref.7) | copy-start | bytes 73732
  124.9 24.7 %copy-start.1 = (bf16[512,1536]{1,0:T(8,128)(2,1)}, bf16[512,1536]{1,0:T(8,128)(2,1)S(1)}, u32[]{:S(2)}) copy-start(bf16[512,1536]{1,0:T(8,128)(2,1)S(1)} %mlp.3.refs_0_) | copy-start | bytes 4718596
  125.0 41.6 %collective-permute-start.7 = (bf16[512,1536]{1,0:T(8,128)(2,1)S(1)}, bf16[512,1536]{1,0:T(8,128)(2,1)S(1)}, u32[]{:S(2)}, u32[]{:S(2)}) collective-permute-start(bf16[512,1536]{1,0:T(8,128)(2,1)S(1)} %mlp.3.refs_0_), channel_id=1, source_target_pairs={{0,2},{1,3},{4,6},{5,7}} | collective-permute-start | bytes 4718600 | tf_op jit(solution)/shard_map/ppermute | solution.py:625
  149.7 27.3 %copy-start.3 = (bf16[256,1536]{1,0:T(8,128)(2,1)}, bf16[256,1536]{1,0:T(8,128)(2,1)S(1)}, u32[]{:S(2)}) copy-start(bf16[256,1536]{1,0:T(8,128)(2,1)S(1)} %mlp.4.refs_1_) | copy-start | bytes 2359300
  166.4 10.5 %copy-start = (bf16[24,768,128]{2,1,0:T(8,128)(2,1)}, bf16[24,768,128]{2,1,0:T(8,128)(2,1)S(1)}, u32[]{:S(2)}) copy-start(bf16[24,768,128]{2,1,0:T(8,128)(2,1)S(1)} %get-tuple-element.54.refs_10_.refs_11_) | copy-start | bytes 14155780
  166.4 42.8 %collective-permute-start.11 = (bf16[24,768,128]{2,1,0:T(8,128)(2,1)S(1)}, bf16[24,768,128]{2,1,0:T(8,128)(2,1)}, u32[]{:S(2)}, u32[]{:S(2)}) collective-permute-start(bf16[24,768,128]{2,1,0:T(8,128)(2,1)S(1)} %get-tuple-element.54.refs_10_.refs_11_), channel_id=1, source_target_pairs={{0,1},{1,0},{2,3},{3,2},{4,5},{5,4},{6,7},{7,6}} | collective-permute-start | bytes 14155784 | tf_op jit(solution)/shard_map/ppermute | solution.py:631
  176.9 32.3 %collective-permute-start.9 = (bf16[24,512,128]{2,1,0:T(8,128)(2,1)S(1)}, bf16[24,512,128]{2,1,0:T(8,128)(2,1)S(1)}, u32[]{:S(2)}, u32[]{:S(2)}) collective-permute-start(bf16[24,512,128]{2,1,0:T(8,128)(2,1)S(1)} %kv.2.refs_0_.refs_1_), channel_id=1, source_target_pairs={{0,1},{1,0},{2,3},{3,2},{4,5},{5,4},{6,7},{7,6}} | collective-permute-start | bytes 9437192 | tf_op jit(solution)/shard_map/ppermute | solution.py:634
  177.0 22.1 %collective-permute-start.8 = (bf16[256,1536]{1,0:T(8,128)(2,1)S(1)}, bf16[256,1536]{1,0:T(8,128)(2,1)S(1)}, u32[]{:S(2)}, u32[]{:S(2)}) collective-permute-start(bf16[256,1536]{1,0:T(8,128)(2,1)S(1)} %mlp.4.refs_1_), channel_id=1, source_target_pairs={{0,2},{1,3},{4,6},{5,7}} | collective-permute-start | bytes 2359304 | tf_op jit(solution)/shard_map/ppermute | solution.py:628
  205.7 34.1 %copy-start.2 = (bf16[512,1536]{1,0:T(8,128)(2,1)S(1)}, bf16[512,1536]{1,0:T(8,128)(2,1)}, u32[]{:S(2)}) copy-start(bf16[512,1536]{1,0:T(8,128)(2,1)} %copy-done.1) | copy-start | bytes 4718596
  205.7 34.1 %copy-start.4 = (bf16[256,1536]{1,0:T(8,128)(2,1)S(1)}, bf16[256,1536]{1,0:T(8,128)(2,1)}, u32[]{:S(2)}) copy-start(bf16[256,1536]{1,0:T(8,128)(2,1)} %copy-done.3) | copy-start | bytes 2359300
  205.7 3.4 %collective-permute-start.10 = (bf16[24,256,128]{2,1,0:T(8,128)(2,1)S(1)}, bf16[24,256,128]{2,1,0:T(8,128)(2,1)S(1)}, u32[]{:S(2)}, u32[]{:S(2)}) collective-permute-start(bf16[24,256,128]{2,1,0:T(8,128)(2,1)S(1)} %kv.3.refs_2_.refs_3_), channel_id=1, source_target_pairs={{0,1},{1,0},{2,3},{3,2},{4,5},{5,4},{6,7},{7,6}} | collective-permute-start | bytes 4718600 | tf_op jit(solution)/shard_map/ppermute | solution.py:637
